TPU v7x, 256 devices: a whole 4x4x8 slice. The times are simulated.
256 devices in a mesh: seq: 128 (over y, x, z), slide: 2 (over core).
Axes of the slice: x: 4, y: 4, z: 8, core: 2. Of those that a mesh axis runs over, the one named last changes fastest.
Arguments:
- tile_embed: bfloat16 [131072, 768], P(('slide', 'seq')), parts along dimension 0, may hold values from -6 to 6
- valid_tiles: int32 [2], P('slide'), parts along dimension 0, may hold values from 32768 to 65536
- offsets: int32 [16], replicated, may hold values from 0 to 15
- norm_gain: float32 [768], replicated, may hold values from 0.1 to 1.9
- w_qkv: bfloat16 [768, 2304], replicated
- sub_gain: float32 [768], replicated, may hold values from 0.1 to 1.9
- w_out: bfloat16 [768, 768], replicated, may hold values from -0.21875 to 0.21875
Outputs:
- encoded: bfloat16 [131072, 768], P(('slide', 'seq')), parts along dimension 0
There are 2 independent parts, one for each index of `slide`. A program takes and returns all parts, laid end to end along the dimension named above; an argument that names none is the same for every part. Nothing has to cross between parts.
All inputs are finite; a program needn't handle non-finite values.
Results may differ from a plain program's by a relative error of at most 0.0078.
Values may be sent and summed in bfloat16 or wider, within the bound.
No kernel may reach another device: no remote copies, remote signals or barrier semaphores. Data moves between devices by JAX's collectives and lax.ppermute only.
A program may use at most 128 MiB of HBM per device.

v0:
```python
import math

import jax
import jax.numpy as jnp
from jax import lax
from jax.experimental import pallas as pl
from jax.experimental.pallas import tpu as pltpu
from jax.sharding import Mesh, PartitionSpec as P


HEADS = 16
HEAD = 48
WIDE = 64
ROWS = 512
WIDTH = 768
NEGATIVE = -1e30
EPSILON = 1e-05
SCALE = math.log2(math.e) / math.sqrt(HEAD)
BF = jnp.bfloat16
F32 = jnp.float32


def norm_rows(x, gain):
    mean = jnp.mean(x, axis=-1, keepdims=True)
    centred = x - mean
    var = jnp.mean(centred * centred, axis=-1, keepdims=True)
    return centred * lax.rsqrt(var + EPSILON) * gain


def lanes(shape):
    return lax.broadcasted_iota(jnp.int32, shape, len(shape) - 1)


def mask_key_value(k, v, first, valid):
    lane = lanes(k.shape)
    special = lane % WIDE == HEAD
    alive = first + lax.broadcasted_iota(jnp.int32, k.shape, 0) < valid
    k = jnp.where(special, jnp.where(alive, 0.0, NEGATIVE), k)
    v = jnp.where(alive, jnp.where(special, 1.0, v), 0.0)
    return k, v


def nt(a, b):
    return lax.dot_general(a, b, (((1,), (1,)), ((), ())), preferred_element_type=F32)


def project_kernel(s_ref, x_ref, gain_ref, w_ref, own_ref, mid_ref, far_ref, normed, stage):
    p = pl.program_id(0)

    @pl.when(p == 0)
    def _():
        normed[...] = norm_rows(x_ref[...].astype(F32), gain_ref[...]).astype(BF)

    rows = normed[...]
    k = jnp.dot(rows, w_ref[0], preferred_element_type=F32).astype(BF).astype(F32)
    v = jnp.dot(rows, w_ref[1], preferred_element_type=F32).astype(BF).astype(F32)
    q = jnp.dot(rows, w_ref[2], preferred_element_type=F32).astype(BF).astype(F32)
    k, v = mask_key_value(k, v, s_ref[1] * ROWS, s_ref[0])
    q = jnp.where(lanes(q.shape) % WIDE == HEAD, 1.0, q)
    stage[0] = k
    stage[1] = v
    stage[2] = q
    own_ref[0] = k.astype(BF)
    own_ref[1] = v.astype(BF)
    own_ref[2] = q.astype(BF)
    low = lanes((ROWS // 4, 128)) < WIDE
    off = [s_ref[2 + 2 * p + a] for a in range(2)]
    for j in range(3):
        first = stage[j, pl.ds(off[0] % 4, ROWS // 4, stride=4), :]
        second = stage[j, pl.ds(off[1] % 4, ROWS // 4, stride=4), :]
        chosen = jnp.where(low, first, second).astype(BF).T
        mid_ref[0, j, :HEAD] = chosen[:HEAD]
        mid_ref[0, j, HEAD:] = chosen[WIDE : WIDE + HEAD]
    low = lanes((ROWS // 16, 128)) < WIDE
    for a in range(2):
        k, v, q = [stage[j, pl.ds(off[a] % 16, ROWS // 16, stride=16), :] for j in range(3)]
        if a == 0:
            v = pltpu.roll(v, WIDE, 1)
            q_high = pltpu.roll(q, WIDE, 1)
        else:
            k = pltpu.roll(k, WIDE, 1)
            q_high = q
            q = pltpu.roll(q, WIDE, 1)
        far_ref[a, :32] = jnp.where(low, k, v).astype(BF)
        far_ref[a, 32:] = jnp.where(low[:16], q[:16], q_high[16:]).astype(BF)


def project(scalars, rows, gain, weights):
    return pl.pallas_call(
        project_kernel,
        grid_spec=pltpu.PrefetchScalarGridSpec(
            num_scalar_prefetch=1,
            grid=(8,),
            in_specs=[
                pl.BlockSpec((ROWS, WIDTH), lambda p, s: (0, 0)),
                pl.BlockSpec((1, WIDTH), lambda p, s: (0, 0)),
                pl.BlockSpec((3, WIDTH, 128), lambda p, s: (0, 0, p)),
            ],
            out_specs=[
                pl.BlockSpec((3, ROWS, 128), lambda p, s: (0, 0, p)),
                pl.BlockSpec((1, 3, 96, 128), lambda p, s: (p, 0, 0, 0)),
                pl.BlockSpec((2, 48, 128), lambda p, s: (p, 0, 0)),
            ],
            scratch_shapes=[pltpu.VMEM((ROWS, WIDTH), BF), pltpu.VMEM((3, ROWS, 128), F32)],
        ),
        out_shape=[
            jax.ShapeDtypeStruct((3, ROWS, 1024), BF),
            jax.ShapeDtypeStruct((8, 3, 96, 128), BF),
            jax.ShapeDtypeStruct((16, 48, 128), BF),
        ],
        name="project",
    )(scalars, rows, gain, weights)


def attend(s, values_t):
    m = jnp.max(s, axis=0, keepdims=True)
    p = jnp.exp2(s * SCALE - m * SCALE).astype(BF)
    return jnp.dot(values_t, p, preferred_element_type=F32), m


def near_kernel(s_ref, x_ref, gain_ref, w_ref, own_ref, out_ref, normed):
    p = pl.program_id(0)

    @pl.when(p == 0)
    def _():
        normed[...] = norm_rows(x_ref[...].astype(F32), gain_ref[...]).astype(BF)

    rows = normed[...]
    k = jnp.dot(rows, w_ref[0], preferred_element_type=F32).astype(BF).astype(F32)
    v = jnp.dot(rows, w_ref[1], preferred_element_type=F32).astype(BF).astype(F32)
    partner = s_ref[1] + 1 - 2 * (s_ref[1] % 2)
    k, v = mask_key_value(k, v, partner * ROWS, s_ref[0])
    keys = jnp.concatenate([own_ref[0], k.astype(BF)], axis=0)
    values_t = jnp.concatenate([own_ref[1], v.astype(BF)], axis=0).T
    queries = own_ref[2]
    for a in range(2):
        for c in range(0, ROWS, 256):
            part = queries[c : c + 256]
            part = jnp.where(lanes(part.shape) // WIDE == a, part, jnp.zeros_like(part))
            numer, m = attend(nt(keys, part), values_t[a * WIDE : (a + 1) * WIDE])
            row = lax.broadcasted_iota(jnp.int32, numer.shape, 0)
            out_ref[a, :, c : c + 256] = jnp.where(row == HEAD + 1, m, numer)


def near(scalars, rows, gain, weights, own, first, count):
    return pl.pallas_call(
        near_kernel,
        grid_spec=pltpu.PrefetchScalarGridSpec(
            num_scalar_prefetch=1,
            grid=(count,),
            in_specs=[
                pl.BlockSpec((ROWS, WIDTH), lambda p, s: (0, 0)),
                pl.BlockSpec((1, WIDTH), lambda p, s: (0, 0)),
                pl.BlockSpec((2, WIDTH, 128), lambda p, s: (0, 0, p + first)),
                pl.BlockSpec((3, ROWS, 128), lambda p, s: (0, 0, p + first)),
            ],
            out_specs=pl.BlockSpec((2, WIDE, ROWS), lambda p, s: (p, 0, 0)),
            scratch_shapes=[pltpu.VMEM((ROWS, WIDTH), BF)],
        ),
        out_shape=jax.ShapeDtypeStruct((2 * count, WIDE, ROWS), F32),
        cost_estimate=pl.CostEstimate(
            flops=5_000_000_000 * count,
            bytes_accessed=1_000_000 * count,
            transcendentals=1_050_000 * count,
        ),
        name="near",
    )(scalars, rows, gain, weights, own)


def to_lse(numer, m):
    total = numer[HEAD : HEAD + 1]
    lse = jnp.where(total > 0.0, m * SCALE + jnp.log2(jnp.maximum(total, 1.0)), NEGATIVE)
    return numer / jnp.maximum(total, 1.0), lse


def packed_result(numer, m):
    mean, lse = to_lse(numer, m)
    high = lse.astype(BF).astype(F32)
    rest = lse - high
    second = rest.astype(BF).astype(F32)
    third = rest - second
    row = lax.broadcasted_iota(jnp.int32, mean.shape, 0)
    out = jnp.where(row < HEAD, mean, 0.0)
    out = jnp.where(row == HEAD, high, out)
    out = jnp.where(row == HEAD + 1, second, out)
    return jnp.where(row == HEAD + 2, third, out)


def middle_kernel(s_ref, in_ref, out_ref, keys_t, values_t, queries_t):
    column = s_ref[1] // 8
    pair = s_ref[1] % 8
    row = lax.broadcasted_iota(jnp.int32, (WIDE - HEAD, 1024), 0)
    for a in range(2):
        base = a * WIDE
        for i in range(8):
            part = slice(i * 128, (i + 1) * 128)
            for j, ref in enumerate((keys_t, values_t, queries_t)):
                ref[base : base + HEAD, part] = in_ref[i, j, a * HEAD : (a + 1) * HEAD]
        place = column * 4096 + s_ref[2 + 2 * pair + a] % 4 + 4 * lanes(row.shape)
        alive = place < s_ref[0]
        spare = slice(base + HEAD, base + WIDE)
        first = row == 0
        keys_t[spare] = jnp.where(first & (~alive), NEGATIVE, 0.0).astype(BF)
        values_t[spare] = jnp.where(first & alive, 1.0, 0.0).astype(BF)
        queries_t[spare] = jnp.where(first, 1.0, 0.0).astype(BF)
        alive = column * 4096 + s_ref[2 + 2 * pair + a] % 4 + 4 * lanes((HEAD, 1024)) < s_ref[0]
        values = values_t[base : base + HEAD]
        values_t[base : base + HEAD] = jnp.where(alive, values, jnp.zeros_like(values))
    keys = keys_t[...].T
    for c in range(0, 1024, 256):
        queries = queries_t[:, c : c + 256]
        head = lax.broadcasted_iota(jnp.int32, queries.shape, 0) // WIDE
        for a in range(2):
            part = jnp.where(head == a, queries, jnp.zeros_like(queries))
            s = jnp.dot(keys, part, preferred_element_type=F32)
            numer, m = attend(s, values_t[a * WIDE : (a + 1) * WIDE])
            out = packed_result(numer, m).astype(BF)
            for i in range(2):
                out_ref[c // 128 + i, a * WIDE : (a + 1) * WIDE] = out[:, i * 128 : (i + 1) * 128]


def middle(scalars, received):
    return pl.pallas_call(
        middle_kernel,
        grid_spec=pltpu.PrefetchScalarGridSpec(
            num_scalar_prefetch=1,
            grid=(1,),
            in_specs=[pl.BlockSpec((8, 3, 96, 128), lambda i, s: (0, 0, 0, 0))],
            out_specs=pl.BlockSpec((8, 128, 128), lambda i, s: (0, 0, 0)),
            scratch_shapes=[pltpu.VMEM((128, 1024), BF)] * 3,
        ),
        out_shape=jax.ShapeDtypeStruct((8, 128, 128), BF),
        cost_estimate=pl.CostEstimate(
            flops=10_000_000_000, bytes_accessed=1_000_000, transcendentals=2_100_000
        ),
        name="middle",
    )(scalars, received)


def far_kernel(*refs):
    key_refs = refs[:8]
    in_ref, out_ref, scores, values_t = refs[8:]
    for c in range(8):
        values_t[:, 512 * c : 512 * c + 512] = key_refs[c][...].reshape(512, 128).T[WIDE:]
    packed = in_ref[:, 32:48].reshape(256, 128)
    low = lanes(packed.shape) < WIDE
    for half in range(2):
        queries = packed.astype(F32)
        if half:
            queries = pltpu.roll(queries, WIDE, 1)
        queries = jnp.where(low, queries, 0.0).astype(BF)
        m = jnp.full((1, 256), NEGATIVE, F32)
        for c in range(8):
            s = nt(key_refs[c][...].reshape(512, 128), queries)
            scores[c] = s
            m = jnp.maximum(m, jnp.max(s, axis=0, keepdims=True))
        numer = jnp.zeros((WIDE, 256), F32)
        for c in range(8):
            shift = m * SCALE - (1.0 if c < 2 else 0.0)
            p = jnp.exp2(scores[c] * SCALE - shift).astype(BF)
            numer += jnp.dot(
                values_t[:, 512 * c : 512 * c + 512], p, preferred_element_type=F32
            )
        out = packed_result(numer, m)
        out = jnp.concatenate([out, jnp.zeros_like(out)], axis=0).T
        out_ref[:, 16 * half : 16 * half + 16] = out.astype(BF).reshape(16, 16, 128)


def far(keys, received):
    return pl.pallas_call(
        far_kernel,
        out_shape=jax.ShapeDtypeStruct((16, 32, 128), BF),
        scratch_shapes=[pltpu.VMEM((8, 512, 256), F32), pltpu.VMEM((WIDE, 4096), BF)],
        cost_estimate=pl.CostEstimate(
            flops=10_000_000_000, bytes_accessed=1_000_000, transcendentals=2_100_000
        ),
        name="far",
    )(*keys, received)


def finish_kernel(s_ref, near0_ref, near1_ref, near2_ref, mid_ref, far_ref, x_ref, gain_ref, w_ref, out_ref, mixed):
    lane = lanes((1, ROWS))
    column4 = lanes((128, ROWS)) - 4 * lax.broadcasted_iota(jnp.int32, (128, ROWS), 0)
    column16 = lanes((32, ROWS)) - 16 * lax.broadcasted_iota(jnp.int32, (32, ROWS), 0)
    for h in range(HEADS):
        off = s_ref[2 + h]
        off4 = off % 4
        off16 = off % 16
        near_ref = (near0_ref, near1_ref, near2_ref)[h // 6]
        mean_n, lse_n = to_lse(near_ref[h % 6], near_ref[h % 6, HEAD + 1 : HEAD + 2])
        a = h % 2
        spread4 = jnp.where(column4 == off4, 1.0, 0.0).astype(BF)
        mid = jnp.dot(
            mid_ref[h // 2, a * WIDE : (a + 1) * WIDE], spread4, preferred_element_type=F32
        )
        spread16 = jnp.where(column16 == off16, 1.0, 0.0).astype(BF)
        distant = lax.dot_general(
            far_ref[h], spread16, (((0,), (0,)), ((), ())), preferred_element_type=F32
        )

        def lse_of(spread):
            lse = spread[HEAD : HEAD + 1] + spread[HEAD + 1 : HEAD + 2]
            return lse + spread[HEAD + 2 : HEAD + 3]

        lse_m = jnp.where(lane % 4 == off4, lse_of(mid), NEGATIVE)
        lse_f = jnp.where(lane % 16 == off16, lse_of(distant), NEGATIVE)
        top = jnp.maximum(jnp.maximum(lse_n, lse_m), lse_f)
        weight_n = jnp.exp2(lse_n - top)
        weight_m = jnp.exp2(lse_m - top)
        weight_f = jnp.exp2(lse_f - top)
        inverse = 1.0 / jnp.maximum(weight_n + weight_m + weight_f, 1.0)
        mixed[HEAD * h : HEAD * (h + 1)] = (
            mean_n[:HEAD] * (weight_n * inverse)
            + mid[:HEAD] * (weight_m * inverse)
            + distant[:HEAD] * (weight_f * inverse)
        ).astype(BF)
    attended = mixed[...].T.astype(F32)
    sub = norm_rows(attended, gain_ref[...]).astype(BF)
    out = x_ref[...].astype(F32) + jnp.dot(sub, w_ref[...], preferred_element_type=F32)
    out_ref[...] = out.astype(BF)


def finish(scalars, near_results, mid_result, far_result, rows, gain, w_out):
    def whole(*shape):
        return pl.BlockSpec(shape, lambda i, s: (0,) * len(shape))

    return pl.pallas_call(
        finish_kernel,
        grid_spec=pltpu.PrefetchScalarGridSpec(
            num_scalar_prefetch=1,
            grid=(1,),
            in_specs=[
                whole(6, WIDE, ROWS),
                whole(6, WIDE, ROWS),
                whole(4, WIDE, ROWS),
                whole(8, 128, 128),
                whole(16, 32, 128),
                whole(ROWS, WIDTH),
                whole(1, WIDTH),
                whole(WIDTH, WIDTH),
            ],
            out_specs=whole(ROWS, WIDTH),
            scratch_shapes=[pltpu.VMEM((WIDTH, ROWS), BF)],
        ),
        out_shape=jax.ShapeDtypeStruct((ROWS, WIDTH), BF),
        name="finish",
    )(scalars, *near_results, mid_result, far_result, rows, gain, w_out)


def exchange(value, axis):
    return lax.all_to_all(value, axis, split_axis=0, concat_axis=0, tiled=True)


def body(tile_embed, valid_tiles, offsets, norm_gain, w_qkv, sub_gain, w_out):
    position = lax.axis_index(("y", "xh", "xl", "z"))
    scalars = jnp.concatenate([valid_tiles, position.astype(jnp.int32)[None], offsets])
    arrived = exchange(tile_embed.reshape(128, 4, WIDTH), ("y", "xh", "xl", "z"))
    rows = arrived.transpose(1, 0, 2).reshape(ROWS, WIDTH)
    partner = lax.ppermute(rows, "z", [(i, i ^ 1) for i in range(8)])
    wide = w_qkv.reshape(WIDTH, 3, HEADS, HEAD)
    wide = jnp.pad(wide, ((0, 0), (0, 0), (0, 0), (0, WIDE - HEAD))).reshape(WIDTH, 3, 1024)
    weights = jnp.stack([wide[:, 1], wide[:, 2], wide[:, 0]])
    gain = norm_gain[None]
    own, mid_send, far_send = project(scalars, rows, gain, weights)
    received = exchange(far_send, ("xl", "z"))
    mine = received[:, :32]
    keys = [mine]
    for y in range(4):
        for xh in range(2):
            if y or xh:
                moves = [
                    (2 * i + j, 2 * ((i + y) % 4) + (j ^ xh)) for i in range(4) for j in range(2)
                ]
                keys.append(lax.ppermute(mine, ("y", "xh"), moves))
    mid = exchange(mid_send, "z")
    near_results = []
    for first, count in ((0, 3), (3, 3), (6, 2)):
        near_results.append(near(scalars, partner, gain, weights, own, first, count))
    mid_result = middle(scalars, mid)
    far_result = far(keys, received)
    mid_result = exchange(mid_result, "z")
    far_result = exchange(far_result, ("xl", "z"))
    return finish(
        scalars, near_results, mid_result, far_result, rows, sub_gain[None], w_out
    )


def solution(mesh):
    inner = Mesh(mesh.devices.reshape(4, 2, 2, 8, 2), ("y", "xh", "xl", "z", "slide"))
    split = P(("slide", "y", "xh", "xl", "z"), None)
    return jax.shard_map(
        body,
        mesh=inner,
        in_specs=(split, P("slide"), P(), P(), P(), P(), P()),
        out_specs=split,
        check_vma=False,
    )
```

profile of v0, /device:TPU:38, one launch (start us, length us, event | category | flops | bytes accessed | tf_op | source)
XLA Modules:
  0.0 185.3 jit_solution(1709907059278531229)
XLA Ops:
  0.0 2.4 %reshape.12 = bf16[128,4,768]{2,1,0:T(4,128)(2,1)} reshape(bf16[512,768]{1,0:T(8,128)(2,1)} %param.7) | data formatting | bytes 1572864 | tf_op jit(solution)/shard_map/reshape | solution.py:357
  2.4 15.4 %all-to-all-start = ((bf16[128,4,768]{2,1,0:T(4,128)(2,1)}), bf16[128,4,768]{2,1,0:T(4,128)(2,1)}, u32[]{:S(2)}, u32[]{:S(2)}) async-start(bf16[128,4,768]{2,1,0:T(4,128)(2,1)} %reshape.12), calls=%async_computation | async-start | bytes 1572864 | tf_op jit(solution)/shard_map/all_to_all | solution.py:351
  18.4 0.6 broadcast_in_dim.10.gain_ref
  19.0 4.5 %copy.16 = bf16[768,2304]{0,1:T(8,128)(2,1)S(1)} copy(bf16[768,2304]{1,0:T(8,128)(2,1)} %param.11) | data formatting | bytes 7077888 | tf_op args[4]
  23.5 0.6 pad.4
  24.2 2.0 %fusion = (bf16[768,1,1024]{0,2,1:T(8,128)(2,1)S(1)}, bf16[768,1,1024]{0,2,1:T(8,128)(2,1)}, bf16[768,1,1024]{0,2,1:T(8,128)(2,1)}) fusion(bf16[768,3,1024]{0,2,1:T(8,128)(2,1)S(1)} %bitcast.8), kind=kLoop, calls=%fused_computation.2 | loop fusion | bytes 9437184 | tf_op jit(solution)/shard_map/slice | solution.py:362
  26.1 0.7 copy.20
  26.9 1.7 copy.21
  28.6 0.0 copy-start.8
  28.6 2.6 %copy.22 = bf16[768,1,1024]{2,0,1:T(8,128)(2,1)} copy(bf16[768,1,1024]{0,2,1:T(8,128)(2,1)} %get-tuple-element.13) | data formatting | bytes 3145728
  31.2 0.6 pad_add_fusion.s_ref
  31.9 3.6 %pad_maximum_fusion.w_ref = bf16[3,768,1024]{2,1,0:T(8,128)(2,1)} fusion(bf16[1,768,1024]{2,1,0:T(8,128)(2,1)} %bitcast.15, bf16[1,768,1024]{2,1,0:T(8,128)(2,1)S(1)} %bitcast.14, bf16[1,768,1024]{2,1,0:T(8,128)(2,1)S(1)} %bitcast.13), kind=kLoop, calls=%fused_computation | loop fusion | flops 4718592 | bytes 9437184 | tf_op jit(solution)/shard_map/stack | solution.py:362
  35.4 5.3 %all-to-all-done = bf16[128,4,768]{2,1,0:T(4,128)(2,1)} async-done(((bf16[128,4,768]{2,1,0:T(4,128)(2,1)}), bf16[128,4,768]{2,1,0:T(4,128)(2,1)}, u32[]{:S(2)}, u32[]{:S(2)}) %all-to-all-start) | async-done | bytes 786464 | tf_op jit(solution)/shard_map/all_to_all | solution.py:351
  40.7 2.1 %copy.15 = bf16[4,128,768]{2,1,0:T(8,128)(2,1)} copy(bf16[4,128,768]{2,0,1:T(4,128)(2,1)} %bitcast.1) | data formatting | bytes 1572864 | tf_op jit(solution)/shard_map/transpose | solution.py:358
  42.8 11.4 %project.1 = (bf16[3,512,1024]{2,1,0:T(8,128)(2,1)}, bf16[8,3,96,128]{3,2,1,0:T(8,128)(2,1)}, bf16[16,48,128]{2,1,0:T(8,128)(2,1)}) custom-call(s32[18]{0:T(128)} %pad_add_fusion.s_ref, bf16[512,768]{1,0:T(8,128)(2,1)} %bitcast.10, f32[1,768]{1,0:T(1,128)} %broadcast_in_dim.10.gain_ref, bf16[3,768,1024]{2,1,0:T(8,128)(2,1)} %pad_maximum_fusion.w_ref), custom_call_target="tpu_custom_call" | custom-call | tf_op jit(solution)/shard_map/project/pallas_call | solution.py:89
  54.2 13.1 %all_to_all.25.refs_8_ = bf16[16,48,128]{2,1,0:T(8,128)(2,1)S(1)} all-to-all(bf16[16,48,128]{2,1,0:T(8,128)(2,1)} %get-tuple-element.10), channel_id=1, replica_groups=mesh['y'=4,'xh'=2,'xl'=2,'z'=8,'slide'=2] {'xl','z'}, dimensions={0} | all-to-all | bytes 393216 | tf_op jit(solution)/shard_map/all_to_all | solution.py:351
  67.4 4.1 %collective-permute-start.7 = (bf16[16,32,128]{2,1,0:T(8,128)(2,1)S(1)}, bf16[16,32,128]{2,1,0:T(8,128)(2,1)S(1)}, u32[]{:S(2)}, u32[]{:S(2)}) collective-permute-start(bf16[16,32,128]{2,1,0:T(8,128)(2,1)S(1)} %slice.19.refs_0_), channel_id=1, source_target_pairs={{0,224},{32,192},{64,32},{96,0},{128,96},{160,64},{192,160},{224,1... | collective-permute-start | bytes 393224 | tf_op jit(solution)/shard_map/ppermute | solution.py:374
  71.5 0.4 collective-permute-start.6
  71.8 2.1 %collective-permute-start.5 = (bf16[16,32,128]{2,1,0:T(8,128)(2,1)S(1)}, bf16[16,32,128]{2,1,0:T(8,128)(2,1)S(1)}, u32[]{:S(2)}, u32[]{:S(2)}) collective-permute-start(bf16[16,32,128]{2,1,0:T(8,128)(2,1)S(1)} %slice.19.refs_0_), channel_id=1, source_target_pairs={{0,160},{32,128},{64,224},{96,192},{128,32},{160,0},{192,96},{224,... | collective-permute-start | bytes 393224 | tf_op jit(solution)/shard_map/ppermute | solution.py:374
  74.0 1.4 collective-permute-start.4
  75.4 4.1 %collective-permute-start.3 = (bf16[16,32,128]{2,1,0:T(8,128)(2,1)S(1)}, bf16[16,32,128]{2,1,0:T(8,128)(2,1)S(1)}, u32[]{:S(2)}, u32[]{:S(2)}) collective-permute-start(bf16[16,32,128]{2,1,0:T(8,128)(2,1)S(1)} %slice.19.refs_0_), channel_id=1, source_target_pairs={{0,96},{32,64},{64,160},{96,128},{128,224},{160,192},{192,32},{224... | collective-permute-start | bytes 393224 | tf_op jit(solution)/shard_map/ppermute | solution.py:374
  79.4 0.0 collective-permute-done.7.refs_7_
  79.5 1.4 collective-permute-start.2
  80.9 0.7 collective-permute-start.1
  81.6 0.6 broadcast_in_dim.11.gain_ref
  82.2 4.0 %all-to-all-start.1 = ((bf16[8,3,96,128]{3,2,1,0:T(8,128)(2,1)}), bf16[8,3,96,128]{3,2,1,0:T(8,128)(2,1)S(1)}, u32[]{:S(2)}, u32[]{:S(2)}) async-start(bf16[8,3,96,128]{3,2,1,0:T(8,128)(2,1)} %get-tuple-element.9), calls=%async_computation.1 | async-start | bytes 1179648 | tf_op jit(solution)/shard_map/all_to_all | solution.py:351
  86.2 0.0 collective-permute-done.5.refs_5_
  86.2 0.3 collective-permute-start
  86.5 0.0 collective-permute-done.4.refs_4_
  86.5 0.0 collective-permute-done.3.refs_3_
  86.6 0.5 collective-permute-done.2.refs_2_
  87.1 0.2 collective-permute-done.1.refs_1_
  87.4 0.4 copy-done.15
  87.8 0.7 copy-done.16
  88.4 6.1 %far.1 = bf16[16,32,128]{2,1,0:T(8,128)(2,1)} custom-call(bf16[16,32,128]{2,1,0:T(8,128)(2,1)} %copy-done.5, bf16[16,32,128]{2,1,0:T(8,128)(2,1)} %copy-done.16, bf16[16,32,128]{2,1,0:T(8,128)(2,1)} %copy-done.15, bf16[16,32,128]{2,1,0:T(8,128)(2,1)} %copy-done.14, bf16[16,32,128]{2,1,0:T(8,128)(2,1)} %copy-done.13, bf16[16,32,128]{2,1,0:T(8,128)(2,1)} %copy-done.12, ...), custom_call_target="tpu_custom_call" | custom-call | flops 10000000000 | bytes 1000000 | tf_op jit(solution)/shard_map/far/pallas_call | solution.py:270
  94.5 20.3 %collective-permute-done.x_ref = bf16[512,768]{1,0:T(8,128)(2,1)S(1)} collective-permute-done((bf16[512,768]{1,0:T(8,128)(2,1)S(1)}, bf16[512,768]{1,0:T(8,128)(2,1)S(1)}, u32[]{:S(2)}, u32[]{:S(2)}) %collective-permute-start) | collective-permute-done | bytes 786464 | tf_op jit(solution)/shard_map/ppermute | solution.py:359
  114.8 0.9 copy-done.9
  115.6 14.2 %near.4.near1_ref = f32[6,64,512]{2,1,0:T(8,128)} custom-call(s32[18]{0:T(128)} %pad_add_fusion.s_ref, bf16[512,768]{1,0:T(8,128)(2,1)} %copy-done.9, f32[1,768]{1,0:T(1,128)} %broadcast_in_dim.10.gain_ref, bf16[3,768,1024]{2,1,0:T(8,128)(2,1)} %pad_maximum_fusion.w_ref, bf16[3,512,1024]{2,1,0:T(8,128)(2,1)} %get-tuple-element.8.own_ref), custom_call_target="tpu_custom_call" | custom-call | flops 15000000512 | bytes 3000000 | tf_op jit(solution)/shard_map/near/pallas_call | solution.py:146
  129.8 14.2 %near.3.near0_ref = f32[6,64,512]{2,1,0:T(8,128)} custom-call(s32[18]{0:T(128)} %pad_add_fusion.s_ref, bf16[512,768]{1,0:T(8,128)(2,1)} %copy-done.9, f32[1,768]{1,0:T(1,128)} %broadcast_in_dim.10.gain_ref, bf16[3,768,1024]{2,1,0:T(8,128)(2,1)} %pad_maximum_fusion.w_ref, bf16[3,512,1024]{2,1,0:T(8,128)(2,1)} %get-tuple-element.8.own_ref), custom_call_target="tpu_custom_call" | custom-call | flops 15000000512 | bytes 3000000 | tf_op jit(solution)/shard_map/near/pallas_call | solution.py:146
  144.0 0.0 all-to-all-done.1.in_ref
  144.0 8.4 %all-to-all-start.4 = ((bf16[16,32,128]{2,1,0:T(8,128)(2,1)}), bf16[16,32,128]{2,1,0:T(8,128)(2,1)S(1)}, u32[]{:S(2)}, u32[]{:S(2)}) async-start(bf16[16,32,128]{2,1,0:T(8,128)(2,1)} %far.1), calls=%async_computation.4 | async-start | bytes 262144 | tf_op jit(solution)/shard_map/all_to_all | solution.py:351
  152.4 8.3 %middle.1 = bf16[8,128,128]{2,1,0:T(8,128)(2,1)} custom-call(s32[18]{0:T(128)} %pad_add_fusion.s_ref, bf16[8,3,96,128]{3,2,1,0:T(8,128)(2,1)} %copy-done.2), custom_call_target="tpu_custom_call" | custom-call | flops 10000000000 | bytes 1000000 | tf_op jit(solution)/shard_map/middle/pallas_call | solution.py:223
  160.7 0.0 all-to-all-done.4.far_ref
  160.7 7.2 %all-to-all-start.2 = ((bf16[8,128,128]{2,1,0:T(8,128)(2,1)}), bf16[8,128,128]{2,1,0:T(8,128)(2,1)S(1)}, u32[]{:S(2)}, u32[]{:S(2)}) async-start(bf16[8,128,128]{2,1,0:T(8,128)(2,1)} %middle.1), calls=%async_computation.2 | async-start | bytes 524288 | tf_op jit(solution)/shard_map/all_to_all | solution.py:351
  167.9 10.6 %near.5.near2_ref = f32[4,64,512]{2,1,0:T(8,128)} custom-call(s32[18]{0:T(128)} %pad_add_fusion.s_ref, bf16[512,768]{1,0:T(8,128)(2,1)} %copy-done.9, f32[1,768]{1,0:T(1,128)} %broadcast_in_dim.10.gain_ref, bf16[3,768,1024]{2,1,0:T(8,128)(2,1)} %pad_maximum_fusion.w_ref, bf16[3,512,1024]{2,1,0:T(8,128)(2,1)} %get-tuple-element.8.own_ref), custom_call_target="tpu_custom_call" | custom-call | flops 10000000000 | bytes 2000000 | tf_op jit(solution)/shard_map/near/pallas_call | solution.py:146
  178.5 0.0 all-to-all-done.2.mid_ref
  178.5 0.7 copy-done.1
  179.2 6.1 %finish.1 = bf16[512,768]{1,0:T(8,128)(2,1)} custom-call(s32[18]{0:T(128)} %pad_add_fusion.s_ref, f32[6,64,512]{2,1,0:T(8,128)} %near.3.near0_ref, f32[6,64,512]{2,1,0:T(8,128)} %near.4.near1_ref, f32[4,64,512]{2,1,0:T(8,128)} %near.5.near2_ref, bf16[8,128,128]{2,1,0:T(8,128)(2,1)} %copy-done.1, bf16[16,32,128]{2,1,0:T(8,128)(2,1)} %copy-done.4, ...), custom_call_target="tpu_custom_call" | custom-call | tf_op jit(solution)/shard_map/finish/pallas_call | solution.py:327
  (31 shorter events, 0.1 us)
Async XLA Ops:
  0.0 18.4 %copy-start.6 = (f32[768]{0:T(1024)S(1)}, f32[768]{0:T(1024)}, u32[]{:S(2)}) copy-start(f32[768]{0:T(1024)} %param.10) | copy-start | bytes 9220
  2.4 38.3 %all-to-all-start = ((bf16[128,4,768]{2,1,0:T(4,128)(2,1)}), bf16[128,4,768]{2,1,0:T(4,128)(2,1)}, u32[]{:S(2)}, u32[]{:S(2)}) async-start(bf16[128,4,768]{2,1,0:T(4,128)(2,1)} %reshape.12), calls=%async_computation | async-start | bytes 1572864 | tf_op jit(solution)/shard_map/all_to_all | solution.py:351
  28.6 2.6 %copy-start.8 = (s32[16]{0:T(128)S(1)}, s32[16]{0:T(128)}, u32[]{:S(2)}) copy-start(s32[16]{0:T(128)} %param.9) | copy-start | bytes 196
  42.8 38.8 %copy-start.7 = (f32[768]{0:T(1024)S(1)}, f32[768]{0:T(1024)}, u32[]{:S(2)}) copy-start(f32[768]{0:T(1024)} %param.12) | copy-start | bytes 9220
  54.2 32.0 %copy-start = (bf16[4,128,768]{2,1,0:T(8,128)(2,1)S(1)}, bf16[4,128,768]{2,1,0:T(8,128)(2,1)}, u32[]{:S(2)}) copy-start(bf16[4,128,768]{2,1,0:T(8,128)(2,1)} %copy.15) | copy-start | bytes 2359300
  67.4 20.0 %copy-start.3 = (bf16[16,48,128]{2,1,0:T(8,128)(2,1)}, bf16[16,48,128]{2,1,0:T(8,128)(2,1)S(1)}, u32[]{:S(2)}) copy-start(bf16[16,48,128]{2,1,0:T(8,128)(2,1)S(1)} %all_to_all.25.refs_8_) | copy-start | bytes 589828
  67.4 20.0 %copy-start.5 = (bf16[16,32,128]{2,1,0:T(8,128)(2,1)}, bf16[16,32,128]{2,1,0:T(8,128)(2,1)S(1)}, u32[]{:S(2)}) copy-start(bf16[16,32,128]{2,1,0:T(8,128)(2,1)S(1)} %slice.19.refs_0_) | copy-start | bytes 393220
  67.4 12.1 %collective-permute-start.7 = (bf16[16,32,128]{2,1,0:T(8,128)(2,1)S(1)}, bf16[16,32,128]{2,1,0:T(8,128)(2,1)S(1)}, u32[]{:S(2)}, u32[]{:S(2)}) collective-permute-start(bf16[16,32,128]{2,1,0:T(8,128)(2,1)S(1)} %slice.19.refs_0_), channel_id=1, source_target_pairs={{0,224},{32,192},{64,32},{96,0},{128,96},{160,64},{192,160},{224,1... | collective-permute-start | bytes 393224 | tf_op jit(solution)/shard_map/ppermute | solution.py:374
  71.5 9.4 %collective-permute-start.6 = (bf16[16,32,128]{2,1,0:T(8,128)(2,1)S(1)}, bf16[16,32,128]{2,1,0:T(8,128)(2,1)S(1)}, u32[]{:S(2)}, u32[]{:S(2)}) collective-permute-start(bf16[16,32,128]{2,1,0:T(8,128)(2,1)S(1)} %slice.19.refs_0_), channel_id=1, source_target_pairs={{0,192},{32,224},{64,0},{96,32},{128,64},{160,96},{192,128},{224,1... | collective-permute-start | bytes 393224 | tf_op jit(solution)/shard_map/ppermute | solution.py:374
  71.8 14.4 %collective-permute-start.5 = (bf16[16,32,128]{2,1,0:T(8,128)(2,1)S(1)}, bf16[16,32,128]{2,1,0:T(8,128)(2,1)S(1)}, u32[]{:S(2)}, u32[]{:S(2)}) collective-permute-start(bf16[16,32,128]{2,1,0:T(8,128)(2,1)S(1)} %slice.19.refs_0_), channel_id=1, source_target_pairs={{0,160},{32,128},{64,224},{96,192},{128,32},{160,0},{192,96},{224,... | collective-permute-start | bytes 393224 | tf_op jit(solution)/shard_map/ppermute | solution.py:374
  74.0 12.6 %collective-permute-start.4 = (bf16[16,32,128]{2,1,0:T(8,128)(2,1)S(1)}, bf16[16,32,128]{2,1,0:T(8,128)(2,1)S(1)}, u32[]{:S(2)}, u32[]{:S(2)}) collective-permute-start(bf16[16,32,128]{2,1,0:T(8,128)(2,1)S(1)} %slice.19.refs_0_), channel_id=1, source_target_pairs={{0,128},{32,160},{64,192},{96,224},{128,0},{160,32},{192,64},{224,... | collective-permute-start | bytes 393224 | tf_op jit(solution)/shard_map/ppermute | solution.py:374
  75.4 11.2 %collective-permute-start.3 = (bf16[16,32,128]{2,1,0:T(8,128)(2,1)S(1)}, bf16[16,32,128]{2,1,0:T(8,128)(2,1)S(1)}, u32[]{:S(2)}, u32[]{:S(2)}) collective-permute-start(bf16[16,32,128]{2,1,0:T(8,128)(2,1)S(1)} %slice.19.refs_0_), channel_id=1, source_target_pairs={{0,96},{32,64},{64,160},{96,128},{128,224},{160,192},{192,32},{224... | collective-permute-start | bytes 393224 | tf_op jit(solution)/shard_map/ppermute | solution.py:374
  79.4 7.9 %copy-start.10 = (bf16[16,32,128]{2,1,0:T(8,128)(2,1)}, bf16[16,32,128]{2,1,0:T(8,128)(2,1)S(1)}, u32[]{:S(2)}) copy-start(bf16[16,32,128]{2,1,0:T(8,128)(2,1)S(1)} %collective-permute-done.7.refs_7_) | copy-start | bytes 393220
  79.5 7.7 %collective-permute-start.2 = (bf16[16,32,128]{2,1,0:T(8,128)(2,1)S(1)}, bf16[16,32,128]{2,1,0:T(8,128)(2,1)S(1)}, u32[]{:S(2)}, u32[]{:S(2)}) collective-permute-start(bf16[16,32,128]{2,1,0:T(8,128)(2,1)S(1)} %slice.19.refs_0_), channel_id=1, source_target_pairs={{0,64},{32,96},{64,128},{96,160},{128,192},{160,224},{192,0},{224,... | collective-permute-start | bytes 393224 | tf_op jit(solution)/shard_map/ppermute | solution.py:374
  80.9 6.5 %copy-start.11 = (bf16[16,32,128]{2,1,0:T(8,128)(2,1)}, bf16[16,32,128]{2,1,0:T(8,128)(2,1)S(1)}, u32[]{:S(2)}) copy-start(bf16[16,32,128]{2,1,0:T(8,128)(2,1)S(1)} %collective-permute-done.6.refs_6_) | copy-start | bytes 393220
  80.9 6.5 %collective-permute-start.1 = (bf16[16,32,128]{2,1,0:T(8,128)(2,1)S(1)}, bf16[16,32,128]{2,1,0:T(8,128)(2,1)S(1)}, u32[]{:S(2)}, u32[]{:S(2)}) collective-permute-start(bf16[16,32,128]{2,1,0:T(8,128)(2,1)S(1)} %slice.19.refs_0_), channel_id=1, source_target_pairs={{0,32},{32,0},{64,96},{96,64},{128,160},{160,128},{192,224},{224,1... | collective-permute-start | bytes 393224 | tf_op jit(solution)/shard_map/ppermute | solution.py:374
  82.2 61.8 %all-to-all-start.1 = ((bf16[8,3,96,128]{3,2,1,0:T(8,128)(2,1)}), bf16[8,3,96,128]{3,2,1,0:T(8,128)(2,1)S(1)}, u32[]{:S(2)}, u32[]{:S(2)}) async-start(bf16[8,3,96,128]{3,2,1,0:T(8,128)(2,1)} %get-tuple-element.9), calls=%async_computation.1 | async-start | bytes 1179648 | tf_op jit(solution)/shard_map/all_to_all | solution.py:351
  86.2 1.1 copy-start.12
  86.2 28.5 %collective-permute-start = (bf16[512,768]{1,0:T(8,128)(2,1)S(1)}, bf16[512,768]{1,0:T(8,128)(2,1)S(1)}, u32[]{:S(2)}, u32[]{:S(2)}) collective-permute-start(bf16[512,768]{1,0:T(8,128)(2,1)S(1)} %bitcast.12), channel_id=1, source_target_pairs={{0,2},{2,0},{4,6},{6,4},{8,10},{10,8},{12,14},{14,12},{1,3},{3,1},... | collective-permute-start | bytes 2359304 | tf_op jit(solution)/shard_map/ppermute | solution.py:359
  86.5 0.8 copy-start.13
  86.6 0.8 copy-start.14
  87.1 0.7 copy-start.15
  87.8 0.7 copy-start.16
  114.7 0.9 copy-start.9
  144.0 8.4 %copy-start.2 = (bf16[8,3,96,128]{3,2,1,0:T(8,128)(2,1)}, bf16[8,3,96,128]{3,2,1,0:T(8,128)(2,1)S(1)}, u32[]{:S(2)}) copy-start(bf16[8,3,96,128]{3,2,1,0:T(8,128)(2,1)S(1)} %all-to-all-done.1.in_ref) | copy-start | bytes 1769476
  144.0 16.7 %all-to-all-start.4 = ((bf16[16,32,128]{2,1,0:T(8,128)(2,1)}), bf16[16,32,128]{2,1,0:T(8,128)(2,1)S(1)}, u32[]{:S(2)}, u32[]{:S(2)}) async-start(bf16[16,32,128]{2,1,0:T(8,128)(2,1)} %far.1), calls=%async_computation.4 | async-start | bytes 262144 | tf_op jit(solution)/shard_map/all_to_all | solution.py:351
  160.7 17.8 %copy-start.4 = (bf16[16,32,128]{2,1,0:T(8,128)(2,1)}, bf16[16,32,128]{2,1,0:T(8,128)(2,1)S(1)}, u32[]{:S(2)}) copy-start(bf16[16,32,128]{2,1,0:T(8,128)(2,1)S(1)} %all-to-all-done.4.far_ref) | copy-start | bytes 393220
  160.7 17.8 %all-to-all-start.2 = ((bf16[8,128,128]{2,1,0:T(8,128)(2,1)}), bf16[8,128,128]{2,1,0:T(8,128)(2,1)S(1)}, u32[]{:S(2)}, u32[]{:S(2)}) async-start(bf16[8,128,128]{2,1,0:T(8,128)(2,1)} %middle.1), calls=%async_computation.2 | async-start | bytes 524288 | tf_op jit(solution)/shard_map/all_to_all | solution.py:351
  178.5 0.7 copy-start.1
where the time goes:
time: 186 us; the launch traced here: 185 us
  Pallas kernels  70.8 us (38%)
  starting transfers between devices  49.5 us (27%)
  waiting for transfers between devices  26.3 us (14%)
  local copies, waits for them, and re-layouts  20.5 us (11%)
  blocking collectives  13.1 us (7%)
  other arithmetic  4.17 us (2%)
    pallas_call x3, Pallas kernels, near(): pl.pallas_call(near_kernel, grid_spec=pltpu.PrefetchScalarGridSpec(num_sc...  38.9 us
    all_to_all x4, starting transfers between devices, exchange(): return lax.all_to_all(value, axis, split_axis=0, concat_axis=0, tiled=True)  35 us
    ppermute x1, waiting for transfers between devices, body(): partner = lax.ppermute(rows, 'z', [(i, i ^ 1) for i in range(8)])  20.3 us
    ppermute x7, starting transfers between devices, body(): keys.append(lax.ppermute(mine, ('y', 'xh'), moves))  14.2 us
    all_to_all x1, blocking collectives, exchange(): return lax.all_to_all(value, axis, split_axis=0, concat_axis=0, tiled=True)  13.1 us
    unnamed x38, local copies, waits for them, and re-layouts  12.3 us
    pallas_call x1, Pallas kernels, project(): pl.pallas_call(project_kernel, grid_spec=pltpu.PrefetchScalarGridSpec(num...  11.4 us
    pallas_call x1, Pallas kernels, middle(): pl.pallas_call(middle_kernel, grid_spec=pltpu.PrefetchScalarGridSpec(num_...  8.26 us
  transfers between devices with their start and end apart: 12, of which 4 were waited for; matrix products, arithmetic and copies ran while one was open for 9% of the time, Pallas kernels for 29%

commit v1 on v0

--- a/solution.py
+++ b/solution.py
@@ -44,7 +44,7 @@
     return lax.dot_general(a, b, (((1,), (1,)), ((), ())), preferred_element_type=F32)
 
 
-def project_kernel(s_ref, x_ref, gain_ref, w_ref, own_ref, mid_ref, far_ref, normed, stage):
+def project_kernel(s_ref, x_ref, gain_ref, w_ref, own_ref, send_ref, normed, stage):
     p = pl.program_id(0)
 
     @pl.when(p == 0)
@@ -69,8 +69,8 @@
         first = stage[j, pl.ds(off[0] % 4, ROWS // 4, stride=4), :]
         second = stage[j, pl.ds(off[1] % 4, ROWS // 4, stride=4), :]
         chosen = jnp.where(low, first, second).astype(BF).T
-        mid_ref[0, j, :HEAD] = chosen[:HEAD]
-        mid_ref[0, j, HEAD:] = chosen[WIDE : WIDE + HEAD]
+        for a in range(2):
+            send_ref[a, HEAD * (j + 1) : HEAD * (j + 2)] = chosen[a * WIDE : a * WIDE + HEAD]
     low = lanes((ROWS // 16, 128)) < WIDE
     for a in range(2):
         k, v, q = [stage[j, pl.ds(off[a] % 16, ROWS // 16, stride=16), :] for j in range(3)]
@@ -81,8 +81,8 @@
             k = pltpu.roll(k, WIDE, 1)
             q_high = q
             q = pltpu.roll(q, WIDE, 1)
-        far_ref[a, :32] = jnp.where(low, k, v).astype(BF)
-        far_ref[a, 32:] = jnp.where(low[:16], q[:16], q_high[16:]).astype(BF)
+        send_ref[a, :32] = jnp.where(low, k, v).astype(BF)
+        send_ref[a, 32:48] = jnp.where(low[:16], q[:16], q_high[16:]).astype(BF)
 
 
 def project(scalars, rows, gain, weights):
@@ -98,27 +98,35 @@
             ],
             out_specs=[
                 pl.BlockSpec((3, ROWS, 128), lambda p, s: (0, 0, p)),
-                pl.BlockSpec((1, 3, 96, 128), lambda p, s: (p, 0, 0, 0)),
-                pl.BlockSpec((2, 48, 128), lambda p, s: (p, 0, 0)),
+                pl.BlockSpec((2, 192, 128), lambda p, s: (p, 0, 0)),
             ],
             scratch_shapes=[pltpu.VMEM((ROWS, WIDTH), BF), pltpu.VMEM((3, ROWS, 128), F32)],
         ),
         out_shape=[
             jax.ShapeDtypeStruct((3, ROWS, 1024), BF),
-            jax.ShapeDtypeStruct((8, 3, 96, 128), BF),
-            jax.ShapeDtypeStruct((16, 48, 128), BF),
+            jax.ShapeDtypeStruct((16, 192, 128), BF),
         ],
         name="project",
     )(scalars, rows, gain, weights)
 
 
-def attend(s, values_t):
-    m = jnp.max(s, axis=0, keepdims=True)
-    p = jnp.exp2(s * SCALE - m * SCALE).astype(BF)
-    return jnp.dot(values_t, p, preferred_element_type=F32), m
-
-
-def near_kernel(s_ref, x_ref, gain_ref, w_ref, own_ref, out_ref, normed):
+def attend(score, values_t, scores, weights, bonus=()):
+    blocks = scores.shape[0] // 256
+    m = None
+    for c in range(blocks):
+        s = score(c)
+        scores[256 * c : 256 * c + 256] = s
+        part = jnp.max(s.reshape(32, 8, s.shape[1]), axis=0)
+        m = part if m is None else jnp.maximum(m, part)
+    m = jnp.max(m, axis=0, keepdims=True)
+    for c in range(blocks):
+        shift = m * SCALE - (1.0 if c in bonus else 0.0)
+        block = slice(256 * c, 256 * c + 256)
+        weights[block] = jnp.exp2(scores[block] * SCALE - shift).astype(BF)
+    return jnp.dot(values_t, weights[...], preferred_element_type=F32), m
+
+
+def near_kernel(s_ref, x_ref, gain_ref, w_ref, own_ref, out_ref, normed, keys, scores, weights):
     p = pl.program_id(0)
 
     @pl.when(p == 0)
@@ -130,14 +138,21 @@
     v = jnp.dot(rows, w_ref[1], preferred_element_type=F32).astype(BF).astype(F32)
     partner = s_ref[1] + 1 - 2 * (s_ref[1] % 2)
     k, v = mask_key_value(k, v, partner * ROWS, s_ref[0])
-    keys = jnp.concatenate([own_ref[0], k.astype(BF)], axis=0)
+    keys[:ROWS] = own_ref[0]
+    keys[ROWS:] = k.astype(BF)
     values_t = jnp.concatenate([own_ref[1], v.astype(BF)], axis=0).T
     queries = own_ref[2]
     for a in range(2):
         for c in range(0, ROWS, 256):
             part = queries[c : c + 256]
             part = jnp.where(lanes(part.shape) // WIDE == a, part, jnp.zeros_like(part))
-            numer, m = attend(nt(keys, part), values_t[a * WIDE : (a + 1) * WIDE])
+            slot = (2 * a + c // 256) % 2
+            numer, m = attend(
+                lambda i: nt(keys[256 * i : 256 * i + 256], part),
+                values_t[a * WIDE : (a + 1) * WIDE],
+                scores.at[slot],
+                weights.at[slot],
+            )
             row = lax.broadcasted_iota(jnp.int32, numer.shape, 0)
             out_ref[a, :, c : c + 256] = jnp.where(row == HEAD + 1, m, numer)
 
@@ -155,7 +170,12 @@
                 pl.BlockSpec((3, ROWS, 128), lambda p, s: (0, 0, p + first)),
             ],
             out_specs=pl.BlockSpec((2, WIDE, ROWS), lambda p, s: (p, 0, 0)),
-            scratch_shapes=[pltpu.VMEM((ROWS, WIDTH), BF)],
+            scratch_shapes=[
+                pltpu.VMEM((ROWS, WIDTH), BF),
+                pltpu.VMEM((2 * ROWS, 128), BF),
+                pltpu.VMEM((2, 2 * ROWS, 256), F32),
+                pltpu.VMEM((2, 2 * ROWS, 256), BF),
+            ],
         ),
         out_shape=jax.ShapeDtypeStruct((2 * count, WIDE, ROWS), F32),
         cost_estimate=pl.CostEstimate(
@@ -186,37 +206,42 @@
     return jnp.where(row == HEAD + 2, third, out)
 
 
-def middle_kernel(s_ref, in_ref, out_ref, keys_t, values_t, queries_t):
-    column = s_ref[1] // 8
-    pair = s_ref[1] % 8
+def middle_kernel(s_ref, in_ref, out_ref, keys_t, values_t, queries_t, keys, scores, weights):
+    off4 = s_ref[2 + s_ref[1] % HEADS] % 4
     row = lax.broadcasted_iota(jnp.int32, (WIDE - HEAD, 1024), 0)
-    for a in range(2):
-        base = a * WIDE
+    first = row == 0
+    for g in range(2):
+        base = g * WIDE
         for i in range(8):
             part = slice(i * 128, (i + 1) * 128)
             for j, ref in enumerate((keys_t, values_t, queries_t)):
-                ref[base : base + HEAD, part] = in_ref[i, j, a * HEAD : (a + 1) * HEAD]
-        place = column * 4096 + s_ref[2 + 2 * pair + a] % 4 + 4 * lanes(row.shape)
-        alive = place < s_ref[0]
+                ref[base : base + HEAD, part] = in_ref[8 * g + i, HEAD * (j + 1) : HEAD * (j + 2)]
+        start = (s_ref[1] // HEADS * 2 + g) * 4096 + off4
+        alive = start + 4 * lanes(row.shape) < s_ref[0]
         spare = slice(base + HEAD, base + WIDE)
-        first = row == 0
         keys_t[spare] = jnp.where(first & (~alive), NEGATIVE, 0.0).astype(BF)
         values_t[spare] = jnp.where(first & alive, 1.0, 0.0).astype(BF)
         queries_t[spare] = jnp.where(first, 1.0, 0.0).astype(BF)
-        alive = column * 4096 + s_ref[2 + 2 * pair + a] % 4 + 4 * lanes((HEAD, 1024)) < s_ref[0]
+        alive = start + 4 * lanes((HEAD, 1024)) < s_ref[0]
         values = values_t[base : base + HEAD]
         values_t[base : base + HEAD] = jnp.where(alive, values, jnp.zeros_like(values))
-    keys = keys_t[...].T
+    keys[...] = keys_t[...].T
     for c in range(0, 1024, 256):
         queries = queries_t[:, c : c + 256]
-        head = lax.broadcasted_iota(jnp.int32, queries.shape, 0) // WIDE
-        for a in range(2):
-            part = jnp.where(head == a, queries, jnp.zeros_like(queries))
-            s = jnp.dot(keys, part, preferred_element_type=F32)
-            numer, m = attend(s, values_t[a * WIDE : (a + 1) * WIDE])
+        owner = lax.broadcasted_iota(jnp.int32, queries.shape, 0) // WIDE
+        for g in range(2):
+            part = jnp.where(owner == g, queries, jnp.zeros_like(queries))
+            numer, m = attend(
+                lambda i: jnp.dot(
+                    keys[256 * i : 256 * i + 256], part, preferred_element_type=F32
+                ),
+                values_t[g * WIDE : (g + 1) * WIDE],
+                scores.at[g],
+                weights.at[g],
+            )
             out = packed_result(numer, m).astype(BF)
             for i in range(2):
-                out_ref[c // 128 + i, a * WIDE : (a + 1) * WIDE] = out[:, i * 128 : (i + 1) * 128]
+                out_ref[8 * g + c // 128 + i] = out[:, i * 128 : (i + 1) * 128]
 
 
 def middle(scalars, received):
@@ -225,11 +250,16 @@
         grid_spec=pltpu.PrefetchScalarGridSpec(
             num_scalar_prefetch=1,
             grid=(1,),
-            in_specs=[pl.BlockSpec((8, 3, 96, 128), lambda i, s: (0, 0, 0, 0))],
-            out_specs=pl.BlockSpec((8, 128, 128), lambda i, s: (0, 0, 0)),
-            scratch_shapes=[pltpu.VMEM((128, 1024), BF)] * 3,
-        ),
-        out_shape=jax.ShapeDtypeStruct((8, 128, 128), BF),
+            in_specs=[pl.BlockSpec((16, 192, 128), lambda i, s: (0, 0, 0))],
+            out_specs=pl.BlockSpec((16, WIDE, 128), lambda i, s: (0, 0, 0)),
+            scratch_shapes=[pltpu.VMEM((128, 1024), BF)] * 3
+            + [
+                pltpu.VMEM((1024, 128), BF),
+                pltpu.VMEM((2, 1024, 256), F32),
+                pltpu.VMEM((2, 1024, 256), BF),
+            ],
+        ),
+        out_shape=jax.ShapeDtypeStruct((16, WIDE, 128), BF),
         cost_estimate=pl.CostEstimate(
             flops=10_000_000_000, bytes_accessed=1_000_000, transcendentals=2_100_000
         ),
@@ -237,48 +267,46 @@
     )(scalars, received)
 
 
-def far_kernel(*refs):
-    key_refs = refs[:8]
-    in_ref, out_ref, scores, values_t = refs[8:]
+def far_kernel(own_ref, *refs):
+    key_refs = (own_ref,) + refs[:3]
+    in_ref, mid_ref, out_ref, scores, weights, values_t = refs[3:]
     for c in range(8):
-        values_t[:, 512 * c : 512 * c + 512] = key_refs[c][...].reshape(512, 128).T[WIDE:]
-    packed = in_ref[:, 32:48].reshape(256, 128)
+        block = key_refs[c // 2][16 * (c % 2) : 16 * (c % 2) + 16].reshape(512, 128)
+        values_t[:, 512 * c : 512 * c + 512] = block.T[WIDE:]
+    packed = in_ref[:, 32:48].reshape(256, 128).astype(F32)
     low = lanes(packed.shape) < WIDE
     for half in range(2):
-        queries = packed.astype(F32)
-        if half:
-            queries = pltpu.roll(queries, WIDE, 1)
+        queries = pltpu.roll(packed, WIDE, 1) if half else packed
         queries = jnp.where(low, queries, 0.0).astype(BF)
-        m = jnp.full((1, 256), NEGATIVE, F32)
-        for c in range(8):
-            s = nt(key_refs[c][...].reshape(512, 128), queries)
-            scores[c] = s
-            m = jnp.maximum(m, jnp.max(s, axis=0, keepdims=True))
-        numer = jnp.zeros((WIDE, 256), F32)
-        for c in range(8):
-            shift = m * SCALE - (1.0 if c < 2 else 0.0)
-            p = jnp.exp2(scores[c] * SCALE - shift).astype(BF)
-            numer += jnp.dot(
-                values_t[:, 512 * c : 512 * c + 512], p, preferred_element_type=F32
-            )
+
+        def score(c):
+            block = key_refs[c // 4][8 * (c % 4) : 8 * (c % 4) + 8]
+            return nt(block.reshape(256, 128), queries)
+
+        numer, m = attend(score, values_t[...], scores.at[half], weights.at[half], range(4))
         out = packed_result(numer, m)
         out = jnp.concatenate([out, jnp.zeros_like(out)], axis=0).T
         out_ref[:, 16 * half : 16 * half + 16] = out.astype(BF).reshape(16, 16, 128)
-
-
-def far(keys, received):
+    out_ref[:, 32:] = mid_ref[...]
+
+
+def far(keys, received, mid_result):
     return pl.pallas_call(
         far_kernel,
-        out_shape=jax.ShapeDtypeStruct((16, 32, 128), BF),
-        scratch_shapes=[pltpu.VMEM((8, 512, 256), F32), pltpu.VMEM((WIDE, 4096), BF)],
+        out_shape=jax.ShapeDtypeStruct((16, 96, 128), BF),
+        scratch_shapes=[
+            pltpu.VMEM((2, 4096, 256), F32),
+            pltpu.VMEM((2, 4096, 256), BF),
+            pltpu.VMEM((WIDE, 4096), BF),
+        ],
         cost_estimate=pl.CostEstimate(
             flops=10_000_000_000, bytes_accessed=1_000_000, transcendentals=2_100_000
         ),
         name="far",
-    )(*keys, received)
-
-
-def finish_kernel(s_ref, near0_ref, near1_ref, near2_ref, mid_ref, far_ref, x_ref, gain_ref, w_ref, out_ref, mixed):
+    )(*keys, received, mid_result)
+
+
+def finish_kernel(s_ref, near0_ref, near1_ref, near2_ref, in_ref, x_ref, gain_ref, w_ref, out_ref, mixed):
     lane = lanes((1, ROWS))
     column4 = lanes((128, ROWS)) - 4 * lax.broadcasted_iota(jnp.int32, (128, ROWS), 0)
     column16 = lanes((32, ROWS)) - 16 * lax.broadcasted_iota(jnp.int32, (32, ROWS), 0)
@@ -288,14 +316,13 @@
         off16 = off % 16
         near_ref = (near0_ref, near1_ref, near2_ref)[h // 6]
         mean_n, lse_n = to_lse(near_ref[h % 6], near_ref[h % 6, HEAD + 1 : HEAD + 2])
-        a = h % 2
         spread4 = jnp.where(column4 == off4, 1.0, 0.0).astype(BF)
         mid = jnp.dot(
-            mid_ref[h // 2, a * WIDE : (a + 1) * WIDE], spread4, preferred_element_type=F32
+            in_ref[h, 32:], spread4, preferred_element_type=F32
         )
         spread16 = jnp.where(column16 == off16, 1.0, 0.0).astype(BF)
         distant = lax.dot_general(
-            far_ref[h], spread16, (((0,), (0,)), ((), ())), preferred_element_type=F32
+            in_ref[h, :32], spread16, (((0,), (0,)), ((), ())), preferred_element_type=F32
         )
 
         def lse_of(spread):
@@ -320,7 +347,7 @@
     out_ref[...] = out.astype(BF)
 
 
-def finish(scalars, near_results, mid_result, far_result, rows, gain, w_out):
+def finish(scalars, near_results, dilated, rows, gain, w_out):
     def whole(*shape):
         return pl.BlockSpec(shape, lambda i, s: (0,) * len(shape))
 
@@ -333,8 +360,7 @@
                 whole(6, WIDE, ROWS),
                 whole(6, WIDE, ROWS),
                 whole(4, WIDE, ROWS),
-                whole(8, 128, 128),
-                whole(16, 32, 128),
+                whole(16, 96, 128),
                 whole(ROWS, WIDTH),
                 whole(1, WIDTH),
                 whole(WIDTH, WIDTH),
@@ -344,7 +370,7 @@
         ),
         out_shape=jax.ShapeDtypeStruct((ROWS, WIDTH), BF),
         name="finish",
-    )(scalars, *near_results, mid_result, far_result, rows, gain, w_out)
+    )(scalars, *near_results, dilated, rows, gain, w_out)
 
 
 def exchange(value, axis):
@@ -361,28 +387,20 @@
     wide = jnp.pad(wide, ((0, 0), (0, 0), (0, 0), (0, WIDE - HEAD))).reshape(WIDTH, 3, 1024)
     weights = jnp.stack([wide[:, 1], wide[:, 2], wide[:, 0]])
     gain = norm_gain[None]
-    own, mid_send, far_send = project(scalars, rows, gain, weights)
-    received = exchange(far_send, ("xl", "z"))
+    own, send = project(scalars, rows, gain, weights)
+    received = exchange(send, ("xl", "z"))
     mine = received[:, :32]
-    keys = [mine]
-    for y in range(4):
-        for xh in range(2):
-            if y or xh:
-                moves = [
-                    (2 * i + j, 2 * ((i + y) % 4) + (j ^ xh)) for i in range(4) for j in range(2)
-                ]
-                keys.append(lax.ppermute(mine, ("y", "xh"), moves))
-    mid = exchange(mid_send, "z")
+    other = lax.ppermute(mine, "xh", [(0, 1), (1, 0)])
+    keys = [jnp.concatenate([mine, other])]
+    for y in range(1, 4):
+        keys.append(lax.ppermute(keys[0], "y", [(i, (i + y) % 4) for i in range(4)]))
     near_results = []
     for first, count in ((0, 3), (3, 3), (6, 2)):
         near_results.append(near(scalars, partner, gain, weights, own, first, count))
-    mid_result = middle(scalars, mid)
-    far_result = far(keys, received)
-    mid_result = exchange(mid_result, "z")
-    far_result = exchange(far_result, ("xl", "z"))
-    return finish(
-        scalars, near_results, mid_result, far_result, rows, sub_gain[None], w_out
-    )
+    mid_result = middle(scalars, received)
+    far_result = far(keys, received, mid_result)
+    dilated = exchange(far_result, ("xl", "z"))
+    return finish(scalars, near_results, dilated, rows, sub_gain[None], w_out)
 
 
 def solution(mesh):

time: 186 us -> 156 us (0.84)
  starting transfers between devices: 49.5 us -> 34.8 us
  blocking collectives: 13.1 us -> 0 us
  Pallas kernels: 70.8 us -> 63.3 us
  local copies, waits for them, and re-layouts: 20.5 us -> 26.1 us
    ppermute x1, waiting for transfers between devices: 20.3 us -> 0.01 us  [body(): partner = lax.ppermute(rows, 'z', [(i, i ^ 1) for i in range(8)])]
    all_to_all x4 -> x3, waiting for transfers between devices: 5.27 us -> 23.2 us  [exchange(): return lax.all_to_all(value, axis, split_axis=0, concat_axis=0, tiled=True)]
    all_to_all x1 -> x0, blocking collectives: 13.1 us -> none  [exchange(): return lax.all_to_all(value, axis, split_axis=0, concat_axis=0, tiled=True)]
    ppermute x7 -> x4, starting transfers between devices: 14.2 us -> 6.47 us  [the longest x3 3.38 us: body(): lax.ppermute(keys[0], 'y', [(i, (i + y) % 4) for i in range(4)])]
    all_to_all x4 -> x3, starting transfers between devices: 35 us -> 27.6 us  [exchange(): return lax.all_to_all(value, axis, split_axis=0, concat_axis=0, tiled=True)]
    pallas_call x3, Pallas kernels: 38.9 us -> 32.6 us  [near(): pl.pallas_call(near_kernel, grid_spec=pltpu.PrefetchScalarGridSpec(num_sc...]
    slice x1, local copies, waits for them, and re-layouts: 1.96 us -> 4.58 us  [body(): weights = jnp.stack([wide[:, 1], wide[:, 2], wide[:, 0]])]
    pad x1, local copies, waits for them, and re-layouts: 0.6 us -> 2.74 us  [body(): jnp.pad(wide, ((0, 0), (0, 0), (0, 0), (0, WIDE - HEAD)))]
  transfers between devices with their start and end apart: 12 -> 8, of which waited for: 4 -> 5; matrix products, arithmetic and copies ran while one was open for 9% -> 16% of each run, Pallas kernels for 29% -> 33%
where the time goes in v1:
time: 156 us; the launch traced here: 155 us
  Pallas kernels  63.3 us (41%)
  starting transfers between devices  34.8 us (22%)
  local copies, waits for them, and re-layouts  26.1 us (17%)
  waiting for transfers between devices  25.4 us (16%)
  other arithmetic  4.42 us (3%)
    pallas_call x3, Pallas kernels, near(): pl.pallas_call(near_kernel, grid_spec=pltpu.PrefetchScalarGridSpec(num_sc...  32.6 us
    all_to_all x3, starting transfers between devices, exchange(): return lax.all_to_all(value, axis, split_axis=0, concat_axis=0, tiled=True)  27.6 us
    all_to_all x3, waiting for transfers between devices, exchange(): return lax.all_to_all(value, axis, split_axis=0, concat_axis=0, tiled=True)  23.2 us
    unnamed x26, local copies, waits for them, and re-layouts  14 us
    pallas_call x1, Pallas kernels, project(): pl.pallas_call(project_kernel, grid_spec=pltpu.PrefetchScalarGridSpec(num...  11.3 us
    pallas_call x1, Pallas kernels, middle(): pl.pallas_call(middle_kernel, grid_spec=pltpu.PrefetchScalarGridSpec(num_...  7.02 us
    pallas_call x1, Pallas kernels, far(): pl.pallas_call(far_kernel, out_shape=jax.ShapeDtypeStruct((16, 96, 128),...  6.26 us
    pallas_call x1, Pallas kernels, finish(): pl.pallas_call(finish_kernel, grid_spec=pltpu.PrefetchScalarGridSpec(num_...  6.1 us
  transfers between devices with their start and end apart: 8, of which 5 were waited for; matrix products, arithmetic and copies ran while one was open for 16% of the time, Pallas kernels for 33%

profile of v1, /device:TPU:38, one launch (start us, length us, event | category | flops | bytes accessed | tf_op | source)
XLA Modules:
  0.0 154.7 jit_solution(2767356548422088993)
XLA Ops:
  0.0 2.4 %reshape.12 = bf16[128,4,768]{2,1,0:T(4,128)(2,1)} reshape(bf16[512,768]{1,0:T(8,128)(2,1)} %param.7) | data formatting | bytes 1572864 | tf_op jit(solution)/shard_map/reshape | solution.py:383
  2.4 15.4 %all-to-all-start = ((bf16[128,4,768]{2,1,0:T(4,128)(2,1)}), bf16[128,4,768]{2,1,0:T(4,128)(2,1)}, u32[]{:S(2)}, u32[]{:S(2)}) async-start(bf16[128,4,768]{2,1,0:T(4,128)(2,1)} %reshape.12), calls=%async_computation | async-start | bytes 1572864 | tf_op jit(solution)/shard_map/all_to_all | solution.py:377
  18.4 4.5 %copy.16 = bf16[768,2304]{0,1:T(8,128)(2,1)S(1)} copy(bf16[768,2304]{1,0:T(8,128)(2,1)} %param.11) | data formatting | bytes 7077888 | tf_op args[4]
  22.9 2.7 %pad.4 = bf16[768,3,16,64]{0,3,2,1:T(8,128)(2,1)} pad(bf16[768,3,16,48]{0,3,2,1:T(8,128)(2,1)S(1)} %bitcast.9, bf16[]{:T(256)} %constant.28.clone.1), padding=0_0x0_0x0_0x0_16 | pad | bytes 8257538 | tf_op jit(solution)/shard_map/jit(_pad)/pad | solution.py:387
  25.7 15.0 %all-to-all-done = bf16[128,4,768]{2,1,0:T(4,128)(2,1)} async-done(((bf16[128,4,768]{2,1,0:T(4,128)(2,1)}), bf16[128,4,768]{2,1,0:T(4,128)(2,1)}, u32[]{:S(2)}, u32[]{:S(2)}) %all-to-all-start) | async-done | bytes 786464 | tf_op jit(solution)/shard_map/all_to_all | solution.py:377
  40.7 1.2 copy.15
  41.9 0.0 copy-start
  41.9 0.7 collective-permute-start
  42.6 4.6 %fusion = (bf16[768,1,1024]{0,2,1:T(8,128)(2,1)}, bf16[768,1,1024]{0,2,1:T(8,128)(2,1)}, bf16[768,1,1024]{0,2,1:T(8,128)(2,1)}) fusion(bf16[768,3,1024]{0,2,1:T(8,128)(2,1)} %bitcast.8), kind=kLoop, calls=%fused_computation.3 | loop fusion | bytes 9437184 | tf_op jit(solution)/shard_map/slice | solution.py:388
  47.2 0.0 copy-done
  47.2 1.7 %copy.20 = bf16[768,1,1024]{2,0,1:T(8,128)(2,1)S(1)} copy(bf16[768,1,1024]{0,2,1:T(8,128)(2,1)} %get-tuple-element.9) | data formatting | bytes 3145728
  48.9 2.6 %copy.21 = bf16[768,1,1024]{2,0,1:T(8,128)(2,1)} copy(bf16[768,1,1024]{0,2,1:T(8,128)(2,1)} %get-tuple-element.10) | data formatting | bytes 3145728
  51.5 2.7 %copy.22 = bf16[768,1,1024]{2,0,1:T(8,128)(2,1)} copy(bf16[768,1,1024]{0,2,1:T(8,128)(2,1)} %get-tuple-element.11) | data formatting | bytes 3145728
  54.2 0.0 copy-done.4
  54.2 0.6 broadcast_in_dim.10.gain_ref
  54.8 0.0 copy-done.6
  54.8 0.6 pad_add_fusion.s_ref
  55.4 3.8 %pad_maximum_fusion.w_ref = bf16[3,768,1024]{2,1,0:T(8,128)(2,1)} fusion(bf16[1,768,1024]{2,1,0:T(8,128)(2,1)} %bitcast.15, bf16[1,768,1024]{2,1,0:T(8,128)(2,1)} %bitcast.14, bf16[1,768,1024]{2,1,0:T(8,128)(2,1)S(1)} %bitcast.13), kind=kLoop, calls=%fused_computation | loop fusion | flops 4718592 | bytes 9437184 | tf_op jit(solution)/shard_map/stack | solution.py:388
  59.2 11.3 %project.1 = (bf16[3,512,1024]{2,1,0:T(8,128)(2,1)}, bf16[16,192,128]{2,1,0:T(8,128)(2,1)}) custom-call(s32[18]{0:T(128)} %pad_add_fusion.s_ref, bf16[512,768]{1,0:T(8,128)(2,1)} %bitcast.11, f32[1,768]{1,0:T(1,128)} %broadcast_in_dim.10.gain_ref, bf16[3,768,1024]{2,1,0:T(8,128)(2,1)} %pad_maximum_fusion.w_ref), custom_call_target="tpu_custom_call" | custom-call | tf_op jit(solution)/shard_map/project/pallas_call | solution.py:89
  70.4 5.8 %all-to-all-start.1 = ((bf16[16,192,128]{2,1,0:T(8,128)(2,1)}), bf16[16,192,128]{2,1,0:T(8,128)(2,1)S(1)}, u32[]{:S(2)}, u32[]{:S(2)}) async-start(bf16[16,192,128]{2,1,0:T(8,128)(2,1)} %get-tuple-element.8), calls=%async_computation.1 | async-start | bytes 1572864 | tf_op jit(solution)/shard_map/all_to_all | solution.py:377
  76.2 0.0 copy-done.5
  76.2 0.6 broadcast_in_dim.11.gain_ref
  76.8 0.0 collective-permute-done.x_ref
  76.8 0.9 copy-done.7
  77.7 11.9 %near.4.near1_ref = f32[6,64,512]{2,1,0:T(8,128)} custom-call(s32[18]{0:T(128)} %pad_add_fusion.s_ref, bf16[512,768]{1,0:T(8,128)(2,1)} %copy-done.7, f32[1,768]{1,0:T(1,128)} %broadcast_in_dim.10.gain_ref, bf16[3,768,1024]{2,1,0:T(8,128)(2,1)} %pad_maximum_fusion.w_ref, bf16[3,512,1024]{2,1,0:T(8,128)(2,1)} %get-tuple-element.7.own_ref), custom_call_target="tpu_custom_call" | custom-call | flops 15000000512 | bytes 3000000 | tf_op jit(solution)/shard_map/near/pallas_call | solution.py:161
  89.5 6.1 %all-to-all-done.1.in_ref.refs_3_ = bf16[16,192,128]{2,1,0:T(8,128)(2,1)S(1)} async-done(((bf16[16,192,128]{2,1,0:T(8,128)(2,1)}), bf16[16,192,128]{2,1,0:T(8,128)(2,1)S(1)}, u32[]{:S(2)}, u32[]{:S(2)}) %all-to-all-start.1) | async-done | bytes 786464 | tf_op jit(solution)/shard_map/all_to_all | solution.py:377
  95.7 3.1 %collective-permute-start.1 = (bf16[16,32,128]{2,1,0:T(8,128)(2,1)S(1)}, bf16[16,32,128]{2,1,0:T(8,128)(2,1)S(1)}, u32[]{:S(2)}, u32[]{:S(2)}) collective-permute-start(bf16[16,32,128]{2,1,0:T(8,128)(2,1)S(1)} %slice.19), channel_id=1, source_target_pairs={{0,32},{32,0},{1,33},{33,1},{2,34},{34,2},{3,35},{35,3},{4,36},{36... | collective-permute-start | bytes 393224 | tf_op jit(solution)/shard_map/ppermute | solution.py:393
  98.8 11.8 %near.3.near0_ref = f32[6,64,512]{2,1,0:T(8,128)} custom-call(s32[18]{0:T(128)} %pad_add_fusion.s_ref, bf16[512,768]{1,0:T(8,128)(2,1)} %copy-done.7, f32[1,768]{1,0:T(1,128)} %broadcast_in_dim.10.gain_ref, bf16[3,768,1024]{2,1,0:T(8,128)(2,1)} %pad_maximum_fusion.w_ref, bf16[3,512,1024]{2,1,0:T(8,128)(2,1)} %get-tuple-element.7.own_ref), custom_call_target="tpu_custom_call" | custom-call | flops 15000000512 | bytes 3000000 | tf_op jit(solution)/shard_map/near/pallas_call | solution.py:161
  110.6 0.0 copy-done.2
  110.6 0.0 collective-permute-done.1
  110.6 0.0 copy-start.3
  110.6 0.1 collective-permute-start.2
  110.7 2.1 %collective-permute-start.3 = (bf16[32,32,128]{2,1,0:T(8,128)(2,1)S(1)}, bf16[32,32,128]{2,1,0:T(8,128)(2,1)S(1)}, u32[]{:S(2)}, u32[]{:S(2)}) collective-permute-start(bf16[32,32,128]{2,1,0:T(8,128)(2,1)S(1)} %pad_maximum_fusion.1.own_ref), channel_id=1, source_target_pairs={{0,128},{64,192},{128,0},{192,64},{1,129},{65,193},{129,1},{193,65... | collective-permute-start | bytes 786440 | tf_op jit(solution)/shard_map/ppermute | solution.py:396
  112.8 1.2 collective-permute-start.4
  114.0 7.0 %middle.1.refs_4_ = bf16[16,64,128]{2,1,0:T(8,128)(2,1)} custom-call(s32[18]{0:T(128)} %pad_add_fusion.s_ref, bf16[16,192,128]{2,1,0:T(8,128)(2,1)} %copy-done.2), custom_call_target="tpu_custom_call" | custom-call | flops 10000000000 | bytes 1000000 | tf_op jit(solution)/shard_map/middle/pallas_call | solution.py:248
  121.0 0.0 copy-done.3
  121.0 1.6 %collective-permute-done.2.refs_0_ = bf16[32,32,128]{2,1,0:T(8,128)(2,1)S(1)} collective-permute-done((bf16[32,32,128]{2,1,0:T(8,128)(2,1)S(1)}, bf16[32,32,128]{2,1,0:T(8,128)(2,1)S(1)}, u32[]{:S(2)}, u32[]{:S(2)}) %collective-permute-start.2) | collective-permute-done | bytes 262176 | tf_op jit(solution)/shard_map/ppermute | solution.py:396
  122.6 0.0 collective-permute-done.3.refs_1_
  122.6 0.7 collective-permute-done.4.refs_2_
  123.2 0.0 copy-done.8
  123.3 0.1 copy-done.9
  123.4 0.7 copy-done.10
  124.1 6.3 %far.1 = bf16[16,96,128]{2,1,0:T(8,128)(2,1)} custom-call(bf16[32,32,128]{2,1,0:T(8,128)(2,1)} %copy-done.3, bf16[32,32,128]{2,1,0:T(8,128)(2,1)} %copy-done.8, bf16[32,32,128]{2,1,0:T(8,128)(2,1)} %copy-done.9, bf16[32,32,128]{2,1,0:T(8,128)(2,1)} %copy-done.10, bf16[16,192,128]{2,1,0:T(8,128)(2,1)} %copy-done.2, bf16[16,64,128]{2,1,0:T(8,128)(2,1)} %middle.1.refs_4_), custom_call_target="tpu_custom_call" | custom-call | flops 10000000000 | bytes 1000000 | tf_op jit(solution)/shard_map/far/pallas_call | solution.py:294
  130.4 6.4 %all-to-all-start.2 = ((bf16[16,96,128]{2,1,0:T(8,128)(2,1)}), bf16[16,96,128]{2,1,0:T(8,128)(2,1)S(1)}, u32[]{:S(2)}, u32[]{:S(2)}) async-start(bf16[16,96,128]{2,1,0:T(8,128)(2,1)} %far.1), calls=%async_computation.2 | async-start | bytes 786432 | tf_op jit(solution)/shard_map/all_to_all | solution.py:377
  136.8 9.0 %near.5.near2_ref = f32[4,64,512]{2,1,0:T(8,128)} custom-call(s32[18]{0:T(128)} %pad_add_fusion.s_ref, bf16[512,768]{1,0:T(8,128)(2,1)} %copy-done.7, f32[1,768]{1,0:T(1,128)} %broadcast_in_dim.10.gain_ref, bf16[3,768,1024]{2,1,0:T(8,128)(2,1)} %pad_maximum_fusion.w_ref, bf16[3,512,1024]{2,1,0:T(8,128)(2,1)} %get-tuple-element.7.own_ref), custom_call_target="tpu_custom_call" | custom-call | flops 10000000000 | bytes 2000000 | tf_op jit(solution)/shard_map/near/pallas_call | solution.py:161
  145.8 2.1 %all-to-all-done.2.in_ref = bf16[16,96,128]{2,1,0:T(8,128)(2,1)S(1)} async-done(((bf16[16,96,128]{2,1,0:T(8,128)(2,1)}), bf16[16,96,128]{2,1,0:T(8,128)(2,1)S(1)}, u32[]{:S(2)}, u32[]{:S(2)}) %all-to-all-start.2) | async-done | bytes 393248 | tf_op jit(solution)/shard_map/all_to_all | solution.py:377
  147.9 0.7 copy-done.1
  148.6 6.1 %finish.1 = bf16[512,768]{1,0:T(8,128)(2,1)} custom-call(s32[18]{0:T(128)} %pad_add_fusion.s_ref, f32[6,64,512]{2,1,0:T(8,128)} %near.3.near0_ref, f32[6,64,512]{2,1,0:T(8,128)} %near.4.near1_ref, f32[4,64,512]{2,1,0:T(8,128)} %near.5.near2_ref, bf16[16,96,128]{2,1,0:T(8,128)(2,1)} %copy-done.1, bf16[512,768]{1,0:T(8,128)(2,1)} %bitcast.12, ...), custom_call_target="tpu_custom_call" | custom-call | tf_op jit(solution)/shard_map/finish/pallas_call | solution.py:354
  (11 shorter events, 0.1 us)
Async XLA Ops:
  2.4 38.3 %all-to-all-start = ((bf16[128,4,768]{2,1,0:T(4,128)(2,1)}), bf16[128,4,768]{2,1,0:T(4,128)(2,1)}, u32[]{:S(2)}, u32[]{:S(2)}) async-start(bf16[128,4,768]{2,1,0:T(4,128)(2,1)} %reshape.12), calls=%async_computation | async-start | bytes 1572864 | tf_op jit(solution)/shard_map/all_to_all | solution.py:377
  41.9 5.3 %copy-start = (bf16[4,128,768]{2,1,0:T(8,128)(2,1)}, bf16[4,128,768]{2,1,0:T(8,128)(2,1)S(1)}, u32[]{:S(2)}) copy-start(bf16[4,128,768]{2,1,0:T(8,128)(2,1)S(1)} %copy.15) | copy-start | bytes 2359300
  41.9 34.9 %collective-permute-start = (bf16[512,768]{1,0:T(8,128)(2,1)S(1)}, bf16[512,768]{1,0:T(8,128)(2,1)S(1)}, u32[]{:S(2)}, u32[]{:S(2)}) collective-permute-start(bf16[512,768]{1,0:T(8,128)(2,1)S(1)} %bitcast.10), channel_id=1, source_target_pairs={{0,2},{2,0},{4,6},{6,4},{8,10},{10,8},{12,14},{14,12},{1,3},{3,1},... | collective-permute-start | bytes 2359304 | tf_op jit(solution)/shard_map/ppermute | solution.py:385
  51.5 2.7 %copy-start.4 = (f32[768]{0:T(1024)S(1)}, f32[768]{0:T(1024)}, u32[]{:S(2)}) copy-start(f32[768]{0:T(1024)} %param.10) | copy-start | bytes 9220
  51.5 3.3 %copy-start.6 = (s32[16]{0:T(128)S(1)}, s32[16]{0:T(128)}, u32[]{:S(2)}) copy-start(s32[16]{0:T(128)} %param.9) | copy-start | bytes 196
  70.4 5.8 %copy-start.5 = (f32[768]{0:T(1024)S(1)}, f32[768]{0:T(1024)}, u32[]{:S(2)}) copy-start(f32[768]{0:T(1024)} %param.12) | copy-start | bytes 9220
  70.4 25.2 %all-to-all-start.1 = ((bf16[16,192,128]{2,1,0:T(8,128)(2,1)}), bf16[16,192,128]{2,1,0:T(8,128)(2,1)S(1)}, u32[]{:S(2)}, u32[]{:S(2)}) async-start(bf16[16,192,128]{2,1,0:T(8,128)(2,1)} %get-tuple-element.8), calls=%async_computation.1 | async-start | bytes 1572864 | tf_op jit(solution)/shard_map/all_to_all | solution.py:377
  76.8 0.9 copy-start.7
  95.6 14.9 %copy-start.2 = (bf16[16,192,128]{2,1,0:T(8,128)(2,1)}, bf16[16,192,128]{2,1,0:T(8,128)(2,1)S(1)}, u32[]{:S(2)}) copy-start(bf16[16,192,128]{2,1,0:T(8,128)(2,1)S(1)} %all-to-all-done.1.in_ref.refs_3_) | copy-start | bytes 2359300
  95.7 14.9 %collective-permute-start.1 = (bf16[16,32,128]{2,1,0:T(8,128)(2,1)S(1)}, bf16[16,32,128]{2,1,0:T(8,128)(2,1)S(1)}, u32[]{:S(2)}, u32[]{:S(2)}) collective-permute-start(bf16[16,32,128]{2,1,0:T(8,128)(2,1)S(1)} %slice.19), channel_id=1, source_target_pairs={{0,32},{32,0},{1,33},{33,1},{2,34},{34,2},{3,35},{35,3},{4,36},{36... | collective-permute-start | bytes 393224 | tf_op jit(solution)/shard_map/ppermute | solution.py:393
  110.6 10.4 %copy-start.3 = (bf16[32,32,128]{2,1,0:T(8,128)(2,1)}, bf16[32,32,128]{2,1,0:T(8,128)(2,1)S(1)}, u32[]{:S(2)}) copy-start(bf16[32,32,128]{2,1,0:T(8,128)(2,1)S(1)} %pad_maximum_fusion.1.own_ref) | copy-start | bytes 786436
  110.6 12.0 %collective-permute-start.2 = (bf16[32,32,128]{2,1,0:T(8,128)(2,1)S(1)}, bf16[32,32,128]{2,1,0:T(8,128)(2,1)S(1)}, u32[]{:S(2)}, u32[]{:S(2)}) collective-permute-start(bf16[32,32,128]{2,1,0:T(8,128)(2,1)S(1)} %pad_maximum_fusion.1.own_ref), channel_id=1, source_target_pairs={{0,64},{64,128},{128,192},{192,0},{1,65},{65,129},{129,193},{193,1... | collective-permute-start | bytes 786440 | tf_op jit(solution)/shard_map/ppermute | solution.py:396
  110.7 11.9 %collective-permute-start.3 = (bf16[32,32,128]{2,1,0:T(8,128)(2,1)S(1)}, bf16[32,32,128]{2,1,0:T(8,128)(2,1)S(1)}, u32[]{:S(2)}, u32[]{:S(2)}) collective-permute-start(bf16[32,32,128]{2,1,0:T(8,128)(2,1)S(1)} %pad_maximum_fusion.1.own_ref), channel_id=1, source_target_pairs={{0,128},{64,192},{128,0},{192,64},{1,129},{65,193},{129,1},{193,65... | collective-permute-start | bytes 786440 | tf_op jit(solution)/shard_map/ppermute | solution.py:396
  112.8 10.4 %collective-permute-start.4 = (bf16[32,32,128]{2,1,0:T(8,128)(2,1)S(1)}, bf16[32,32,128]{2,1,0:T(8,128)(2,1)S(1)}, u32[]{:S(2)}, u32[]{:S(2)}) collective-permute-start(bf16[32,32,128]{2,1,0:T(8,128)(2,1)S(1)} %pad_maximum_fusion.1.own_ref), channel_id=1, source_target_pairs={{0,192},{64,0},{128,64},{192,128},{1,193},{65,1},{129,65},{193,129... | collective-permute-start | bytes 786440 | tf_op jit(solution)/shard_map/ppermute | solution.py:396
  122.6 0.7 copy-start.8
  122.6 0.8 copy-start.9
  123.4 0.7 copy-start.10
  130.4 17.5 %all-to-all-start.2 = ((bf16[16,96,128]{2,1,0:T(8,128)(2,1)}), bf16[16,96,128]{2,1,0:T(8,128)(2,1)S(1)}, u32[]{:S(2)}, u32[]{:S(2)}) async-start(bf16[16,96,128]{2,1,0:T(8,128)(2,1)} %far.1), calls=%async_computation.2 | async-start | bytes 786432 | tf_op jit(solution)/shard_map/all_to_all | solution.py:377
  147.9 0.7 copy-start.1

commit v2 on v1

--- a/solution.py
+++ b/solution.py
@@ -44,6 +44,34 @@
     return lax.dot_general(a, b, (((1,), (1,)), ((), ())), preferred_element_type=F32)
 
 
+def widen_kernel(w_ref, out_ref):
+    for j, start in enumerate((WIDTH, 2 * WIDTH, 0)):
+        for p in range(8):
+            first = start + 2 * HEAD * p
+            window = first // 128 * 128
+            row = lax.broadcasted_iota(jnp.int32, (256, 128), 0) + (window - first)
+            lane = lanes((256, 128))
+            column = lane % WIDE + lane // WIDE * HEAD
+            chosen = (row == column) & (lane % WIDE < HEAD)
+            pick = jnp.where(chosen, 1.0, 0.0).astype(BF)
+            wide = min(256, 3 * WIDTH - window)
+            part = jnp.dot(
+                w_ref[:, window : window + wide], pick[:wide], preferred_element_type=F32
+            )
+            out_ref[p, j] = part.astype(BF)
+
+
+def widen(w_qkv):
+    return pl.pallas_call(
+        widen_kernel,
+        out_shape=jax.ShapeDtypeStruct((8, 3, WIDTH, 128), BF),
+        cost_estimate=pl.CostEstimate(
+            flops=10_000_000_000, bytes_accessed=8_000_000, transcendentals=0
+        ),
+        name="widen",
+    )(w_qkv)
+
+
 def project_kernel(s_ref, x_ref, gain_ref, w_ref, own_ref, send_ref, normed, stage):
     p = pl.program_id(0)
 
@@ -52,17 +80,17 @@
         normed[...] = norm_rows(x_ref[...].astype(F32), gain_ref[...]).astype(BF)
 
     rows = normed[...]
-    k = jnp.dot(rows, w_ref[0], preferred_element_type=F32).astype(BF).astype(F32)
-    v = jnp.dot(rows, w_ref[1], preferred_element_type=F32).astype(BF).astype(F32)
-    q = jnp.dot(rows, w_ref[2], preferred_element_type=F32).astype(BF).astype(F32)
+    k = jnp.dot(rows, w_ref[0, 0], preferred_element_type=F32).astype(BF).astype(F32)
+    v = jnp.dot(rows, w_ref[0, 1], preferred_element_type=F32).astype(BF).astype(F32)
+    q = (jnp.dot(rows, w_ref[0, 2], preferred_element_type=F32) * SCALE).astype(BF).astype(F32)
     k, v = mask_key_value(k, v, s_ref[1] * ROWS, s_ref[0])
     q = jnp.where(lanes(q.shape) % WIDE == HEAD, 1.0, q)
     stage[0] = k
     stage[1] = v
     stage[2] = q
-    own_ref[0] = k.astype(BF)
-    own_ref[1] = v.astype(BF)
-    own_ref[2] = q.astype(BF)
+    own_ref[0, 0] = k.astype(BF)
+    own_ref[0, 1] = v.astype(BF)
+    own_ref[0, 2] = q.astype(BF)
     low = lanes((ROWS // 4, 128)) < WIDE
     off = [s_ref[2 + 2 * p + a] for a in range(2)]
     for j in range(3):
@@ -94,16 +122,16 @@
             in_specs=[
                 pl.BlockSpec((ROWS, WIDTH), lambda p, s: (0, 0)),
                 pl.BlockSpec((1, WIDTH), lambda p, s: (0, 0)),
-                pl.BlockSpec((3, WIDTH, 128), lambda p, s: (0, 0, p)),
+                pl.BlockSpec((1, 3, WIDTH, 128), lambda p, s: (p, 0, 0, 0)),
             ],
             out_specs=[
-                pl.BlockSpec((3, ROWS, 128), lambda p, s: (0, 0, p)),
+                pl.BlockSpec((1, 3, ROWS, 128), lambda p, s: (p, 0, 0, 0)),
                 pl.BlockSpec((2, 192, 128), lambda p, s: (p, 0, 0)),
             ],
             scratch_shapes=[pltpu.VMEM((ROWS, WIDTH), BF), pltpu.VMEM((3, ROWS, 128), F32)],
         ),
         out_shape=[
-            jax.ShapeDtypeStruct((3, ROWS, 1024), BF),
+            jax.ShapeDtypeStruct((8, 3, ROWS, 128), BF),
             jax.ShapeDtypeStruct((16, 192, 128), BF),
         ],
         name="project",
@@ -120,9 +148,9 @@
         m = part if m is None else jnp.maximum(m, part)
     m = jnp.max(m, axis=0, keepdims=True)
     for c in range(blocks):
-        shift = m * SCALE - (1.0 if c in bonus else 0.0)
+        shift = m - (1.0 if c in bonus else 0.0)
         block = slice(256 * c, 256 * c + 256)
-        weights[block] = jnp.exp2(scores[block] * SCALE - shift).astype(BF)
+        weights[block] = jnp.exp2(scores[block] - shift).astype(BF)
     return jnp.dot(values_t, weights[...], preferred_element_type=F32), m
 
 
@@ -134,27 +162,24 @@
         normed[...] = norm_rows(x_ref[...].astype(F32), gain_ref[...]).astype(BF)
 
     rows = normed[...]
-    k = jnp.dot(rows, w_ref[0], preferred_element_type=F32).astype(BF).astype(F32)
-    v = jnp.dot(rows, w_ref[1], preferred_element_type=F32).astype(BF).astype(F32)
+    k = jnp.dot(rows, w_ref[0, 0], preferred_element_type=F32).astype(BF).astype(F32)
+    v = jnp.dot(rows, w_ref[0, 1], preferred_element_type=F32).astype(BF).astype(F32)
     partner = s_ref[1] + 1 - 2 * (s_ref[1] % 2)
     k, v = mask_key_value(k, v, partner * ROWS, s_ref[0])
-    keys[:ROWS] = own_ref[0]
+    keys[:ROWS] = own_ref[0, 0]
     keys[ROWS:] = k.astype(BF)
-    values_t = jnp.concatenate([own_ref[1], v.astype(BF)], axis=0).T
-    queries = own_ref[2]
+    values_t = jnp.concatenate([own_ref[0, 1], v.astype(BF)], axis=0).T
+    queries = own_ref[0, 2]
     for a in range(2):
-        for c in range(0, ROWS, 256):
-            part = queries[c : c + 256]
-            part = jnp.where(lanes(part.shape) // WIDE == a, part, jnp.zeros_like(part))
-            slot = (2 * a + c // 256) % 2
-            numer, m = attend(
-                lambda i: nt(keys[256 * i : 256 * i + 256], part),
-                values_t[a * WIDE : (a + 1) * WIDE],
-                scores.at[slot],
-                weights.at[slot],
-            )
-            row = lax.broadcasted_iota(jnp.int32, numer.shape, 0)
-            out_ref[a, :, c : c + 256] = jnp.where(row == HEAD + 1, m, numer)
+        part = jnp.where(lanes(queries.shape) // WIDE == a, queries, jnp.zeros_like(queries))
+        numer, m = attend(
+            lambda i: nt(keys[256 * i : 256 * i + 256], part),
+            values_t[a * WIDE : (a + 1) * WIDE],
+            scores.at[a],
+            weights.at[a],
+        )
+        row = lax.broadcasted_iota(jnp.int32, numer.shape, 0)
+        out_ref[a] = jnp.where(row == HEAD + 1, m, numer)
 
 
 def near(scalars, rows, gain, weights, own, first, count):
@@ -166,15 +191,15 @@
             in_specs=[
                 pl.BlockSpec((ROWS, WIDTH), lambda p, s: (0, 0)),
                 pl.BlockSpec((1, WIDTH), lambda p, s: (0, 0)),
-                pl.BlockSpec((2, WIDTH, 128), lambda p, s: (0, 0, p + first)),
-                pl.BlockSpec((3, ROWS, 128), lambda p, s: (0, 0, p + first)),
+                pl.BlockSpec((1, 2, WIDTH, 128), lambda p, s: (p + first, 0, 0, 0)),
+                pl.BlockSpec((1, 3, ROWS, 128), lambda p, s: (p + first, 0, 0, 0)),
             ],
             out_specs=pl.BlockSpec((2, WIDE, ROWS), lambda p, s: (p, 0, 0)),
             scratch_shapes=[
                 pltpu.VMEM((ROWS, WIDTH), BF),
                 pltpu.VMEM((2 * ROWS, 128), BF),
-                pltpu.VMEM((2, 2 * ROWS, 256), F32),
-                pltpu.VMEM((2, 2 * ROWS, 256), BF),
+                pltpu.VMEM((2, 2 * ROWS, ROWS), F32),
+                pltpu.VMEM((2, 2 * ROWS, ROWS), BF),
             ],
         ),
         out_shape=jax.ShapeDtypeStruct((2 * count, WIDE, ROWS), F32),
@@ -189,7 +214,7 @@
 
 def to_lse(numer, m):
     total = numer[HEAD : HEAD + 1]
-    lse = jnp.where(total > 0.0, m * SCALE + jnp.log2(jnp.maximum(total, 1.0)), NEGATIVE)
+    lse = jnp.where(total > 0.0, m + jnp.log2(jnp.maximum(total, 1.0)), NEGATIVE)
     return numer / jnp.maximum(total, 1.0), lse
 
 
@@ -226,8 +251,8 @@
         values = values_t[base : base + HEAD]
         values_t[base : base + HEAD] = jnp.where(alive, values, jnp.zeros_like(values))
     keys[...] = keys_t[...].T
-    for c in range(0, 1024, 256):
-        queries = queries_t[:, c : c + 256]
+    for c in range(0, 1024, 512):
+        queries = queries_t[:, c : c + 512]
         owner = lax.broadcasted_iota(jnp.int32, queries.shape, 0) // WIDE
         for g in range(2):
             part = jnp.where(owner == g, queries, jnp.zeros_like(queries))
@@ -240,7 +265,7 @@
                 weights.at[g],
             )
             out = packed_result(numer, m).astype(BF)
-            for i in range(2):
+            for i in range(4):
                 out_ref[8 * g + c // 128 + i] = out[:, i * 128 : (i + 1) * 128]
 
 
@@ -255,8 +280,8 @@
             scratch_shapes=[pltpu.VMEM((128, 1024), BF)] * 3
             + [
                 pltpu.VMEM((1024, 128), BF),
-                pltpu.VMEM((2, 1024, 256), F32),
-                pltpu.VMEM((2, 1024, 256), BF),
+                pltpu.VMEM((2, 1024, 512), F32),
+                pltpu.VMEM((2, 1024, 512), BF),
             ],
         ),
         out_shape=jax.ShapeDtypeStruct((16, WIDE, 128), BF),
@@ -274,19 +299,19 @@
         block = key_refs[c // 2][16 * (c % 2) : 16 * (c % 2) + 16].reshape(512, 128)
         values_t[:, 512 * c : 512 * c + 512] = block.T[WIDE:]
     packed = in_ref[:, 32:48].reshape(256, 128).astype(F32)
-    low = lanes(packed.shape) < WIDE
+    queries = jnp.concatenate([packed, pltpu.roll(packed, WIDE, 1)], axis=0)
+    queries = jnp.where(lanes(queries.shape) < WIDE, queries, 0.0).astype(BF)
+
+    def score(c):
+        block = key_refs[c // 4][8 * (c % 4) : 8 * (c % 4) + 8]
+        return nt(block.reshape(256, 128), queries)
+
+    numer, m = attend(score, values_t[...], scores, weights, range(4))
+    out = packed_result(numer, m)
+    out = jnp.concatenate([out, jnp.zeros_like(out)], axis=0).T.astype(BF)
     for half in range(2):
-        queries = pltpu.roll(packed, WIDE, 1) if half else packed
-        queries = jnp.where(low, queries, 0.0).astype(BF)
-
-        def score(c):
-            block = key_refs[c // 4][8 * (c % 4) : 8 * (c % 4) + 8]
-            return nt(block.reshape(256, 128), queries)
-
-        numer, m = attend(score, values_t[...], scores.at[half], weights.at[half], range(4))
-        out = packed_result(numer, m)
-        out = jnp.concatenate([out, jnp.zeros_like(out)], axis=0).T
-        out_ref[:, 16 * half : 16 * half + 16] = out.astype(BF).reshape(16, 16, 128)
+        part = out[256 * half : 256 * half + 256]
+        out_ref[:, 16 * half : 16 * half + 16] = part.reshape(16, 16, 128)
     out_ref[:, 32:] = mid_ref[...]
 
 
@@ -295,8 +320,8 @@
         far_kernel,
         out_shape=jax.ShapeDtypeStruct((16, 96, 128), BF),
         scratch_shapes=[
-            pltpu.VMEM((2, 4096, 256), F32),
-            pltpu.VMEM((2, 4096, 256), BF),
+            pltpu.VMEM((4096, 512), F32),
+            pltpu.VMEM((4096, 512), BF),
             pltpu.VMEM((WIDE, 4096), BF),
         ],
         cost_estimate=pl.CostEstimate(
@@ -314,8 +339,8 @@
         off = s_ref[2 + h]
         off4 = off % 4
         off16 = off % 16
-        near_ref = (near0_ref, near1_ref, near2_ref)[h // 6]
-        mean_n, lse_n = to_lse(near_ref[h % 6], near_ref[h % 6, HEAD + 1 : HEAD + 2])
+        near_ref, i = ((near0_ref, h), (near1_ref, h - 8), (near2_ref, h - 12))[max(h // 4 - 1, 0)]
+        mean_n, lse_n = to_lse(near_ref[i], near_ref[i, HEAD + 1 : HEAD + 2])
         spread4 = jnp.where(column4 == off4, 1.0, 0.0).astype(BF)
         mid = jnp.dot(
             in_ref[h, 32:], spread4, preferred_element_type=F32
@@ -357,8 +382,8 @@
             num_scalar_prefetch=1,
             grid=(1,),
             in_specs=[
-                whole(6, WIDE, ROWS),
-                whole(6, WIDE, ROWS),
+                whole(8, WIDE, ROWS),
+                whole(4, WIDE, ROWS),
                 whole(4, WIDE, ROWS),
                 whole(16, 96, 128),
                 whole(ROWS, WIDTH),
@@ -383,9 +408,7 @@
     arrived = exchange(tile_embed.reshape(128, 4, WIDTH), ("y", "xh", "xl", "z"))
     rows = arrived.transpose(1, 0, 2).reshape(ROWS, WIDTH)
     partner = lax.ppermute(rows, "z", [(i, i ^ 1) for i in range(8)])
-    wide = w_qkv.reshape(WIDTH, 3, HEADS, HEAD)
-    wide = jnp.pad(wide, ((0, 0), (0, 0), (0, 0), (0, WIDE - HEAD))).reshape(WIDTH, 3, 1024)
-    weights = jnp.stack([wide[:, 1], wide[:, 2], wide[:, 0]])
+    weights = widen(w_qkv)
     gain = norm_gain[None]
     own, send = project(scalars, rows, gain, weights)
     received = exchange(send, ("xl", "z"))
@@ -395,7 +418,7 @@
     for y in range(1, 4):
         keys.append(lax.ppermute(keys[0], "y", [(i, (i + y) % 4) for i in range(4)]))
     near_results = []
-    for first, count in ((0, 3), (3, 3), (6, 2)):
+    for first, count in ((0, 4), (4, 2), (6, 2)):
         near_results.append(near(scalars, partner, gain, weights, own, first, count))
     mid_result = middle(scalars, received)
     far_result = far(keys, received, mid_result)

time: 156 us -> 140 us (0.90)
  local copies, waits for them, and re-layouts: 26.1 us -> 7.49 us
  waiting for transfers between devices: 25.4 us -> 30.8 us
  other arithmetic: 4.42 us -> 1.26 us
    unnamed x26 -> x16, local copies, waits for them, and re-layouts: 14 us -> 2.47 us
    pallas_call x0 -> x1, Pallas kernels: none -> 6.71 us  [widen(): pl.pallas_call(widen_kernel, out_shape=jax.ShapeDtypeStruct((8, 3, WIDTH,...]
    all_to_all x3, waiting for transfers between devices: 23.2 us -> 27.8 us  [exchange(): return lax.all_to_all(value, axis, split_axis=0, concat_axis=0, tiled=True)]
    slice x1 -> x0, local copies, waits for them, and re-layouts: 4.58 us -> none  [body(): weights = jnp.stack([wide[:, 1], wide[:, 2], wide[:, 0]])]
    pallas_call x3, Pallas kernels: 32.6 us -> 28.5 us  [near(): pl.pallas_call(near_kernel, grid_spec=pltpu.PrefetchScalarGridSpec(num_sc...]
    another operation x1 -> x0, other arithmetic: 3.8 us -> none  [body(): weights = jnp.stack([wide[:, 1], wide[:, 2], wide[:, 0]])]
    pad x1 -> x0, local copies, waits for them, and re-layouts: 2.74 us -> none  [body(): jnp.pad(wide, ((0, 0), (0, 0), (0, 0), (0, WIDE - HEAD)))]
  transfers between devices with their start and end apart: 8 -> 8, of which waited for: 5 -> 5; matrix products, arithmetic and copies ran while one was open for 16% -> 3% of each run, Pallas kernels for 33% -> 38%
where the time goes in v2:
time: 140 us; the launch traced here: 139 us
  Pallas kernels  64.4 us (46%)
  starting transfers between devices  34.2 us (24%)
  waiting for transfers between devices  30.8 us (22%)
  local copies, waits for them, and re-layouts  7.49 us (5%)
    pallas_call x3, Pallas kernels, near(): pl.pallas_call(near_kernel, grid_spec=pltpu.PrefetchScalarGridSpec(num_sc...  28.5 us
    all_to_all x3, waiting for transfers between devices, exchange(): return lax.all_to_all(value, axis, split_axis=0, concat_axis=0, tiled=True)  27.8 us
    all_to_all x3, starting transfers between devices, exchange(): return lax.all_to_all(value, axis, split_axis=0, concat_axis=0, tiled=True)  27 us
    pallas_call x1, Pallas kernels, project(): pl.pallas_call(project_kernel, grid_spec=pltpu.PrefetchScalarGridSpec(num...  11.2 us
    pallas_call x1, Pallas kernels, widen(): pl.pallas_call(widen_kernel, out_shape=jax.ShapeDtypeStruct((8, 3, WIDTH,...  6.71 us
    pallas_call x1, Pallas kernels, middle(): pl.pallas_call(middle_kernel, grid_spec=pltpu.PrefetchScalarGridSpec(num_...  6.27 us
    pallas_call x1, Pallas kernels, finish(): pl.pallas_call(finish_kernel, grid_spec=pltpu.PrefetchScalarGridSpec(num_...  6.1 us
    pallas_call x1, Pallas kernels, far(): pl.pallas_call(far_kernel, out_shape=jax.ShapeDtypeStruct((16, 96, 128),...  5.6 us
  transfers between devices with their start and end apart: 8, of which 5 were waited for; matrix products, arithmetic and copies ran while one was open for 3% of the time, Pallas kernels for 38%

profile of v2, /device:TPU:38, one launch (start us, length us, event | category | flops | bytes accessed | tf_op | source)
XLA Modules:
  0.0 138.9 jit_solution(2712816541952337970)
XLA Ops:
  0.0 2.4 %reshape.6 = bf16[128,4,768]{2,1,0:T(4,128)(2,1)} reshape(bf16[512,768]{1,0:T(8,128)(2,1)} %param.7) | data formatting | bytes 1572864 | tf_op jit(solution)/shard_map/reshape | solution.py:408
  2.4 15.0 %all-to-all-start = ((bf16[128,4,768]{2,1,0:T(4,128)(2,1)}), bf16[128,4,768]{2,1,0:T(4,128)(2,1)S(1)}, u32[]{:S(2)}, u32[]{:S(2)}) async-start(bf16[128,4,768]{2,1,0:T(4,128)(2,1)} %reshape.6), calls=%async_computation | async-start | bytes 1572864 | tf_op jit(solution)/shard_map/all_to_all | solution.py:402
  18.0 1.3 broadcast_in_dim.10.gain_ref
  19.3 1.3 broadcast_in_dim.11.gain_ref
  20.6 1.2 pad_add_fusion.s_ref
  21.8 18.8 %all-to-all-done = bf16[128,4,768]{2,1,0:T(4,128)(2,1)S(1)} async-done(((bf16[128,4,768]{2,1,0:T(4,128)(2,1)}), bf16[128,4,768]{2,1,0:T(4,128)(2,1)S(1)}, u32[]{:S(2)}, u32[]{:S(2)}) %all-to-all-start) | async-done | bytes 786464 | tf_op jit(solution)/shard_map/all_to_all | solution.py:402
  40.6 0.1 copy.9
  40.6 0.0 copy-start
  40.7 0.7 collective-permute-start
  41.4 6.7 %widen.1.w_ref = bf16[8,3,768,128]{3,2,1,0:T(8,128)(2,1)} custom-call(bf16[768,2304]{1,0:T(8,128)(2,1)} %w_ref.2), custom_call_target="tpu_custom_call" | custom-call | flops 10000000000 | bytes 8000000 | tf_op jit(solution)/shard_map/widen/pallas_call | solution.py:65
  48.1 0.0 copy-done
  48.1 11.2 %project.1 = (bf16[8,3,512,128]{3,2,1,0:T(8,128)(2,1)}, bf16[16,192,128]{2,1,0:T(8,128)(2,1)}) custom-call(s32[18]{0:T(128)} %pad_add_fusion.s_ref, bf16[512,768]{1,0:T(8,128)(2,1)} %bitcast.4, f32[1,768]{1,0:T(1,128)} %broadcast_in_dim.10.gain_ref, bf16[8,3,768,128]{3,2,1,0:T(8,128)(2,1)} %widen.1.w_ref), custom_call_target="tpu_custom_call" | custom-call | tf_op jit(solution)/shard_map/project/pallas_call | solution.py:117
  59.3 5.6 %all-to-all-start.1 = ((bf16[16,192,128]{2,1,0:T(8,128)(2,1)}), bf16[16,192,128]{2,1,0:T(8,128)(2,1)S(1)}, u32[]{:S(2)}, u32[]{:S(2)}) async-start(bf16[16,192,128]{2,1,0:T(8,128)(2,1)} %get-tuple-element.8), calls=%async_computation.1 | async-start | bytes 1572864 | tf_op jit(solution)/shard_map/all_to_all | solution.py:402
  64.9 0.0 collective-permute-done.x_ref
  65.0 0.0 copy-start.4
  65.0 0.9 copy-done.4
  65.8 12.6 %near.3.near0_ref = f32[8,64,512]{2,1,0:T(8,128)} custom-call(s32[18]{0:T(128)} %pad_add_fusion.s_ref, bf16[512,768]{1,0:T(8,128)(2,1)} %copy-done.4, f32[1,768]{1,0:T(1,128)} %broadcast_in_dim.10.gain_ref, bf16[8,3,768,128]{3,2,1,0:T(8,128)(2,1)} %widen.1.w_ref, bf16[8,3,512,128]{3,2,1,0:T(8,128)(2,1)} %get-tuple-element.7.own_ref), custom_call_target="tpu_custom_call" | custom-call | flops 20000000000 | bytes 4000000 | tf_op jit(solution)/shard_map/near/pallas_call | solution.py:186
  78.5 5.9 %all-to-all-done.1.in_ref.refs_3_ = bf16[16,192,128]{2,1,0:T(8,128)(2,1)S(1)} async-done(((bf16[16,192,128]{2,1,0:T(8,128)(2,1)}), bf16[16,192,128]{2,1,0:T(8,128)(2,1)S(1)}, u32[]{:S(2)}, u32[]{:S(2)}) %all-to-all-start.1) | async-done | bytes 786464 | tf_op jit(solution)/shard_map/all_to_all | solution.py:402
  84.4 0.0 copy-start.2
  84.4 3.1 %collective-permute-start.1 = (bf16[16,32,128]{2,1,0:T(8,128)(2,1)S(1)}, bf16[16,32,128]{2,1,0:T(8,128)(2,1)S(1)}, u32[]{:S(2)}, u32[]{:S(2)}) collective-permute-start(bf16[16,32,128]{2,1,0:T(8,128)(2,1)S(1)} %slice.4), channel_id=1, source_target_pairs={{0,32},{32,0},{1,33},{33,1},{2,34},{34,2},{3,35},{35,3},{4,36},{36... | collective-permute-start | bytes 393224 | tf_op jit(solution)/shard_map/ppermute | solution.py:416
  87.5 8.0 %near.5.near2_ref = f32[4,64,512]{2,1,0:T(8,128)} custom-call(s32[18]{0:T(128)} %pad_add_fusion.s_ref, bf16[512,768]{1,0:T(8,128)(2,1)} %copy-done.4, f32[1,768]{1,0:T(1,128)} %broadcast_in_dim.10.gain_ref, bf16[8,3,768,128]{3,2,1,0:T(8,128)(2,1)} %widen.1.w_ref, bf16[8,3,512,128]{3,2,1,0:T(8,128)(2,1)} %get-tuple-element.7.own_ref), custom_call_target="tpu_custom_call" | custom-call | flops 10000000000 | bytes 2000000 | tf_op jit(solution)/shard_map/near/pallas_call | solution.py:186
  95.4 0.0 copy-done.2
  95.4 0.0 collective-permute-done.1
  95.5 0.0 copy-start.3
  95.5 0.1 collective-permute-start.2
  95.6 2.1 %collective-permute-start.3 = (bf16[32,32,128]{2,1,0:T(8,128)(2,1)S(1)}, bf16[32,32,128]{2,1,0:T(8,128)(2,1)S(1)}, u32[]{:S(2)}, u32[]{:S(2)}) collective-permute-start(bf16[32,32,128]{2,1,0:T(8,128)(2,1)S(1)} %pad_maximum_fusion.own_ref), channel_id=1, source_target_pairs={{0,128},{64,192},{128,0},{192,64},{1,129},{65,193},{129,1},{193,65... | collective-permute-start | bytes 786440 | tf_op jit(solution)/shard_map/ppermute | solution.py:419
  97.7 1.2 collective-permute-start.4
  98.9 6.3 %middle.1.refs_4_ = bf16[16,64,128]{2,1,0:T(8,128)(2,1)} custom-call(s32[18]{0:T(128)} %pad_add_fusion.s_ref, bf16[16,192,128]{2,1,0:T(8,128)(2,1)} %copy-done.2), custom_call_target="tpu_custom_call" | custom-call | flops 10000000000 | bytes 1000000 | tf_op jit(solution)/shard_map/middle/pallas_call | solution.py:273
  105.1 0.0 copy-done.3
  105.1 2.3 %collective-permute-done.2.refs_0_ = bf16[32,32,128]{2,1,0:T(8,128)(2,1)S(1)} collective-permute-done((bf16[32,32,128]{2,1,0:T(8,128)(2,1)S(1)}, bf16[32,32,128]{2,1,0:T(8,128)(2,1)S(1)}, u32[]{:S(2)}, u32[]{:S(2)}) %collective-permute-start.2) | collective-permute-done | bytes 262176 | tf_op jit(solution)/shard_map/ppermute | solution.py:419
  107.5 0.0 copy-start.5
  107.5 0.0 collective-permute-done.3.refs_1_
  107.5 0.0 copy-start.6
  107.5 0.7 collective-permute-done.4.refs_2_
  108.1 0.0 copy-done.5
  108.2 0.1 copy-done.6
  108.3 0.0 copy-start.7
  108.3 0.7 copy-done.7
  109.0 5.6 %far.1 = bf16[16,96,128]{2,1,0:T(8,128)(2,1)} custom-call(bf16[32,32,128]{2,1,0:T(8,128)(2,1)} %copy-done.3, bf16[32,32,128]{2,1,0:T(8,128)(2,1)} %copy-done.5, bf16[32,32,128]{2,1,0:T(8,128)(2,1)} %copy-done.6, bf16[32,32,128]{2,1,0:T(8,128)(2,1)} %copy-done.7, bf16[16,192,128]{2,1,0:T(8,128)(2,1)} %copy-done.2, bf16[16,64,128]{2,1,0:T(8,128)(2,1)} %middle.1.refs_4_), custom_call_target="tpu_custom_call" | custom-call | flops 10000000000 | bytes 1000000 | tf_op jit(solution)/shard_map/far/pallas_call | solution.py:319
  114.6 6.4 %all-to-all-start.2 = ((bf16[16,96,128]{2,1,0:T(8,128)(2,1)}), bf16[16,96,128]{2,1,0:T(8,128)(2,1)S(1)}, u32[]{:S(2)}, u32[]{:S(2)}) async-start(bf16[16,96,128]{2,1,0:T(8,128)(2,1)} %far.1), calls=%async_computation.2 | async-start | bytes 786432 | tf_op jit(solution)/shard_map/all_to_all | solution.py:402
  121.0 7.9 %near.4.near1_ref = f32[4,64,512]{2,1,0:T(8,128)} custom-call(s32[18]{0:T(128)} %pad_add_fusion.s_ref, bf16[512,768]{1,0:T(8,128)(2,1)} %copy-done.4, f32[1,768]{1,0:T(1,128)} %broadcast_in_dim.10.gain_ref, bf16[8,3,768,128]{3,2,1,0:T(8,128)(2,1)} %widen.1.w_ref, bf16[8,3,512,128]{3,2,1,0:T(8,128)(2,1)} %get-tuple-element.7.own_ref), custom_call_target="tpu_custom_call" | custom-call | flops 10000000000 | bytes 2000000 | tf_op jit(solution)/shard_map/near/pallas_call | solution.py:186
  128.9 3.1 %all-to-all-done.2.in_ref = bf16[16,96,128]{2,1,0:T(8,128)(2,1)S(1)} async-done(((bf16[16,96,128]{2,1,0:T(8,128)(2,1)}), bf16[16,96,128]{2,1,0:T(8,128)(2,1)S(1)}, u32[]{:S(2)}, u32[]{:S(2)}) %all-to-all-start.2) | async-done | bytes 393248 | tf_op jit(solution)/shard_map/all_to_all | solution.py:402
  132.1 0.0 copy-start.1
  132.1 0.7 copy-done.1
  132.8 6.1 %finish.1 = bf16[512,768]{1,0:T(8,128)(2,1)} custom-call(s32[18]{0:T(128)} %pad_add_fusion.s_ref, f32[8,64,512]{2,1,0:T(8,128)} %near.3.near0_ref, f32[4,64,512]{2,1,0:T(8,128)} %near.4.near1_ref, f32[4,64,512]{2,1,0:T(8,128)} %near.5.near2_ref, bf16[16,96,128]{2,1,0:T(8,128)(2,1)} %copy-done.1, bf16[512,768]{1,0:T(8,128)(2,1)} %bitcast.5, ...), custom_call_target="tpu_custom_call" | custom-call | tf_op jit(solution)/shard_map/finish/pallas_call | solution.py:379
  (2 shorter events, 0.0 us)
Async XLA Ops:
  2.4 38.2 %all-to-all-start = ((bf16[128,4,768]{2,1,0:T(4,128)(2,1)}), bf16[128,4,768]{2,1,0:T(4,128)(2,1)S(1)}, u32[]{:S(2)}, u32[]{:S(2)}) async-start(bf16[128,4,768]{2,1,0:T(4,128)(2,1)} %reshape.6), calls=%async_computation | async-start | bytes 1572864 | tf_op jit(solution)/shard_map/all_to_all | solution.py:402
  40.6 7.5 %copy-start = (bf16[4,128,768]{2,1,0:T(8,128)(2,1)}, bf16[4,128,768]{2,1,0:T(8,128)(2,1)S(1)}, u32[]{:S(2)}) copy-start(bf16[4,128,768]{2,1,0:T(8,128)(2,1)S(1)} %copy.9) | copy-start | bytes 2359300
  40.7 24.3 %collective-permute-start = (bf16[512,768]{1,0:T(8,128)(2,1)S(1)}, bf16[512,768]{1,0:T(8,128)(2,1)S(1)}, u32[]{:S(2)}, u32[]{:S(2)}) collective-permute-start(bf16[512,768]{1,0:T(8,128)(2,1)S(1)} %bitcast.3), channel_id=1, source_target_pairs={{0,2},{2,0},{4,6},{6,4},{8,10},{10,8},{12,14},{14,12},{1,3},{3,1},... | collective-permute-start | bytes 2359304 | tf_op jit(solution)/shard_map/ppermute | solution.py:410
  59.3 25.1 %all-to-all-start.1 = ((bf16[16,192,128]{2,1,0:T(8,128)(2,1)}), bf16[16,192,128]{2,1,0:T(8,128)(2,1)S(1)}, u32[]{:S(2)}, u32[]{:S(2)}) async-start(bf16[16,192,128]{2,1,0:T(8,128)(2,1)} %get-tuple-element.8), calls=%async_computation.1 | async-start | bytes 1572864 | tf_op jit(solution)/shard_map/all_to_all | solution.py:402
  65.0 0.9 copy-start.4
  84.4 11.1 %copy-start.2 = (bf16[16,192,128]{2,1,0:T(8,128)(2,1)}, bf16[16,192,128]{2,1,0:T(8,128)(2,1)S(1)}, u32[]{:S(2)}) copy-start(bf16[16,192,128]{2,1,0:T(8,128)(2,1)S(1)} %all-to-all-done.1.in_ref.refs_3_) | copy-start | bytes 2359300
  84.4 11.0 %collective-permute-start.1 = (bf16[16,32,128]{2,1,0:T(8,128)(2,1)S(1)}, bf16[16,32,128]{2,1,0:T(8,128)(2,1)S(1)}, u32[]{:S(2)}, u32[]{:S(2)}) collective-permute-start(bf16[16,32,128]{2,1,0:T(8,128)(2,1)S(1)} %slice.4), channel_id=1, source_target_pairs={{0,32},{32,0},{1,33},{33,1},{2,34},{34,2},{3,35},{35,3},{4,36},{36... | collective-permute-start | bytes 393224 | tf_op jit(solution)/shard_map/ppermute | solution.py:416
  95.5 9.7 %copy-start.3 = (bf16[32,32,128]{2,1,0:T(8,128)(2,1)}, bf16[32,32,128]{2,1,0:T(8,128)(2,1)S(1)}, u32[]{:S(2)}) copy-start(bf16[32,32,128]{2,1,0:T(8,128)(2,1)S(1)} %pad_maximum_fusion.own_ref) | copy-start | bytes 786436
  95.5 12.0 %collective-permute-start.2 = (bf16[32,32,128]{2,1,0:T(8,128)(2,1)S(1)}, bf16[32,32,128]{2,1,0:T(8,128)(2,1)S(1)}, u32[]{:S(2)}, u32[]{:S(2)}) collective-permute-start(bf16[32,32,128]{2,1,0:T(8,128)(2,1)S(1)} %pad_maximum_fusion.own_ref), channel_id=1, source_target_pairs={{0,64},{64,128},{128,192},{192,0},{1,65},{65,129},{129,193},{193,1... | collective-permute-start | bytes 786440 | tf_op jit(solution)/shard_map/ppermute | solution.py:419
  95.6 11.9 %collective-permute-start.3 = (bf16[32,32,128]{2,1,0:T(8,128)(2,1)S(1)}, bf16[32,32,128]{2,1,0:T(8,128)(2,1)S(1)}, u32[]{:S(2)}, u32[]{:S(2)}) collective-permute-start(bf16[32,32,128]{2,1,0:T(8,128)(2,1)S(1)} %pad_maximum_fusion.own_ref), channel_id=1, source_target_pairs={{0,128},{64,192},{128,0},{192,64},{1,129},{65,193},{129,1},{193,65... | collective-permute-start | bytes 786440 | tf_op jit(solution)/shard_map/ppermute | solution.py:419
  97.7 10.5 %collective-permute-start.4 = (bf16[32,32,128]{2,1,0:T(8,128)(2,1)S(1)}, bf16[32,32,128]{2,1,0:T(8,128)(2,1)S(1)}, u32[]{:S(2)}, u32[]{:S(2)}) collective-permute-start(bf16[32,32,128]{2,1,0:T(8,128)(2,1)S(1)} %pad_maximum_fusion.own_ref), channel_id=1, source_target_pairs={{0,192},{64,0},{128,64},{192,128},{1,193},{65,1},{129,65},{193,129... | collective-permute-start | bytes 786440 | tf_op jit(solution)/shard_map/ppermute | solution.py:419
  107.5 0.7 copy-start.5
  107.5 0.8 copy-start.6
  108.3 0.7 copy-start.7
  114.6 17.5 %all-to-all-start.2 = ((bf16[16,96,128]{2,1,0:T(8,128)(2,1)}), bf16[16,96,128]{2,1,0:T(8,128)(2,1)S(1)}, u32[]{:S(2)}, u32[]{:S(2)}) async-start(bf16[16,96,128]{2,1,0:T(8,128)(2,1)} %far.1), calls=%async_computation.2 | async-start | bytes 786432 | tf_op jit(solution)/shard_map/all_to_all | solution.py:402
  132.1 0.7 copy-start.1

commit v3 on v2

--- a/solution.py
+++ b/solution.py
@@ -80,37 +80,38 @@
         normed[...] = norm_rows(x_ref[...].astype(F32), gain_ref[...]).astype(BF)
 
     rows = normed[...]
-    k = jnp.dot(rows, w_ref[0, 0], preferred_element_type=F32).astype(BF).astype(F32)
-    v = jnp.dot(rows, w_ref[0, 1], preferred_element_type=F32).astype(BF).astype(F32)
-    q = (jnp.dot(rows, w_ref[0, 2], preferred_element_type=F32) * SCALE).astype(BF).astype(F32)
-    k, v = mask_key_value(k, v, s_ref[1] * ROWS, s_ref[0])
-    q = jnp.where(lanes(q.shape) % WIDE == HEAD, 1.0, q)
-    stage[0] = k
-    stage[1] = v
-    stage[2] = q
-    own_ref[0, 0] = k.astype(BF)
-    own_ref[0, 1] = v.astype(BF)
-    own_ref[0, 2] = q.astype(BF)
-    low = lanes((ROWS // 4, 128)) < WIDE
-    off = [s_ref[2 + 2 * p + a] for a in range(2)]
-    for j in range(3):
-        first = stage[j, pl.ds(off[0] % 4, ROWS // 4, stride=4), :]
-        second = stage[j, pl.ds(off[1] % 4, ROWS // 4, stride=4), :]
-        chosen = jnp.where(low, first, second).astype(BF).T
+    for u in range(2):
+        k = jnp.dot(rows, w_ref[u, 0], preferred_element_type=F32).astype(BF).astype(F32)
+        v = jnp.dot(rows, w_ref[u, 1], preferred_element_type=F32).astype(BF).astype(F32)
+        q = jnp.dot(rows, w_ref[u, 2], preferred_element_type=F32).astype(BF).astype(F32)
+        k, v = mask_key_value(k, v, s_ref[1] * ROWS, s_ref[0])
+        q = jnp.where(lanes(q.shape) % WIDE == HEAD, 1.0, q)
+        stage[u, 0] = k
+        stage[u, 1] = v
+        stage[u, 2] = q
+        own_ref[u, 0] = k.astype(BF)
+        own_ref[u, 1] = v.astype(BF)
+        own_ref[u, 2] = q.astype(BF)
+        low = lanes((ROWS // 4, 128)) < WIDE
+        off = [s_ref[2 + 4 * p + 2 * u + a] for a in range(2)]
+        for j in range(3):
+            first = stage[u, j, pl.ds(off[0] % 4, ROWS // 4, stride=4), :]
+            second = stage[u, j, pl.ds(off[1] % 4, ROWS // 4, stride=4), :]
+            chosen = jnp.where(low, first, second).astype(BF).T
+            for a in range(2):
+                send_ref[2 * u + a, HEAD * (j + 1) : HEAD * (j + 2)] = chosen[a * WIDE : a * WIDE + HEAD]
+        low = lanes((ROWS // 16, 128)) < WIDE
         for a in range(2):
-            send_ref[a, HEAD * (j + 1) : HEAD * (j + 2)] = chosen[a * WIDE : a * WIDE + HEAD]
-    low = lanes((ROWS // 16, 128)) < WIDE
-    for a in range(2):
-        k, v, q = [stage[j, pl.ds(off[a] % 16, ROWS // 16, stride=16), :] for j in range(3)]
-        if a == 0:
-            v = pltpu.roll(v, WIDE, 1)
-            q_high = pltpu.roll(q, WIDE, 1)
-        else:
-            k = pltpu.roll(k, WIDE, 1)
-            q_high = q
-            q = pltpu.roll(q, WIDE, 1)
-        send_ref[a, :32] = jnp.where(low, k, v).astype(BF)
-        send_ref[a, 32:48] = jnp.where(low[:16], q[:16], q_high[16:]).astype(BF)
+            k, v, q = [stage[u, j, pl.ds(off[a] % 16, ROWS // 16, stride=16), :] for j in range(3)]
+            if a == 0:
+                v = pltpu.roll(v, WIDE, 1)
+                q_high = pltpu.roll(q, WIDE, 1)
+            else:
+                k = pltpu.roll(k, WIDE, 1)
+                q_high = q
+                q = pltpu.roll(q, WIDE, 1)
+            send_ref[2 * u + a, :32] = jnp.where(low, k, v).astype(BF)
+            send_ref[2 * u + a, 32:48] = jnp.where(low[:16], q[:16], q_high[16:]).astype(BF)
 
 
 def project(scalars, rows, gain, weights):
@@ -118,17 +119,17 @@
         project_kernel,
         grid_spec=pltpu.PrefetchScalarGridSpec(
             num_scalar_prefetch=1,
-            grid=(8,),
+            grid=(4,),
             in_specs=[
                 pl.BlockSpec((ROWS, WIDTH), lambda p, s: (0, 0)),
                 pl.BlockSpec((1, WIDTH), lambda p, s: (0, 0)),
-                pl.BlockSpec((1, 3, WIDTH, 128), lambda p, s: (p, 0, 0, 0)),
+                pl.BlockSpec((2, 3, WIDTH, 128), lambda p, s: (p, 0, 0, 0)),
             ],
             out_specs=[
-                pl.BlockSpec((1, 3, ROWS, 128), lambda p, s: (p, 0, 0, 0)),
-                pl.BlockSpec((2, 192, 128), lambda p, s: (p, 0, 0)),
-            ],
-            scratch_shapes=[pltpu.VMEM((ROWS, WIDTH), BF), pltpu.VMEM((3, ROWS, 128), F32)],
+                pl.BlockSpec((2, 3, ROWS, 128), lambda p, s: (p, 0, 0, 0)),
+                pl.BlockSpec((4, 192, 128), lambda p, s: (p, 0, 0)),
+            ],
+            scratch_shapes=[pltpu.VMEM((ROWS, WIDTH), BF), pltpu.VMEM((2, 3, ROWS, 128), F32)],
         ),
         out_shape=[
             jax.ShapeDtypeStruct((8, 3, ROWS, 128), BF),
@@ -139,19 +140,32 @@
 
 
 def attend(score, values_t, scores, weights, bonus=()):
-    blocks = scores.shape[0] // 256
-    m = None
-    for c in range(blocks):
-        s = score(c)
+    return attend_all([(score, values_t, scores, weights, bonus)])[0]
+
+
+def attend_all(streams):
+    results = []
+    tops = [None] * len(streams)
+
+    def score_block(n, c):
+        score, _, scores, _, _ = streams[n]
+        s = score(c) * SCALE
         scores[256 * c : 256 * c + 256] = s
         part = jnp.max(s.reshape(32, 8, s.shape[1]), axis=0)
-        m = part if m is None else jnp.maximum(m, part)
-    m = jnp.max(m, axis=0, keepdims=True)
-    for c in range(blocks):
-        shift = m - (1.0 if c in bonus else 0.0)
-        block = slice(256 * c, 256 * c + 256)
-        weights[block] = jnp.exp2(scores[block] - shift).astype(BF)
-    return jnp.dot(values_t, weights[...], preferred_element_type=F32), m
+        tops[n] = part if tops[n] is None else jnp.maximum(tops[n], part)
+
+    for c in range(streams[0][2].shape[0] // 256):
+        score_block(0, c)
+    for n, (_, values_t, scores, weights, bonus) in enumerate(streams):
+        m = jnp.max(tops[n], axis=0, keepdims=True)
+        for c in range(scores.shape[0] // 256):
+            if n + 1 < len(streams):
+                score_block(n + 1, c)
+            shift = m - (1.0 if c in bonus else 0.0)
+            block = slice(256 * c, 256 * c + 256)
+            weights[block] = jnp.exp2(scores[block] - shift).astype(BF)
+        results.append((jnp.dot(values_t, weights[...], preferred_element_type=F32), m))
+    return results
 
 
 def near_kernel(s_ref, x_ref, gain_ref, w_ref, own_ref, out_ref, normed, keys, scores, weights):
@@ -170,14 +184,19 @@
     keys[ROWS:] = k.astype(BF)
     values_t = jnp.concatenate([own_ref[0, 1], v.astype(BF)], axis=0).T
     queries = own_ref[0, 2]
+    streams = []
     for a in range(2):
         part = jnp.where(lanes(queries.shape) // WIDE == a, queries, jnp.zeros_like(queries))
-        numer, m = attend(
-            lambda i: nt(keys[256 * i : 256 * i + 256], part),
-            values_t[a * WIDE : (a + 1) * WIDE],
-            scores.at[a],
-            weights.at[a],
+        streams.append(
+            (
+                lambda i, part=part: nt(keys[256 * i : 256 * i + 256], part),
+                values_t[a * WIDE : (a + 1) * WIDE],
+                scores.at[a],
+                weights.at[a],
+                (),
+            )
         )
+    for a, (numer, m) in enumerate(attend_all(streams)):
         row = lax.broadcasted_iota(jnp.int32, numer.shape, 0)
         out_ref[a] = jnp.where(row == HEAD + 1, m, numer)
 
@@ -308,17 +327,15 @@
 
     numer, m = attend(score, values_t[...], scores, weights, range(4))
     out = packed_result(numer, m)
-    out = jnp.concatenate([out, jnp.zeros_like(out)], axis=0).T.astype(BF)
-    for half in range(2):
-        part = out[256 * half : 256 * half + 256]
-        out_ref[:, 16 * half : 16 * half + 16] = part.reshape(16, 16, 128)
-    out_ref[:, 32:] = mid_ref[...]
+    out = jnp.concatenate([out[:, :256], out[:, 256:]], axis=0).T.astype(BF)
+    out_ref[:, :16] = out.reshape(16, 16, 128)
+    out_ref[:, 16:] = mid_ref[:, :56]
 
 
 def far(keys, received, mid_result):
     return pl.pallas_call(
         far_kernel,
-        out_shape=jax.ShapeDtypeStruct((16, 96, 128), BF),
+        out_shape=jax.ShapeDtypeStruct((16, 72, 128), BF),
         scratch_shapes=[
             pltpu.VMEM((4096, 512), F32),
             pltpu.VMEM((4096, 512), BF),
@@ -334,21 +351,23 @@
 def finish_kernel(s_ref, near0_ref, near1_ref, near2_ref, in_ref, x_ref, gain_ref, w_ref, out_ref, mixed):
     lane = lanes((1, ROWS))
     column4 = lanes((128, ROWS)) - 4 * lax.broadcasted_iota(jnp.int32, (128, ROWS), 0)
-    column16 = lanes((32, ROWS)) - 16 * lax.broadcasted_iota(jnp.int32, (32, ROWS), 0)
+    column16 = lanes((16, 256)) - 16 * lax.broadcasted_iota(jnp.int32, (16, 256), 0)
     for h in range(HEADS):
         off = s_ref[2 + h]
         off4 = off % 4
         off16 = off % 16
-        near_ref, i = ((near0_ref, h), (near1_ref, h - 8), (near2_ref, h - 12))[max(h // 4 - 1, 0)]
+        near_ref = near0_ref if h < 10 else near1_ref if h < 14 else near2_ref
+        i = h if h < 10 else h - 10 if h < 14 else h - 14
         mean_n, lse_n = to_lse(near_ref[i], near_ref[i, HEAD + 1 : HEAD + 2])
         spread4 = jnp.where(column4 == off4, 1.0, 0.0).astype(BF)
         mid = jnp.dot(
-            in_ref[h, 32:], spread4, preferred_element_type=F32
+            in_ref[h, 16:], spread4, preferred_element_type=F32
         )
         spread16 = jnp.where(column16 == off16, 1.0, 0.0).astype(BF)
         distant = lax.dot_general(
-            in_ref[h, :32], spread16, (((0,), (0,)), ((), ())), preferred_element_type=F32
+            in_ref[h, :16], spread16, (((0,), (0,)), ((), ())), preferred_element_type=F32
         )
+        distant = jnp.concatenate([distant[:WIDE], distant[WIDE:]], axis=1)
 
         def lse_of(spread):
             lse = spread[HEAD : HEAD + 1] + spread[HEAD + 1 : HEAD + 2]
@@ -382,10 +401,10 @@
             num_scalar_prefetch=1,
             grid=(1,),
             in_specs=[
-                whole(8, WIDE, ROWS),
+                whole(10, WIDE, ROWS),
                 whole(4, WIDE, ROWS),
-                whole(4, WIDE, ROWS),
-                whole(16, 96, 128),
+                whole(2, WIDE, ROWS),
+                whole(16, 72, 128),
                 whole(ROWS, WIDTH),
                 whole(1, WIDTH),
                 whole(WIDTH, WIDTH),
@@ -405,11 +424,11 @@
 def body(tile_embed, valid_tiles, offsets, norm_gain, w_qkv, sub_gain, w_out):
     position = lax.axis_index(("y", "xh", "xl", "z"))
     scalars = jnp.concatenate([valid_tiles, position.astype(jnp.int32)[None], offsets])
+    gain, last_gain = norm_gain[None], sub_gain[None]
     arrived = exchange(tile_embed.reshape(128, 4, WIDTH), ("y", "xh", "xl", "z"))
     rows = arrived.transpose(1, 0, 2).reshape(ROWS, WIDTH)
     partner = lax.ppermute(rows, "z", [(i, i ^ 1) for i in range(8)])
     weights = widen(w_qkv)
-    gain = norm_gain[None]
     own, send = project(scalars, rows, gain, weights)
     received = exchange(send, ("xl", "z"))
     mine = received[:, :32]
@@ -418,12 +437,12 @@
     for y in range(1, 4):
         keys.append(lax.ppermute(keys[0], "y", [(i, (i + y) % 4) for i in range(4)]))
     near_results = []
-    for first, count in ((0, 4), (4, 2), (6, 2)):
+    for first, count in ((0, 5), (5, 2), (7, 1)):
         near_results.append(near(scalars, partner, gain, weights, own, first, count))
     mid_result = middle(scalars, received)
     far_result = far(keys, received, mid_result)
     dilated = exchange(far_result, ("xl", "z"))
-    return finish(scalars, near_results, dilated, rows, sub_gain[None], w_out)
+    return finish(scalars, near_results, dilated, rows, last_gain, w_out)
 
 
 def solution(mesh):

time: 140 us -> 155 us (1.11)
  waiting for transfers between devices: 30.8 us -> 48.4 us
  Pallas kernels: 64.4 us -> 60 us
  starting transfers between devices: 34.2 us -> 36.7 us
    ppermute x1, waiting for transfers between devices: 0.01 us -> 10.4 us  [body(): partner = lax.ppermute(rows, 'z', [(i, i ^ 1) for i in range(8)])]
    all_to_all x3, waiting for transfers between devices: 27.8 us -> 33.5 us  [exchange(): return lax.all_to_all(value, axis, split_axis=0, concat_axis=0, tiled=True)]
    pallas_call x3, Pallas kernels: 28.5 us -> 25.3 us  [near(): pl.pallas_call(near_kernel, grid_spec=pltpu.PrefetchScalarGridSpec(num_sc...]
    all_to_all x3, starting transfers between devices: 27 us -> 29.2 us  [exchange(): return lax.all_to_all(value, axis, split_axis=0, concat_axis=0, tiled=True)]
  transfers between devices with their start and end apart: 8 -> 8, of which waited for: 5 -> 5; matrix products, arithmetic and copies ran while one was open for 3% -> 1% of each run, Pallas kernels for 38% -> 25%
where the time goes in v3:
time: 155 us; the launch traced here: 153 us
  Pallas kernels  60 us (39%)
  waiting for transfers between devices  48.4 us (31%)
  starting transfers between devices  36.7 us (24%)
  local copies, waits for them, and re-layouts  7.05 us (5%)
    all_to_all x3, waiting for transfers between devices, exchange(): return lax.all_to_all(value, axis, split_axis=0, concat_axis=0, tiled=True)  33.5 us
    all_to_all x3, starting transfers between devices, exchange(): return lax.all_to_all(value, axis, split_axis=0, concat_axis=0, tiled=True)  29.2 us
    pallas_call x3, Pallas kernels, near(): pl.pallas_call(near_kernel, grid_spec=pltpu.PrefetchScalarGridSpec(num_sc...  25.3 us
    ppermute x1, waiting for transfers between devices, body(): partner = lax.ppermute(rows, 'z', [(i, i ^ 1) for i in range(8)])  10.4 us
    pallas_call x1, Pallas kernels, project(): pl.pallas_call(project_kernel, grid_spec=pltpu.PrefetchScalarGridSpec(num...  10.3 us
    pallas_call x1, Pallas kernels, widen(): pl.pallas_call(widen_kernel, out_shape=jax.ShapeDtypeStruct((8, 3, WIDTH,...  6.73 us
    pallas_call x1, Pallas kernels, middle(): pl.pallas_call(middle_kernel, grid_spec=pltpu.PrefetchScalarGridSpec(num_...  6.12 us
    pallas_call x1, Pallas kernels, finish(): pl.pallas_call(finish_kernel, grid_spec=pltpu.PrefetchScalarGridSpec(num_...  6.04 us
  transfers between devices with their start and end apart: 8, of which 5 were waited for; matrix products, arithmetic and copies ran while one was open for 1% of the time, Pallas kernels for 25%

profile of v3, /device:TPU:38, one launch (start us, length us, event | category | flops | bytes accessed | tf_op | source)
XLA Modules:
  0.0 153.5 jit_solution(6680562240275051102)
XLA Ops:
  0.0 0.0 copy-start.4
  0.0 0.0 copy-start.6
  0.0 2.4 %reshape.6 = bf16[128,4,768]{2,1,0:T(4,128)(2,1)} reshape(bf16[512,768]{1,0:T(8,128)(2,1)} %param.7) | data formatting | bytes 1572864 | tf_op jit(solution)/shard_map/reshape | solution.py:428
  2.4 15.0 %all-to-all-start = ((bf16[128,4,768]{2,1,0:T(4,128)(2,1)}), bf16[128,4,768]{2,1,0:T(4,128)(2,1)S(1)}, u32[]{:S(2)}, u32[]{:S(2)}) async-start(bf16[128,4,768]{2,1,0:T(4,128)(2,1)} %reshape.6), calls=%async_computation | async-start | bytes 1572864 | tf_op jit(solution)/shard_map/all_to_all | solution.py:421
  18.0 0.0 copy-done.4
  18.0 0.6 broadcast_in_dim.10.gain_ref
  18.6 0.0 copy-done.6
  18.6 0.6 pad_add_fusion.s_ref
  19.2 6.7 %widen.1.w_ref = bf16[8,3,768,128]{3,2,1,0:T(8,128)(2,1)} custom-call(bf16[768,2304]{1,0:T(8,128)(2,1)} %w_ref.2), custom_call_target="tpu_custom_call" | custom-call | flops 10000000000 | bytes 8000000 | tf_op jit(solution)/shard_map/widen/pallas_call | solution.py:65
  25.9 14.7 %all-to-all-done = bf16[128,4,768]{2,1,0:T(4,128)(2,1)S(1)} async-done(((bf16[128,4,768]{2,1,0:T(4,128)(2,1)}), bf16[128,4,768]{2,1,0:T(4,128)(2,1)S(1)}, u32[]{:S(2)}, u32[]{:S(2)}) %all-to-all-start) | async-done | bytes 786464 | tf_op jit(solution)/shard_map/all_to_all | solution.py:421
  40.6 1.0 copy.9
  41.5 0.0 copy-start
  41.6 0.0 copy-start.5
  41.6 10.3 %project.1 = (bf16[8,3,512,128]{3,2,1,0:T(8,128)(2,1)}, bf16[16,192,128]{2,1,0:T(8,128)(2,1)}) custom-call(s32[18]{0:T(128)} %pad_add_fusion.s_ref, bf16[512,768]{1,0:T(8,128)(2,1)} %bitcast.3, f32[1,768]{1,0:T(1,128)} %broadcast_in_dim.10.gain_ref, bf16[8,3,768,128]{3,2,1,0:T(8,128)(2,1)} %widen.1.w_ref), custom_call_target="tpu_custom_call" | custom-call | tf_op jit(solution)/shard_map/project/pallas_call | solution.py:118
  51.9 4.9 %all-to-all-start.1 = ((bf16[16,192,128]{2,1,0:T(8,128)(2,1)}), bf16[16,192,128]{2,1,0:T(8,128)(2,1)S(1)}, u32[]{:S(2)}, u32[]{:S(2)}) async-start(bf16[16,192,128]{2,1,0:T(8,128)(2,1)} %get-tuple-element.8), calls=%async_computation.1 | async-start | bytes 1572864 | tf_op jit(solution)/shard_map/all_to_all | solution.py:421
  56.8 0.0 copy-done
  56.8 0.7 collective-permute-start
  57.4 0.0 copy-done.5
  57.4 0.6 broadcast_in_dim.11.gain_ref
  58.0 18.8 %all-to-all-done.1.in_ref.refs_3_ = bf16[16,192,128]{2,1,0:T(8,128)(2,1)S(1)} async-done(((bf16[16,192,128]{2,1,0:T(8,128)(2,1)}), bf16[16,192,128]{2,1,0:T(8,128)(2,1)S(1)}, u32[]{:S(2)}, u32[]{:S(2)}) %all-to-all-start.1) | async-done | bytes 786464 | tf_op jit(solution)/shard_map/all_to_all | solution.py:421
  76.8 0.0 copy-start.2
  76.9 3.6 %collective-permute-start.1 = (bf16[16,32,128]{2,1,0:T(8,128)(2,1)S(1)}, bf16[16,32,128]{2,1,0:T(8,128)(2,1)S(1)}, u32[]{:S(2)}, u32[]{:S(2)}) collective-permute-start(bf16[16,32,128]{2,1,0:T(8,128)(2,1)S(1)} %slice.4), channel_id=1, source_target_pairs={{0,32},{32,0},{1,33},{33,1},{2,34},{34,2},{3,35},{35,3},{4,36},{36... | collective-permute-start | bytes 393224 | tf_op jit(solution)/shard_map/ppermute | solution.py:435
  80.4 10.4 %collective-permute-done.x_ref = bf16[512,768]{1,0:T(8,128)(2,1)S(1)} collective-permute-done((bf16[512,768]{1,0:T(8,128)(2,1)S(1)}, bf16[512,768]{1,0:T(8,128)(2,1)S(1)}, u32[]{:S(2)}, u32[]{:S(2)}) %collective-permute-start) | collective-permute-done | bytes 786464 | tf_op jit(solution)/shard_map/ppermute | solution.py:430
  90.9 0.0 copy-start.7
  90.9 0.9 copy-done.7
  91.8 13.1 %near.3.near0_ref = f32[10,64,512]{2,1,0:T(8,128)} custom-call(s32[18]{0:T(128)} %pad_add_fusion.s_ref, bf16[512,768]{1,0:T(8,128)(2,1)} %copy-done.7, f32[1,768]{1,0:T(1,128)} %broadcast_in_dim.10.gain_ref, bf16[8,3,768,128]{3,2,1,0:T(8,128)(2,1)} %widen.1.w_ref, bf16[8,3,512,128]{3,2,1,0:T(8,128)(2,1)} %get-tuple-element.7.own_ref), custom_call_target="tpu_custom_call" | custom-call | flops 24999999488 | bytes 5000000 | tf_op jit(solution)/shard_map/near/pallas_call | solution.py:205
  104.9 0.0 copy-done.2
  104.9 0.0 collective-permute-done.1
  104.9 0.0 copy-start.3
  104.9 0.5 collective-permute-start.2
  105.4 1.7 %collective-permute-start.3 = (bf16[32,32,128]{2,1,0:T(8,128)(2,1)S(1)}, bf16[32,32,128]{2,1,0:T(8,128)(2,1)S(1)}, u32[]{:S(2)}, u32[]{:S(2)}) collective-permute-start(bf16[32,32,128]{2,1,0:T(8,128)(2,1)S(1)} %pad_maximum_fusion.own_ref), channel_id=1, source_target_pairs={{0,128},{64,192},{128,0},{192,64},{1,129},{65,193},{129,1},{193,65... | collective-permute-start | bytes 786440 | tf_op jit(solution)/shard_map/ppermute | solution.py:438
  107.1 1.2 collective-permute-start.4
  108.3 6.1 %middle.1.refs_4_ = bf16[16,64,128]{2,1,0:T(8,128)(2,1)} custom-call(s32[18]{0:T(128)} %pad_add_fusion.s_ref, bf16[16,192,128]{2,1,0:T(8,128)(2,1)} %copy-done.2), custom_call_target="tpu_custom_call" | custom-call | flops 10000000000 | bytes 1000000 | tf_op jit(solution)/shard_map/middle/pallas_call | solution.py:292
  114.4 0.0 copy-done.3
  114.4 3.8 %collective-permute-done.2.refs_0_ = bf16[32,32,128]{2,1,0:T(8,128)(2,1)S(1)} collective-permute-done((bf16[32,32,128]{2,1,0:T(8,128)(2,1)S(1)}, bf16[32,32,128]{2,1,0:T(8,128)(2,1)S(1)}, u32[]{:S(2)}, u32[]{:S(2)}) %collective-permute-start.2) | collective-permute-done | bytes 262176 | tf_op jit(solution)/shard_map/ppermute | solution.py:438
  118.2 0.0 copy-start.8
  118.2 0.0 collective-permute-done.3.refs_1_
  118.2 0.6 collective-permute-done.4.refs_2_
  118.8 0.1 copy-done.8
  118.9 0.1 copy-done.9
  119.0 0.7 copy-done.10
  119.7 5.5 %far.1 = bf16[16,72,128]{2,1,0:T(8,128)(2,1)} custom-call(bf16[32,32,128]{2,1,0:T(8,128)(2,1)} %copy-done.3, bf16[32,32,128]{2,1,0:T(8,128)(2,1)} %copy-done.8, bf16[32,32,128]{2,1,0:T(8,128)(2,1)} %copy-done.9, bf16[32,32,128]{2,1,0:T(8,128)(2,1)} %copy-done.10, bf16[16,192,128]{2,1,0:T(8,128)(2,1)} %copy-done.2, bf16[16,64,128]{2,1,0:T(8,128)(2,1)} %middle.1.refs_4_), custom_call_target="tpu_custom_call" | custom-call | flops 10000000000 | bytes 1000000 | tf_op jit(solution)/shard_map/far/pallas_call | solution.py:336
  125.2 9.3 %all-to-all-start.2 = ((bf16[16,72,128]{2,1,0:T(8,128)(2,1)}), bf16[16,72,128]{2,1,0:T(8,128)(2,1)S(1)}, u32[]{:S(2)}, u32[]{:S(2)}) async-start(bf16[16,72,128]{2,1,0:T(8,128)(2,1)} %far.1), calls=%async_computation.2 | async-start | bytes 589824 | tf_op jit(solution)/shard_map/all_to_all | solution.py:421
  134.5 7.2 %near.4.near1_ref = f32[4,64,512]{2,1,0:T(8,128)} custom-call(s32[18]{0:T(128)} %pad_add_fusion.s_ref, bf16[512,768]{1,0:T(8,128)(2,1)} %copy-done.7, f32[1,768]{1,0:T(1,128)} %broadcast_in_dim.10.gain_ref, bf16[8,3,768,128]{3,2,1,0:T(8,128)(2,1)} %widen.1.w_ref, bf16[8,3,512,128]{3,2,1,0:T(8,128)(2,1)} %get-tuple-element.7.own_ref), custom_call_target="tpu_custom_call" | custom-call | flops 10000000000 | bytes 2000000 | tf_op jit(solution)/shard_map/near/pallas_call | solution.py:205
  141.7 5.0 %near.5.near2_ref = f32[2,64,512]{2,1,0:T(8,128)} custom-call(s32[18]{0:T(128)} %pad_add_fusion.s_ref, bf16[512,768]{1,0:T(8,128)(2,1)} %copy-done.7, f32[1,768]{1,0:T(1,128)} %broadcast_in_dim.10.gain_ref, bf16[8,3,768,128]{3,2,1,0:T(8,128)(2,1)} %widen.1.w_ref, bf16[8,3,512,128]{3,2,1,0:T(8,128)(2,1)} %get-tuple-element.7.own_ref), custom_call_target="tpu_custom_call" | custom-call | flops 5000000000 | bytes 1000000 | tf_op jit(solution)/shard_map/near/pallas_call | solution.py:205
  146.7 0.0 all-to-all-done.2.in_ref
  146.7 0.7 copy-done.1
  147.4 6.0 %finish.1 = bf16[512,768]{1,0:T(8,128)(2,1)} custom-call(s32[18]{0:T(128)} %pad_add_fusion.s_ref, f32[10,64,512]{2,1,0:T(8,128)} %near.3.near0_ref, f32[4,64,512]{2,1,0:T(8,128)} %near.4.near1_ref, f32[2,64,512]{2,1,0:T(8,128)} %near.5.near2_ref, bf16[16,72,128]{2,1,0:T(8,128)(2,1)} %copy-done.1, bf16[512,768]{1,0:T(8,128)(2,1)} %bitcast.4, ...), custom_call_target="tpu_custom_call" | custom-call | tf_op jit(solution)/shard_map/finish/pallas_call | solution.py:398
  (5 shorter events, 0.0 us)
Async XLA Ops:
  0.0 18.0 %copy-start.4 = (f32[768]{0:T(1024)S(1)}, f32[768]{0:T(1024)}, u32[]{:S(2)}) copy-start(f32[768]{0:T(1024)} %param.10) | copy-start | bytes 9220
  0.0 18.6 %copy-start.6 = (s32[16]{0:T(128)S(1)}, s32[16]{0:T(128)}, u32[]{:S(2)}) copy-start(s32[16]{0:T(128)} %param.9) | copy-start | bytes 196
  2.4 38.2 %all-to-all-start = ((bf16[128,4,768]{2,1,0:T(4,128)(2,1)}), bf16[128,4,768]{2,1,0:T(4,128)(2,1)S(1)}, u32[]{:S(2)}, u32[]{:S(2)}) async-start(bf16[128,4,768]{2,1,0:T(4,128)(2,1)} %reshape.6), calls=%async_computation | async-start | bytes 1572864 | tf_op jit(solution)/shard_map/all_to_all | solution.py:421
  41.5 15.2 %copy-start = (bf16[4,128,768]{2,1,0:T(8,128)(2,1)S(1)}, bf16[4,128,768]{2,1,0:T(8,128)(2,1)}, u32[]{:S(2)}) copy-start(bf16[4,128,768]{2,1,0:T(8,128)(2,1)} %copy.9) | copy-start | bytes 2359300
  41.6 15.9 %copy-start.5 = (f32[768]{0:T(1024)S(1)}, f32[768]{0:T(1024)}, u32[]{:S(2)}) copy-start(f32[768]{0:T(1024)} %param.12) | copy-start | bytes 9220
  51.9 24.9 %all-to-all-start.1 = ((bf16[16,192,128]{2,1,0:T(8,128)(2,1)}), bf16[16,192,128]{2,1,0:T(8,128)(2,1)S(1)}, u32[]{:S(2)}, u32[]{:S(2)}) async-start(bf16[16,192,128]{2,1,0:T(8,128)(2,1)} %get-tuple-element.8), calls=%async_computation.1 | async-start | bytes 1572864 | tf_op jit(solution)/shard_map/all_to_all | solution.py:421
  56.8 34.1 %collective-permute-start = (bf16[512,768]{1,0:T(8,128)(2,1)S(1)}, bf16[512,768]{1,0:T(8,128)(2,1)S(1)}, u32[]{:S(2)}, u32[]{:S(2)}) collective-permute-start(bf16[512,768]{1,0:T(8,128)(2,1)S(1)} %bitcast.5), channel_id=1, source_target_pairs={{0,2},{2,0},{4,6},{6,4},{8,10},{10,8},{12,14},{14,12},{1,3},{3,1},... | collective-permute-start | bytes 2359304 | tf_op jit(solution)/shard_map/ppermute | solution.py:430
  76.8 28.0 %copy-start.2 = (bf16[16,192,128]{2,1,0:T(8,128)(2,1)}, bf16[16,192,128]{2,1,0:T(8,128)(2,1)S(1)}, u32[]{:S(2)}) copy-start(bf16[16,192,128]{2,1,0:T(8,128)(2,1)S(1)} %all-to-all-done.1.in_ref.refs_3_) | copy-start | bytes 2359300
  76.9 28.0 %collective-permute-start.1 = (bf16[16,32,128]{2,1,0:T(8,128)(2,1)S(1)}, bf16[16,32,128]{2,1,0:T(8,128)(2,1)S(1)}, u32[]{:S(2)}, u32[]{:S(2)}) collective-permute-start(bf16[16,32,128]{2,1,0:T(8,128)(2,1)S(1)} %slice.4), channel_id=1, source_target_pairs={{0,32},{32,0},{1,33},{33,1},{2,34},{34,2},{3,35},{35,3},{4,36},{36... | collective-permute-start | bytes 393224 | tf_op jit(solution)/shard_map/ppermute | solution.py:435
  90.9 0.9 copy-start.7
  104.9 9.5 %copy-start.3 = (bf16[32,32,128]{2,1,0:T(8,128)(2,1)}, bf16[32,32,128]{2,1,0:T(8,128)(2,1)S(1)}, u32[]{:S(2)}) copy-start(bf16[32,32,128]{2,1,0:T(8,128)(2,1)S(1)} %pad_maximum_fusion.own_ref) | copy-start | bytes 786436
  104.9 13.3 %collective-permute-start.2 = (bf16[32,32,128]{2,1,0:T(8,128)(2,1)S(1)}, bf16[32,32,128]{2,1,0:T(8,128)(2,1)S(1)}, u32[]{:S(2)}, u32[]{:S(2)}) collective-permute-start(bf16[32,32,128]{2,1,0:T(8,128)(2,1)S(1)} %pad_maximum_fusion.own_ref), channel_id=1, source_target_pairs={{0,64},{64,128},{128,192},{192,0},{1,65},{65,129},{129,193},{193,1... | collective-permute-start | bytes 786440 | tf_op jit(solution)/shard_map/ppermute | solution.py:438
  105.4 12.8 %collective-permute-start.3 = (bf16[32,32,128]{2,1,0:T(8,128)(2,1)S(1)}, bf16[32,32,128]{2,1,0:T(8,128)(2,1)S(1)}, u32[]{:S(2)}, u32[]{:S(2)}) collective-permute-start(bf16[32,32,128]{2,1,0:T(8,128)(2,1)S(1)} %pad_maximum_fusion.own_ref), channel_id=1, source_target_pairs={{0,128},{64,192},{128,0},{192,64},{1,129},{65,193},{129,1},{193,65... | collective-permute-start | bytes 786440 | tf_op jit(solution)/shard_map/ppermute | solution.py:438
  107.1 11.8 %collective-permute-start.4 = (bf16[32,32,128]{2,1,0:T(8,128)(2,1)S(1)}, bf16[32,32,128]{2,1,0:T(8,128)(2,1)S(1)}, u32[]{:S(2)}, u32[]{:S(2)}) collective-permute-start(bf16[32,32,128]{2,1,0:T(8,128)(2,1)S(1)} %pad_maximum_fusion.own_ref), channel_id=1, source_target_pairs={{0,192},{64,0},{128,64},{192,128},{1,193},{65,1},{129,65},{193,129... | collective-permute-start | bytes 786440 | tf_op jit(solution)/shard_map/ppermute | solution.py:438
  118.2 0.7 copy-start.8
  118.2 0.8 copy-start.9
  119.0 0.7 copy-start.10
  125.2 21.5 %all-to-all-start.2 = ((bf16[16,72,128]{2,1,0:T(8,128)(2,1)}), bf16[16,72,128]{2,1,0:T(8,128)(2,1)S(1)}, u32[]{:S(2)}, u32[]{:S(2)}) async-start(bf16[16,72,128]{2,1,0:T(8,128)(2,1)} %far.1), calls=%async_computation.2 | async-start | bytes 589824 | tf_op jit(solution)/shard_map/all_to_all | solution.py:421
  146.7 0.7 copy-start.1

commit v4 on v3

--- a/solution.py
+++ b/solution.py
@@ -58,13 +58,14 @@
             part = jnp.dot(
                 w_ref[:, window : window + wide], pick[:wide], preferred_element_type=F32
             )
-            out_ref[p, j] = part.astype(BF)
+            column = 512 + 128 * (p % 2) if j == 2 else 256 * (p % 2) + 128 * j
+            out_ref[p // 2, :, column : column + 128] = part.astype(BF)
 
 
 def widen(w_qkv):
     return pl.pallas_call(
         widen_kernel,
-        out_shape=jax.ShapeDtypeStruct((8, 3, WIDTH, 128), BF),
+        out_shape=jax.ShapeDtypeStruct((4, WIDTH, WIDTH), BF),
         cost_estimate=pl.CostEstimate(
             flops=10_000_000_000, bytes_accessed=8_000_000, transcendentals=0
         ),
@@ -80,10 +81,12 @@
         normed[...] = norm_rows(x_ref[...].astype(F32), gain_ref[...]).astype(BF)
 
     rows = normed[...]
+    projected = jnp.dot(rows, w_ref[0], preferred_element_type=F32)
+    projected = projected.astype(BF).astype(F32)
     for u in range(2):
-        k = jnp.dot(rows, w_ref[u, 0], preferred_element_type=F32).astype(BF).astype(F32)
-        v = jnp.dot(rows, w_ref[u, 1], preferred_element_type=F32).astype(BF).astype(F32)
-        q = jnp.dot(rows, w_ref[u, 2], preferred_element_type=F32).astype(BF).astype(F32)
+        k = projected[:, 256 * u : 256 * u + 128]
+        v = projected[:, 256 * u + 128 : 256 * u + 256]
+        q = projected[:, 512 + 128 * u : 640 + 128 * u]
         k, v = mask_key_value(k, v, s_ref[1] * ROWS, s_ref[0])
         q = jnp.where(lanes(q.shape) % WIDE == HEAD, 1.0, q)
         stage[u, 0] = k
@@ -123,7 +126,7 @@
             in_specs=[
                 pl.BlockSpec((ROWS, WIDTH), lambda p, s: (0, 0)),
                 pl.BlockSpec((1, WIDTH), lambda p, s: (0, 0)),
-                pl.BlockSpec((2, 3, WIDTH, 128), lambda p, s: (p, 0, 0, 0)),
+                pl.BlockSpec((1, WIDTH, WIDTH), lambda p, s: (p, 0, 0)),
             ],
             out_specs=[
                 pl.BlockSpec((2, 3, ROWS, 128), lambda p, s: (p, 0, 0, 0)),
@@ -176,8 +179,8 @@
         normed[...] = norm_rows(x_ref[...].astype(F32), gain_ref[...]).astype(BF)
 
     rows = normed[...]
-    k = jnp.dot(rows, w_ref[0, 0], preferred_element_type=F32).astype(BF).astype(F32)
-    v = jnp.dot(rows, w_ref[0, 1], preferred_element_type=F32).astype(BF).astype(F32)
+    projected = jnp.dot(rows, w_ref[0], preferred_element_type=F32).astype(BF).astype(F32)
+    k, v = projected[:, :128], projected[:, 128:]
     partner = s_ref[1] + 1 - 2 * (s_ref[1] % 2)
     k, v = mask_key_value(k, v, partner * ROWS, s_ref[0])
     keys[:ROWS] = own_ref[0, 0]
@@ -210,7 +213,9 @@
             in_specs=[
                 pl.BlockSpec((ROWS, WIDTH), lambda p, s: (0, 0)),
                 pl.BlockSpec((1, WIDTH), lambda p, s: (0, 0)),
-                pl.BlockSpec((1, 2, WIDTH, 128), lambda p, s: (p + first, 0, 0, 0)),
+                pl.BlockSpec(
+                    (1, WIDTH, 256), lambda p, s: ((p + first) // 2, 0, (p + first) % 2)
+                ),
                 pl.BlockSpec((1, 3, ROWS, 128), lambda p, s: (p + first, 0, 0, 0)),
             ],
             out_specs=pl.BlockSpec((2, WIDE, ROWS), lambda p, s: (p, 0, 0)),
@@ -270,22 +275,27 @@
         values = values_t[base : base + HEAD]
         values_t[base : base + HEAD] = jnp.where(alive, values, jnp.zeros_like(values))
     keys[...] = keys_t[...].T
+    streams = []
     for c in range(0, 1024, 512):
         queries = queries_t[:, c : c + 512]
         owner = lax.broadcasted_iota(jnp.int32, queries.shape, 0) // WIDE
         for g in range(2):
             part = jnp.where(owner == g, queries, jnp.zeros_like(queries))
-            numer, m = attend(
-                lambda i: jnp.dot(
-                    keys[256 * i : 256 * i + 256], part, preferred_element_type=F32
-                ),
-                values_t[g * WIDE : (g + 1) * WIDE],
-                scores.at[g],
-                weights.at[g],
+            streams.append(
+                (
+                    lambda i, part=part: jnp.dot(
+                        keys[256 * i : 256 * i + 256], part, preferred_element_type=F32
+                    ),
+                    values_t[g * WIDE : (g + 1) * WIDE],
+                    scores.at[g],
+                    weights.at[g],
+                    (),
+                )
             )
-            out = packed_result(numer, m).astype(BF)
-            for i in range(4):
-                out_ref[8 * g + c // 128 + i] = out[:, i * 128 : (i + 1) * 128]
+    for n, (numer, m) in enumerate(attend_all(streams)):
+        out = packed_result(numer, m).astype(BF)
+        for i in range(4):
+            out_ref[8 * (n % 2) + 4 * (n // 2) + i] = out[:, i * 128 : (i + 1) * 128]
 
 
 def middle(scalars, received):
@@ -348,7 +358,20 @@
     )(*keys, received, mid_result)
 
 
-def finish_kernel(s_ref, near0_ref, near1_ref, near2_ref, in_ref, x_ref, gain_ref, w_ref, out_ref, mixed):
+def finish_kernel(
+    s_ref, near0, near1, near2, in_ref, x_hbm, gain_ref, w_hbm, out_ref, mixed, x_ref, w_ref, near_ref, sems
+):
+    arrivals = {}
+    for n, (source, first, heads) in enumerate(((near0, 0, 5), (near0, 5, 5), (near1, 10, 4), (near2, 14, 2))):
+        part = source.at[5:10] if n == 1 else source.at[0:heads]
+        arrivals[first] = pltpu.make_async_copy(part, near_ref.at[first : first + heads], sems.at[n])
+        arrivals[first].start()
+    copies = [
+        pltpu.make_async_copy(x_hbm, x_ref, sems.at[4]),
+        pltpu.make_async_copy(w_hbm, w_ref, sems.at[5]),
+    ]
+    for copy in copies:
+        copy.start()
     lane = lanes((1, ROWS))
     column4 = lanes((128, ROWS)) - 4 * lax.broadcasted_iota(jnp.int32, (128, ROWS), 0)
     column16 = lanes((16, 256)) - 16 * lax.broadcasted_iota(jnp.int32, (16, 256), 0)
@@ -356,9 +379,9 @@
         off = s_ref[2 + h]
         off4 = off % 4
         off16 = off % 16
-        near_ref = near0_ref if h < 10 else near1_ref if h < 14 else near2_ref
-        i = h if h < 10 else h - 10 if h < 14 else h - 14
-        mean_n, lse_n = to_lse(near_ref[i], near_ref[i, HEAD + 1 : HEAD + 2])
+        if h in arrivals:
+            arrivals[h].wait()
+        mean_n, lse_n = to_lse(near_ref[h], near_ref[h, HEAD + 1 : HEAD + 2])
         spread4 = jnp.where(column4 == off4, 1.0, 0.0).astype(BF)
         mid = jnp.dot(
             in_ref[h, 16:], spread4, preferred_element_type=F32
@@ -387,6 +410,8 @@
         ).astype(BF)
     attended = mixed[...].T.astype(F32)
     sub = norm_rows(attended, gain_ref[...]).astype(BF)
+    for copy in copies:
+        copy.wait()
     out = x_ref[...].astype(F32) + jnp.dot(sub, w_ref[...], preferred_element_type=F32)
     out_ref[...] = out.astype(BF)
 
@@ -401,16 +426,22 @@
             num_scalar_prefetch=1,
             grid=(1,),
             in_specs=[
-                whole(10, WIDE, ROWS),
-                whole(4, WIDE, ROWS),
-                whole(2, WIDE, ROWS),
+                pl.BlockSpec(memory_space=pl.ANY),
+                pl.BlockSpec(memory_space=pl.ANY),
+                pl.BlockSpec(memory_space=pl.ANY),
                 whole(16, 72, 128),
-                whole(ROWS, WIDTH),
+                pl.BlockSpec(memory_space=pl.ANY),
                 whole(1, WIDTH),
-                whole(WIDTH, WIDTH),
+                pl.BlockSpec(memory_space=pl.ANY),
             ],
             out_specs=whole(ROWS, WIDTH),
-            scratch_shapes=[pltpu.VMEM((WIDTH, ROWS), BF)],
+            scratch_shapes=[
+                pltpu.VMEM((WIDTH, ROWS), BF),
+                pltpu.VMEM((ROWS, WIDTH), BF),
+                pltpu.VMEM((WIDTH, WIDTH), BF),
+                pltpu.VMEM((HEADS, WIDE, ROWS), F32),
+                pltpu.SemaphoreType.DMA((6,)),
+            ],
         ),
         out_shape=jax.ShapeDtypeStruct((ROWS, WIDTH), BF),
         name="finish",

time: 155 us -> 153 us (0.987)
  Pallas kernels: 60 us -> 56.8 us
    pallas_call x1, Pallas kernels: 10.3 us -> 8.53 us  [project(): pl.pallas_call(project_kernel, grid_spec=pltpu.PrefetchScalarGridSpec(num...]
  transfers between devices with their start and end apart: 8 -> 8, of which waited for: 5 -> 5; matrix products, arithmetic and copies ran while one was open for 1% -> 1% of each run, Pallas kernels for 25% -> 24%
where the time goes in v4:
time: 153 us; the launch traced here: 151 us
  Pallas kernels  56.8 us (37%)
  waiting for transfers between devices  49.1 us (32%)
  starting transfers between devices  36.7 us (24%)
  local copies, waits for them, and re-layouts  7.05 us (5%)
    all_to_all x3, waiting for transfers between devices, exchange(): return lax.all_to_all(value, axis, split_axis=0, concat_axis=0, tiled=True)  33.5 us
    all_to_all x3, starting transfers between devices, exchange(): return lax.all_to_all(value, axis, split_axis=0, concat_axis=0, tiled=True)  29.2 us
    pallas_call x3, Pallas kernels, near(): pl.pallas_call(near_kernel, grid_spec=pltpu.PrefetchScalarGridSpec(num_sc...  24.2 us
    ppermute x1, waiting for transfers between devices, body(): partner = lax.ppermute(rows, 'z', [(i, i ^ 1) for i in range(8)])  10.4 us
    pallas_call x1, Pallas kernels, project(): pl.pallas_call(project_kernel, grid_spec=pltpu.PrefetchScalarGridSpec(num...  8.53 us
    pallas_call x1, Pallas kernels, widen(): pl.pallas_call(widen_kernel, out_shape=jax.ShapeDtypeStruct((4, WIDTH, WI...  6.73 us
    pallas_call x1, Pallas kernels, finish(): pl.pallas_call(finish_kernel, grid_spec=pltpu.PrefetchScalarGridSpec(num_...  6.42 us
    pallas_call x1, Pallas kernels, far(): pl.pallas_call(far_kernel, out_shape=jax.ShapeDtypeStruct((16, 72, 128),...  5.48 us
  transfers between devices with their start and end apart: 8, of which 5 were waited for; matrix products, arithmetic and copies ran while one was open for 1% of the time, Pallas kernels for 24%

profile of v4, /device:TPU:38, one launch (start us, length us, event | category | flops | bytes accessed | tf_op | source)
XLA Modules:
  0.0 151.1 jit_solution(4433058775145905728)
XLA Ops:
  0.0 0.0 copy-start.4
  0.0 0.0 copy-start.6
  0.0 2.4 %reshape.6 = bf16[128,4,768]{2,1,0:T(4,128)(2,1)} reshape(bf16[512,768]{1,0:T(8,128)(2,1)} %param.7) | data formatting | bytes 1572864 | tf_op jit(solution)/shard_map/reshape | solution.py:459
  2.4 15.0 %all-to-all-start = ((bf16[128,4,768]{2,1,0:T(4,128)(2,1)}), bf16[128,4,768]{2,1,0:T(4,128)(2,1)S(1)}, u32[]{:S(2)}, u32[]{:S(2)}) async-start(bf16[128,4,768]{2,1,0:T(4,128)(2,1)} %reshape.6), calls=%async_computation | async-start | bytes 1572864 | tf_op jit(solution)/shard_map/all_to_all | solution.py:452
  18.0 0.0 copy-done.4
  18.0 0.6 broadcast_in_dim.10.gain_ref
  18.6 0.0 copy-done.6
  18.6 0.6 pad_add_fusion.s_ref
  19.2 6.7 %widen.1.w_ref = bf16[4,768,768]{2,1,0:T(8,128)(2,1)} custom-call(bf16[768,2304]{1,0:T(8,128)(2,1)} %w_ref.1), custom_call_target="tpu_custom_call" | custom-call | flops 10000000000 | bytes 8000000 | tf_op jit(solution)/shard_map/widen/pallas_call | solution.py:66
  25.9 14.7 %all-to-all-done = bf16[128,4,768]{2,1,0:T(4,128)(2,1)S(1)} async-done(((bf16[128,4,768]{2,1,0:T(4,128)(2,1)}), bf16[128,4,768]{2,1,0:T(4,128)(2,1)S(1)}, u32[]{:S(2)}, u32[]{:S(2)}) %all-to-all-start) | async-done | bytes 786464 | tf_op jit(solution)/shard_map/all_to_all | solution.py:452
  40.6 1.0 copy.9
  41.5 0.0 copy-start
  41.6 0.0 copy-start.5
  41.6 8.5 %project.1 = (bf16[8,3,512,128]{3,2,1,0:T(8,128)(2,1)}, bf16[16,192,128]{2,1,0:T(8,128)(2,1)}) custom-call(s32[18]{0:T(128)} %pad_add_fusion.s_ref, bf16[512,768]{1,0:T(8,128)(2,1)} %bitcast.3, f32[1,768]{1,0:T(1,128)} %broadcast_in_dim.10.gain_ref, bf16[4,768,768]{2,1,0:T(8,128)(2,1)} %widen.1.w_ref), custom_call_target="tpu_custom_call" | custom-call | tf_op jit(solution)/shard_map/project/pallas_call | solution.py:121
  50.1 4.9 %all-to-all-start.1 = ((bf16[16,192,128]{2,1,0:T(8,128)(2,1)}), bf16[16,192,128]{2,1,0:T(8,128)(2,1)S(1)}, u32[]{:S(2)}, u32[]{:S(2)}) async-start(bf16[16,192,128]{2,1,0:T(8,128)(2,1)} %get-tuple-element.8), calls=%async_computation.1 | async-start | bytes 1572864 | tf_op jit(solution)/shard_map/all_to_all | solution.py:452
  54.9 0.0 copy-done
  54.9 0.7 collective-permute-start
  55.6 0.0 copy-done.5
  55.6 0.6 broadcast_in_dim.11.gain_ref
  56.2 18.8 %all-to-all-done.1.in_ref.refs_3_ = bf16[16,192,128]{2,1,0:T(8,128)(2,1)S(1)} async-done(((bf16[16,192,128]{2,1,0:T(8,128)(2,1)}), bf16[16,192,128]{2,1,0:T(8,128)(2,1)S(1)}, u32[]{:S(2)}, u32[]{:S(2)}) %all-to-all-start.1) | async-done | bytes 786464 | tf_op jit(solution)/shard_map/all_to_all | solution.py:452
  75.0 0.0 copy-start.2
  75.0 3.6 %collective-permute-start.1 = (bf16[16,32,128]{2,1,0:T(8,128)(2,1)S(1)}, bf16[16,32,128]{2,1,0:T(8,128)(2,1)S(1)}, u32[]{:S(2)}, u32[]{:S(2)}) collective-permute-start(bf16[16,32,128]{2,1,0:T(8,128)(2,1)S(1)} %slice.4), channel_id=1, source_target_pairs={{0,32},{32,0},{1,33},{33,1},{2,34},{34,2},{3,35},{35,3},{4,36},{36... | collective-permute-start | bytes 393224 | tf_op jit(solution)/shard_map/ppermute | solution.py:466
  78.6 10.4 %collective-permute-done.x_ref = bf16[512,768]{1,0:T(8,128)(2,1)S(1)} collective-permute-done((bf16[512,768]{1,0:T(8,128)(2,1)S(1)}, bf16[512,768]{1,0:T(8,128)(2,1)S(1)}, u32[]{:S(2)}, u32[]{:S(2)}) %collective-permute-start) | collective-permute-done | bytes 786464 | tf_op jit(solution)/shard_map/ppermute | solution.py:461
  89.1 0.0 copy-start.7
  89.1 0.9 copy-done.7
  89.9 12.4 %near.3.near0 = f32[10,64,512]{2,1,0:T(8,128)} custom-call(s32[18]{0:T(128)} %pad_add_fusion.s_ref, bf16[512,768]{1,0:T(8,128)(2,1)} %copy-done.7, f32[1,768]{1,0:T(1,128)} %broadcast_in_dim.10.gain_ref, bf16[4,768,768]{2,1,0:T(8,128)(2,1)} %widen.1.w_ref, bf16[8,3,512,128]{3,2,1,0:T(8,128)(2,1)} %get-tuple-element.7.own_ref), custom_call_target="tpu_custom_call" | custom-call | flops 24999999488 | bytes 5000000 | tf_op jit(solution)/shard_map/near/pallas_call | solution.py:208
  102.4 0.0 copy-done.2
  102.4 0.0 collective-permute-done.1
  102.4 0.0 copy-start.3
  102.4 0.5 collective-permute-start.2
  102.9 1.7 %collective-permute-start.3 = (bf16[32,32,128]{2,1,0:T(8,128)(2,1)S(1)}, bf16[32,32,128]{2,1,0:T(8,128)(2,1)S(1)}, u32[]{:S(2)}, u32[]{:S(2)}) collective-permute-start(bf16[32,32,128]{2,1,0:T(8,128)(2,1)S(1)} %pad_maximum_fusion.own_ref), channel_id=1, source_target_pairs={{0,128},{64,192},{128,0},{192,64},{1,129},{65,193},{129,1},{193,65... | collective-permute-start | bytes 786440 | tf_op jit(solution)/shard_map/ppermute | solution.py:469
  104.6 1.2 collective-permute-start.4
  105.8 5.4 %middle.1.refs_4_ = bf16[16,64,128]{2,1,0:T(8,128)(2,1)} custom-call(s32[18]{0:T(128)} %pad_add_fusion.s_ref, bf16[16,192,128]{2,1,0:T(8,128)(2,1)} %copy-done.2), custom_call_target="tpu_custom_call" | custom-call | flops 10000000000 | bytes 1000000 | tf_op jit(solution)/shard_map/middle/pallas_call | solution.py:302
  111.1 0.0 copy-done.3
  111.2 4.6 %collective-permute-done.2.refs_0_ = bf16[32,32,128]{2,1,0:T(8,128)(2,1)S(1)} collective-permute-done((bf16[32,32,128]{2,1,0:T(8,128)(2,1)S(1)}, bf16[32,32,128]{2,1,0:T(8,128)(2,1)S(1)}, u32[]{:S(2)}, u32[]{:S(2)}) %collective-permute-start.2) | collective-permute-done | bytes 262176 | tf_op jit(solution)/shard_map/ppermute | solution.py:469
  115.7 0.0 copy-start.8
  115.7 0.0 collective-permute-done.3.refs_1_
  115.7 0.6 collective-permute-done.4.refs_2_
  116.3 0.1 copy-done.8
  116.4 0.1 copy-done.9
  116.5 0.7 copy-done.10
  117.2 5.5 %far.1 = bf16[16,72,128]{2,1,0:T(8,128)(2,1)} custom-call(bf16[32,32,128]{2,1,0:T(8,128)(2,1)} %copy-done.3, bf16[32,32,128]{2,1,0:T(8,128)(2,1)} %copy-done.8, bf16[32,32,128]{2,1,0:T(8,128)(2,1)} %copy-done.9, bf16[32,32,128]{2,1,0:T(8,128)(2,1)} %copy-done.10, bf16[16,192,128]{2,1,0:T(8,128)(2,1)} %copy-done.2, bf16[16,64,128]{2,1,0:T(8,128)(2,1)} %middle.1.refs_4_), custom_call_target="tpu_custom_call" | custom-call | flops 10000000000 | bytes 1000000 | tf_op jit(solution)/shard_map/far/pallas_call | solution.py:346
  122.7 9.3 %all-to-all-start.2 = ((bf16[16,72,128]{2,1,0:T(8,128)(2,1)}), bf16[16,72,128]{2,1,0:T(8,128)(2,1)S(1)}, u32[]{:S(2)}, u32[]{:S(2)}) async-start(bf16[16,72,128]{2,1,0:T(8,128)(2,1)} %far.1), calls=%async_computation.2 | async-start | bytes 589824 | tf_op jit(solution)/shard_map/all_to_all | solution.py:452
  132.0 6.9 %near.4.near1 = f32[4,64,512]{2,1,0:T(8,128)} custom-call(s32[18]{0:T(128)} %pad_add_fusion.s_ref, bf16[512,768]{1,0:T(8,128)(2,1)} %copy-done.7, f32[1,768]{1,0:T(1,128)} %broadcast_in_dim.10.gain_ref, bf16[4,768,768]{2,1,0:T(8,128)(2,1)} %widen.1.w_ref, bf16[8,3,512,128]{3,2,1,0:T(8,128)(2,1)} %get-tuple-element.7.own_ref), custom_call_target="tpu_custom_call" | custom-call | flops 10000000000 | bytes 2000000 | tf_op jit(solution)/shard_map/near/pallas_call | solution.py:208
  139.0 4.8 %near.5.near2 = f32[2,64,512]{2,1,0:T(8,128)} custom-call(s32[18]{0:T(128)} %pad_add_fusion.s_ref, bf16[512,768]{1,0:T(8,128)(2,1)} %copy-done.7, f32[1,768]{1,0:T(1,128)} %broadcast_in_dim.10.gain_ref, bf16[4,768,768]{2,1,0:T(8,128)(2,1)} %widen.1.w_ref, bf16[8,3,512,128]{3,2,1,0:T(8,128)(2,1)} %get-tuple-element.7.own_ref), custom_call_target="tpu_custom_call" | custom-call | flops 5000000000 | bytes 1000000 | tf_op jit(solution)/shard_map/near/pallas_call | solution.py:208
  143.8 0.0 all-to-all-done.2.in_ref
  143.8 0.7 copy-done.1
  144.5 6.4 %finish.1 = bf16[512,768]{1,0:T(8,128)(2,1)} custom-call(s32[18]{0:T(128)} %pad_add_fusion.s_ref, f32[10,64,512]{2,1,0:T(8,128)} %near.3.near0, f32[4,64,512]{2,1,0:T(8,128)} %near.4.near1, f32[2,64,512]{2,1,0:T(8,128)} %near.5.near2, bf16[16,72,128]{2,1,0:T(8,128)(2,1)} %copy-done.1, bf16[512,768]{1,0:T(8,128)(2,1)} %bitcast.4, ...), custom_call_target="tpu_custom_call" | custom-call | tf_op jit(solution)/shard_map/finish/pallas_call | solution.py:423
  (5 shorter events, 0.0 us)
Async XLA Ops:
  0.0 18.0 %copy-start.4 = (f32[768]{0:T(1024)S(1)}, f32[768]{0:T(1024)}, u32[]{:S(2)}) copy-start(f32[768]{0:T(1024)} %param.10) | copy-start | bytes 9220
  0.0 18.6 %copy-start.6 = (s32[16]{0:T(128)S(1)}, s32[16]{0:T(128)}, u32[]{:S(2)}) copy-start(s32[16]{0:T(128)} %param.9) | copy-start | bytes 196
  2.4 38.2 %all-to-all-start = ((bf16[128,4,768]{2,1,0:T(4,128)(2,1)}), bf16[128,4,768]{2,1,0:T(4,128)(2,1)S(1)}, u32[]{:S(2)}, u32[]{:S(2)}) async-start(bf16[128,4,768]{2,1,0:T(4,128)(2,1)} %reshape.6), calls=%async_computation | async-start | bytes 1572864 | tf_op jit(solution)/shard_map/all_to_all | solution.py:452
  41.5 13.4 %copy-start = (bf16[4,128,768]{2,1,0:T(8,128)(2,1)S(1)}, bf16[4,128,768]{2,1,0:T(8,128)(2,1)}, u32[]{:S(2)}) copy-start(bf16[4,128,768]{2,1,0:T(8,128)(2,1)} %copy.9) | copy-start | bytes 2359300
  41.6 14.0 %copy-start.5 = (f32[768]{0:T(1024)S(1)}, f32[768]{0:T(1024)}, u32[]{:S(2)}) copy-start(f32[768]{0:T(1024)} %param.12) | copy-start | bytes 9220
  50.1 24.9 %all-to-all-start.1 = ((bf16[16,192,128]{2,1,0:T(8,128)(2,1)}), bf16[16,192,128]{2,1,0:T(8,128)(2,1)S(1)}, u32[]{:S(2)}, u32[]{:S(2)}) async-start(bf16[16,192,128]{2,1,0:T(8,128)(2,1)} %get-tuple-element.8), calls=%async_computation.1 | async-start | bytes 1572864 | tf_op jit(solution)/shard_map/all_to_all | solution.py:452
  54.9 34.1 %collective-permute-start = (bf16[512,768]{1,0:T(8,128)(2,1)S(1)}, bf16[512,768]{1,0:T(8,128)(2,1)S(1)}, u32[]{:S(2)}, u32[]{:S(2)}) collective-permute-start(bf16[512,768]{1,0:T(8,128)(2,1)S(1)} %bitcast.5), channel_id=1, source_target_pairs={{0,2},{2,0},{4,6},{6,4},{8,10},{10,8},{12,14},{14,12},{1,3},{3,1},... | collective-permute-start | bytes 2359304 | tf_op jit(solution)/shard_map/ppermute | solution.py:461
  75.0 27.4 %copy-start.2 = (bf16[16,192,128]{2,1,0:T(8,128)(2,1)}, bf16[16,192,128]{2,1,0:T(8,128)(2,1)S(1)}, u32[]{:S(2)}) copy-start(bf16[16,192,128]{2,1,0:T(8,128)(2,1)S(1)} %all-to-all-done.1.in_ref.refs_3_) | copy-start | bytes 2359300
  75.0 27.3 %collective-permute-start.1 = (bf16[16,32,128]{2,1,0:T(8,128)(2,1)S(1)}, bf16[16,32,128]{2,1,0:T(8,128)(2,1)S(1)}, u32[]{:S(2)}, u32[]{:S(2)}) collective-permute-start(bf16[16,32,128]{2,1,0:T(8,128)(2,1)S(1)} %slice.4), channel_id=1, source_target_pairs={{0,32},{32,0},{1,33},{33,1},{2,34},{34,2},{3,35},{35,3},{4,36},{36... | collective-permute-start | bytes 393224 | tf_op jit(solution)/shard_map/ppermute | solution.py:466
  89.1 0.9 copy-start.7
  102.4 8.7 %copy-start.3 = (bf16[32,32,128]{2,1,0:T(8,128)(2,1)}, bf16[32,32,128]{2,1,0:T(8,128)(2,1)S(1)}, u32[]{:S(2)}) copy-start(bf16[32,32,128]{2,1,0:T(8,128)(2,1)S(1)} %pad_maximum_fusion.own_ref) | copy-start | bytes 786436
  102.4 13.3 %collective-permute-start.2 = (bf16[32,32,128]{2,1,0:T(8,128)(2,1)S(1)}, bf16[32,32,128]{2,1,0:T(8,128)(2,1)S(1)}, u32[]{:S(2)}, u32[]{:S(2)}) collective-permute-start(bf16[32,32,128]{2,1,0:T(8,128)(2,1)S(1)} %pad_maximum_fusion.own_ref), channel_id=1, source_target_pairs={{0,64},{64,128},{128,192},{192,0},{1,65},{65,129},{129,193},{193,1... | collective-permute-start | bytes 786440 | tf_op jit(solution)/shard_map/ppermute | solution.py:469
  102.9 12.8 %collective-permute-start.3 = (bf16[32,32,128]{2,1,0:T(8,128)(2,1)S(1)}, bf16[32,32,128]{2,1,0:T(8,128)(2,1)S(1)}, u32[]{:S(2)}, u32[]{:S(2)}) collective-permute-start(bf16[32,32,128]{2,1,0:T(8,128)(2,1)S(1)} %pad_maximum_fusion.own_ref), channel_id=1, source_target_pairs={{0,128},{64,192},{128,0},{192,64},{1,129},{65,193},{129,1},{193,65... | collective-permute-start | bytes 786440 | tf_op jit(solution)/shard_map/ppermute | solution.py:469
  104.6 11.8 %collective-permute-start.4 = (bf16[32,32,128]{2,1,0:T(8,128)(2,1)S(1)}, bf16[32,32,128]{2,1,0:T(8,128)(2,1)S(1)}, u32[]{:S(2)}, u32[]{:S(2)}) collective-permute-start(bf16[32,32,128]{2,1,0:T(8,128)(2,1)S(1)} %pad_maximum_fusion.own_ref), channel_id=1, source_target_pairs={{0,192},{64,0},{128,64},{192,128},{1,193},{65,1},{129,65},{193,129... | collective-permute-start | bytes 786440 | tf_op jit(solution)/shard_map/ppermute | solution.py:469
  115.7 0.7 copy-start.8
  115.7 0.8 copy-start.9
  116.5 0.7 copy-start.10
  122.7 21.1 %all-to-all-start.2 = ((bf16[16,72,128]{2,1,0:T(8,128)(2,1)}), bf16[16,72,128]{2,1,0:T(8,128)(2,1)S(1)}, u32[]{:S(2)}, u32[]{:S(2)}) async-start(bf16[16,72,128]{2,1,0:T(8,128)(2,1)} %far.1), calls=%async_computation.2 | async-start | bytes 589824 | tf_op jit(solution)/shard_map/all_to_all | solution.py:452
  143.8 0.7 copy-start.1

commit v5 on v4

--- a/solution.py
+++ b/solution.py
@@ -140,10 +140,6 @@
         ],
         name="project",
     )(scalars, rows, gain, weights)
-
-
-def attend(score, values_t, scores, weights, bonus=()):
-    return attend_all([(score, values_t, scores, weights, bonus)])[0]
 
 
 def attend_all(streams):
@@ -331,13 +327,17 @@
     queries = jnp.concatenate([packed, pltpu.roll(packed, WIDE, 1)], axis=0)
     queries = jnp.where(lanes(queries.shape) < WIDE, queries, 0.0).astype(BF)
 
-    def score(c):
-        block = key_refs[c // 4][8 * (c % 4) : 8 * (c % 4) + 8]
-        return nt(block.reshape(256, 128), queries)
-
-    numer, m = attend(score, values_t[...], scores, weights, range(4))
-    out = packed_result(numer, m)
-    out = jnp.concatenate([out[:, :256], out[:, 256:]], axis=0).T.astype(BF)
+    streams = []
+    for half in range(2):
+        part = queries[256 * half : 256 * half + 256]
+
+        def score(c, part=part):
+            block = key_refs[c // 4][8 * (c % 4) : 8 * (c % 4) + 8]
+            return nt(block.reshape(256, 128), part)
+
+        streams.append((score, values_t[...], scores.at[half], weights.at[half], range(4)))
+    out = [packed_result(numer, m) for numer, m in attend_all(streams)]
+    out = jnp.concatenate(out, axis=0).T.astype(BF)
     out_ref[:, :16] = out.reshape(16, 16, 128)
     out_ref[:, 16:] = mid_ref[:, :56]
 
@@ -347,8 +347,8 @@
         far_kernel,
         out_shape=jax.ShapeDtypeStruct((16, 72, 128), BF),
         scratch_shapes=[
-            pltpu.VMEM((4096, 512), F32),
-            pltpu.VMEM((4096, 512), BF),
+            pltpu.VMEM((2, 4096, 256), F32),
+            pltpu.VMEM((2, 4096, 256), BF),
             pltpu.VMEM((WIDE, 4096), BF),
         ],
         cost_estimate=pl.CostEstimate(
@@ -358,20 +358,7 @@
     )(*keys, received, mid_result)
 
 
-def finish_kernel(
-    s_ref, near0, near1, near2, in_ref, x_hbm, gain_ref, w_hbm, out_ref, mixed, x_ref, w_ref, near_ref, sems
-):
-    arrivals = {}
-    for n, (source, first, heads) in enumerate(((near0, 0, 5), (near0, 5, 5), (near1, 10, 4), (near2, 14, 2))):
-        part = source.at[5:10] if n == 1 else source.at[0:heads]
-        arrivals[first] = pltpu.make_async_copy(part, near_ref.at[first : first + heads], sems.at[n])
-        arrivals[first].start()
-    copies = [
-        pltpu.make_async_copy(x_hbm, x_ref, sems.at[4]),
-        pltpu.make_async_copy(w_hbm, w_ref, sems.at[5]),
-    ]
-    for copy in copies:
-        copy.start()
+def finish_kernel(s_ref, near0_ref, near1_ref, near2_ref, in_ref, x_ref, gain_ref, w_ref, out_ref, mixed):
     lane = lanes((1, ROWS))
     column4 = lanes((128, ROWS)) - 4 * lax.broadcasted_iota(jnp.int32, (128, ROWS), 0)
     column16 = lanes((16, 256)) - 16 * lax.broadcasted_iota(jnp.int32, (16, 256), 0)
@@ -379,9 +366,9 @@
         off = s_ref[2 + h]
         off4 = off % 4
         off16 = off % 16
-        if h in arrivals:
-            arrivals[h].wait()
-        mean_n, lse_n = to_lse(near_ref[h], near_ref[h, HEAD + 1 : HEAD + 2])
+        near_ref = near0_ref if h < 10 else near1_ref if h < 14 else near2_ref
+        i = h if h < 10 else h - 10 if h < 14 else h - 14
+        mean_n, lse_n = to_lse(near_ref[i], near_ref[i, HEAD + 1 : HEAD + 2])
         spread4 = jnp.where(column4 == off4, 1.0, 0.0).astype(BF)
         mid = jnp.dot(
             in_ref[h, 16:], spread4, preferred_element_type=F32
@@ -410,8 +397,6 @@
         ).astype(BF)
     attended = mixed[...].T.astype(F32)
     sub = norm_rows(attended, gain_ref[...]).astype(BF)
-    for copy in copies:
-        copy.wait()
     out = x_ref[...].astype(F32) + jnp.dot(sub, w_ref[...], preferred_element_type=F32)
     out_ref[...] = out.astype(BF)
 
@@ -426,22 +411,16 @@
             num_scalar_prefetch=1,
             grid=(1,),
             in_specs=[
-                pl.BlockSpec(memory_space=pl.ANY),
-                pl.BlockSpec(memory_space=pl.ANY),
-                pl.BlockSpec(memory_space=pl.ANY),
+                whole(10, WIDE, ROWS),
+                whole(4, WIDE, ROWS),
+                whole(2, WIDE, ROWS),
                 whole(16, 72, 128),
-                pl.BlockSpec(memory_space=pl.ANY),
+                whole(ROWS, WIDTH),
                 whole(1, WIDTH),
-                pl.BlockSpec(memory_space=pl.ANY),
+                whole(WIDTH, WIDTH),
             ],
             out_specs=whole(ROWS, WIDTH),
-            scratch_shapes=[
-                pltpu.VMEM((WIDTH, ROWS), BF),
-                pltpu.VMEM((ROWS, WIDTH), BF),
-                pltpu.VMEM((WIDTH, WIDTH), BF),
-                pltpu.VMEM((HEADS, WIDE, ROWS), F32),
-                pltpu.SemaphoreType.DMA((6,)),
-            ],
+            scratch_shapes=[pltpu.VMEM((WIDTH, ROWS), BF)],
         ),
         out_shape=jax.ShapeDtypeStruct((ROWS, WIDTH), BF),
         name="finish",

time: 153 us -> 152 us (level)
  no operation moved by 1% of the time
where the time goes in v5:
time: 152 us; the launch traced here: 150 us
  Pallas kernels  56.2 us (37%)
  waiting for transfers between devices  49.1 us (32%)
  starting transfers between devices  36.7 us (24%)
  local copies, waits for them, and re-layouts  7.05 us (5%)
    all_to_all x3, waiting for transfers between devices, exchange(): return lax.all_to_all(value, axis, split_axis=0, concat_axis=0, tiled=True)  33.5 us
    all_to_all x3, starting transfers between devices, exchange(): return lax.all_to_all(value, axis, split_axis=0, concat_axis=0, tiled=True)  29.2 us
    pallas_call x3, Pallas kernels, near(): pl.pallas_call(near_kernel, grid_spec=pltpu.PrefetchScalarGridSpec(num_sc...  24.2 us
    ppermute x1, waiting for transfers between devices, body(): partner = lax.ppermute(rows, 'z', [(i, i ^ 1) for i in range(8)])  10.4 us
    pallas_call x1, Pallas kernels, project(): pl.pallas_call(project_kernel, grid_spec=pltpu.PrefetchScalarGridSpec(num...  8.53 us
    pallas_call x1, Pallas kernels, widen(): pl.pallas_call(widen_kernel, out_shape=jax.ShapeDtypeStruct((4, WIDTH, WI...  6.73 us
    pallas_call x1, Pallas kernels, finish(): pl.pallas_call(finish_kernel, grid_spec=pltpu.PrefetchScalarGridSpec(num_...  6.04 us
    pallas_call x1, Pallas kernels, middle(): pl.pallas_call(middle_kernel, grid_spec=pltpu.PrefetchScalarGridSpec(num_...  5.39 us
  transfers between devices with their start and end apart: 8, of which 5 were waited for; matrix products, arithmetic and copies ran while one was open for 1% of the time, Pallas kernels for 24%

profile of v5, /device:TPU:38, one launch (start us, length us, event | category | flops | bytes accessed | tf_op | source)
XLA Modules:
  0.0 150.4 jit_solution(4012663793789529213)
XLA Ops:
  0.0 0.0 copy-start.4
  0.0 0.0 copy-start.6
  0.0 2.4 %reshape.6 = bf16[128,4,768]{2,1,0:T(4,128)(2,1)} reshape(bf16[512,768]{1,0:T(8,128)(2,1)} %param.7) | data formatting | bytes 1572864 | tf_op jit(solution)/shard_map/reshape | solution.py:438
  2.4 15.0 %all-to-all-start = ((bf16[128,4,768]{2,1,0:T(4,128)(2,1)}), bf16[128,4,768]{2,1,0:T(4,128)(2,1)S(1)}, u32[]{:S(2)}, u32[]{:S(2)}) async-start(bf16[128,4,768]{2,1,0:T(4,128)(2,1)} %reshape.6), calls=%async_computation | async-start | bytes 1572864 | tf_op jit(solution)/shard_map/all_to_all | solution.py:431
  18.0 0.0 copy-done.4
  18.0 0.6 broadcast_in_dim.10.gain_ref
  18.6 0.0 copy-done.6
  18.6 0.6 pad_add_fusion.s_ref
  19.2 6.7 %widen.1.w_ref = bf16[4,768,768]{2,1,0:T(8,128)(2,1)} custom-call(bf16[768,2304]{1,0:T(8,128)(2,1)} %w_ref.2), custom_call_target="tpu_custom_call" | custom-call | flops 10000000000 | bytes 8000000 | tf_op jit(solution)/shard_map/widen/pallas_call | solution.py:66
  25.9 14.7 %all-to-all-done = bf16[128,4,768]{2,1,0:T(4,128)(2,1)S(1)} async-done(((bf16[128,4,768]{2,1,0:T(4,128)(2,1)}), bf16[128,4,768]{2,1,0:T(4,128)(2,1)S(1)}, u32[]{:S(2)}, u32[]{:S(2)}) %all-to-all-start) | async-done | bytes 786464 | tf_op jit(solution)/shard_map/all_to_all | solution.py:431
  40.6 1.0 copy.9
  41.5 0.0 copy-start
  41.6 0.0 copy-start.5
  41.6 8.5 %project.1 = (bf16[8,3,512,128]{3,2,1,0:T(8,128)(2,1)}, bf16[16,192,128]{2,1,0:T(8,128)(2,1)}) custom-call(s32[18]{0:T(128)} %pad_add_fusion.s_ref, bf16[512,768]{1,0:T(8,128)(2,1)} %bitcast.3, f32[1,768]{1,0:T(1,128)} %broadcast_in_dim.10.gain_ref, bf16[4,768,768]{2,1,0:T(8,128)(2,1)} %widen.1.w_ref), custom_call_target="tpu_custom_call" | custom-call | tf_op jit(solution)/shard_map/project/pallas_call | solution.py:121
  50.1 4.9 %all-to-all-start.1 = ((bf16[16,192,128]{2,1,0:T(8,128)(2,1)}), bf16[16,192,128]{2,1,0:T(8,128)(2,1)S(1)}, u32[]{:S(2)}, u32[]{:S(2)}) async-start(bf16[16,192,128]{2,1,0:T(8,128)(2,1)} %get-tuple-element.8), calls=%async_computation.1 | async-start | bytes 1572864 | tf_op jit(solution)/shard_map/all_to_all | solution.py:431
  54.9 0.0 copy-done
  54.9 0.7 collective-permute-start
  55.6 0.0 copy-done.5
  55.6 0.6 broadcast_in_dim.11.gain_ref
  56.2 18.8 %all-to-all-done.1.in_ref.refs_3_ = bf16[16,192,128]{2,1,0:T(8,128)(2,1)S(1)} async-done(((bf16[16,192,128]{2,1,0:T(8,128)(2,1)}), bf16[16,192,128]{2,1,0:T(8,128)(2,1)S(1)}, u32[]{:S(2)}, u32[]{:S(2)}) %all-to-all-start.1) | async-done | bytes 786464 | tf_op jit(solution)/shard_map/all_to_all | solution.py:431
  75.0 0.0 copy-start.2
  75.0 3.6 %collective-permute-start.1 = (bf16[16,32,128]{2,1,0:T(8,128)(2,1)S(1)}, bf16[16,32,128]{2,1,0:T(8,128)(2,1)S(1)}, u32[]{:S(2)}, u32[]{:S(2)}) collective-permute-start(bf16[16,32,128]{2,1,0:T(8,128)(2,1)S(1)} %slice.4), channel_id=1, source_target_pairs={{0,32},{32,0},{1,33},{33,1},{2,34},{34,2},{3,35},{35,3},{4,36},{36... | collective-permute-start | bytes 393224 | tf_op jit(solution)/shard_map/ppermute | solution.py:445
  78.6 10.4 %collective-permute-done.x_ref = bf16[512,768]{1,0:T(8,128)(2,1)S(1)} collective-permute-done((bf16[512,768]{1,0:T(8,128)(2,1)S(1)}, bf16[512,768]{1,0:T(8,128)(2,1)S(1)}, u32[]{:S(2)}, u32[]{:S(2)}) %collective-permute-start) | collective-permute-done | bytes 786464 | tf_op jit(solution)/shard_map/ppermute | solution.py:440
  89.1 0.0 copy-start.7
  89.1 0.9 copy-done.7
  89.9 12.4 %near.3.near0_ref = f32[10,64,512]{2,1,0:T(8,128)} custom-call(s32[18]{0:T(128)} %pad_add_fusion.s_ref, bf16[512,768]{1,0:T(8,128)(2,1)} %copy-done.7, f32[1,768]{1,0:T(1,128)} %broadcast_in_dim.10.gain_ref, bf16[4,768,768]{2,1,0:T(8,128)(2,1)} %widen.1.w_ref, bf16[8,3,512,128]{3,2,1,0:T(8,128)(2,1)} %get-tuple-element.7.own_ref), custom_call_target="tpu_custom_call" | custom-call | flops 24999999488 | bytes 5000000 | tf_op jit(solution)/shard_map/near/pallas_call | solution.py:204
  102.4 0.0 copy-done.2
  102.4 0.0 collective-permute-done.1
  102.4 0.0 copy-start.3
  102.4 0.5 collective-permute-start.2
  102.9 1.7 %collective-permute-start.3 = (bf16[32,32,128]{2,1,0:T(8,128)(2,1)S(1)}, bf16[32,32,128]{2,1,0:T(8,128)(2,1)S(1)}, u32[]{:S(2)}, u32[]{:S(2)}) collective-permute-start(bf16[32,32,128]{2,1,0:T(8,128)(2,1)S(1)} %pad_maximum_fusion.own_ref), channel_id=1, source_target_pairs={{0,128},{64,192},{128,0},{192,64},{1,129},{65,193},{129,1},{193,65... | collective-permute-start | bytes 786440 | tf_op jit(solution)/shard_map/ppermute | solution.py:448
  104.6 1.2 collective-permute-start.4
  105.8 5.4 %middle.1.refs_4_ = bf16[16,64,128]{2,1,0:T(8,128)(2,1)} custom-call(s32[18]{0:T(128)} %pad_add_fusion.s_ref, bf16[16,192,128]{2,1,0:T(8,128)(2,1)} %copy-done.2), custom_call_target="tpu_custom_call" | custom-call | flops 10000000000 | bytes 1000000 | tf_op jit(solution)/shard_map/middle/pallas_call | solution.py:298
  111.1 0.0 copy-done.3
  111.2 4.6 %collective-permute-done.2.refs_0_ = bf16[32,32,128]{2,1,0:T(8,128)(2,1)S(1)} collective-permute-done((bf16[32,32,128]{2,1,0:T(8,128)(2,1)S(1)}, bf16[32,32,128]{2,1,0:T(8,128)(2,1)S(1)}, u32[]{:S(2)}, u32[]{:S(2)}) %collective-permute-start.2) | collective-permute-done | bytes 262176 | tf_op jit(solution)/shard_map/ppermute | solution.py:448
  115.7 0.0 copy-start.8
  115.7 0.0 collective-permute-done.3.refs_1_
  115.7 0.6 collective-permute-done.4.refs_2_
  116.3 0.1 copy-done.8
  116.4 0.1 copy-done.9
  116.5 0.7 copy-done.10
  117.2 5.3 %far.1 = bf16[16,72,128]{2,1,0:T(8,128)(2,1)} custom-call(bf16[32,32,128]{2,1,0:T(8,128)(2,1)} %copy-done.3, bf16[32,32,128]{2,1,0:T(8,128)(2,1)} %copy-done.8, bf16[32,32,128]{2,1,0:T(8,128)(2,1)} %copy-done.9, bf16[32,32,128]{2,1,0:T(8,128)(2,1)} %copy-done.10, bf16[16,192,128]{2,1,0:T(8,128)(2,1)} %copy-done.2, bf16[16,64,128]{2,1,0:T(8,128)(2,1)} %middle.1.refs_4_), custom_call_target="tpu_custom_call" | custom-call | flops 10000000000 | bytes 1000000 | tf_op jit(solution)/shard_map/far/pallas_call | solution.py:346
  122.5 9.3 %all-to-all-start.2 = ((bf16[16,72,128]{2,1,0:T(8,128)(2,1)}), bf16[16,72,128]{2,1,0:T(8,128)(2,1)S(1)}, u32[]{:S(2)}, u32[]{:S(2)}) async-start(bf16[16,72,128]{2,1,0:T(8,128)(2,1)} %far.1), calls=%async_computation.2 | async-start | bytes 589824 | tf_op jit(solution)/shard_map/all_to_all | solution.py:431
  131.9 6.9 %near.4.near1_ref = f32[4,64,512]{2,1,0:T(8,128)} custom-call(s32[18]{0:T(128)} %pad_add_fusion.s_ref, bf16[512,768]{1,0:T(8,128)(2,1)} %copy-done.7, f32[1,768]{1,0:T(1,128)} %broadcast_in_dim.10.gain_ref, bf16[4,768,768]{2,1,0:T(8,128)(2,1)} %widen.1.w_ref, bf16[8,3,512,128]{3,2,1,0:T(8,128)(2,1)} %get-tuple-element.7.own_ref), custom_call_target="tpu_custom_call" | custom-call | flops 10000000000 | bytes 2000000 | tf_op jit(solution)/shard_map/near/pallas_call | solution.py:204
  138.8 4.8 %near.5.near2_ref = f32[2,64,512]{2,1,0:T(8,128)} custom-call(s32[18]{0:T(128)} %pad_add_fusion.s_ref, bf16[512,768]{1,0:T(8,128)(2,1)} %copy-done.7, f32[1,768]{1,0:T(1,128)} %broadcast_in_dim.10.gain_ref, bf16[4,768,768]{2,1,0:T(8,128)(2,1)} %widen.1.w_ref, bf16[8,3,512,128]{3,2,1,0:T(8,128)(2,1)} %get-tuple-element.7.own_ref), custom_call_target="tpu_custom_call" | custom-call | flops 5000000000 | bytes 1000000 | tf_op jit(solution)/shard_map/near/pallas_call | solution.py:204
  143.6 0.0 all-to-all-done.2.in_ref
  143.6 0.7 copy-done.1
  144.3 6.0 %finish.1 = bf16[512,768]{1,0:T(8,128)(2,1)} custom-call(s32[18]{0:T(128)} %pad_add_fusion.s_ref, f32[10,64,512]{2,1,0:T(8,128)} %near.3.near0_ref, f32[4,64,512]{2,1,0:T(8,128)} %near.4.near1_ref, f32[2,64,512]{2,1,0:T(8,128)} %near.5.near2_ref, bf16[16,72,128]{2,1,0:T(8,128)(2,1)} %copy-done.1, bf16[512,768]{1,0:T(8,128)(2,1)} %bitcast.4, ...), custom_call_target="tpu_custom_call" | custom-call | tf_op jit(solution)/shard_map/finish/pallas_call | solution.py:408
  (5 shorter events, 0.0 us)
Async XLA Ops:
  0.0 18.0 %copy-start.4 = (f32[768]{0:T(1024)S(1)}, f32[768]{0:T(1024)}, u32[]{:S(2)}) copy-start(f32[768]{0:T(1024)} %param.10) | copy-start | bytes 9220
  0.0 18.6 %copy-start.6 = (s32[16]{0:T(128)S(1)}, s32[16]{0:T(128)}, u32[]{:S(2)}) copy-start(s32[16]{0:T(128)} %param.9) | copy-start | bytes 196
  2.4 38.2 %all-to-all-start = ((bf16[128,4,768]{2,1,0:T(4,128)(2,1)}), bf16[128,4,768]{2,1,0:T(4,128)(2,1)S(1)}, u32[]{:S(2)}, u32[]{:S(2)}) async-start(bf16[128,4,768]{2,1,0:T(4,128)(2,1)} %reshape.6), calls=%async_computation | async-start | bytes 1572864 | tf_op jit(solution)/shard_map/all_to_all | solution.py:431
  41.5 13.4 %copy-start = (bf16[4,128,768]{2,1,0:T(8,128)(2,1)S(1)}, bf16[4,128,768]{2,1,0:T(8,128)(2,1)}, u32[]{:S(2)}) copy-start(bf16[4,128,768]{2,1,0:T(8,128)(2,1)} %copy.9) | copy-start | bytes 2359300
  41.6 14.0 %copy-start.5 = (f32[768]{0:T(1024)S(1)}, f32[768]{0:T(1024)}, u32[]{:S(2)}) copy-start(f32[768]{0:T(1024)} %param.12) | copy-start | bytes 9220
  50.1 24.9 %all-to-all-start.1 = ((bf16[16,192,128]{2,1,0:T(8,128)(2,1)}), bf16[16,192,128]{2,1,0:T(8,128)(2,1)S(1)}, u32[]{:S(2)}, u32[]{:S(2)}) async-start(bf16[16,192,128]{2,1,0:T(8,128)(2,1)} %get-tuple-element.8), calls=%async_computation.1 | async-start | bytes 1572864 | tf_op jit(solution)/shard_map/all_to_all | solution.py:431
  54.9 34.1 %collective-permute-start = (bf16[512,768]{1,0:T(8,128)(2,1)S(1)}, bf16[512,768]{1,0:T(8,128)(2,1)S(1)}, u32[]{:S(2)}, u32[]{:S(2)}) collective-permute-start(bf16[512,768]{1,0:T(8,128)(2,1)S(1)} %bitcast.5), channel_id=1, source_target_pairs={{0,2},{2,0},{4,6},{6,4},{8,10},{10,8},{12,14},{14,12},{1,3},{3,1},... | collective-permute-start | bytes 2359304 | tf_op jit(solution)/shard_map/ppermute | solution.py:440
  75.0 27.4 %copy-start.2 = (bf16[16,192,128]{2,1,0:T(8,128)(2,1)}, bf16[16,192,128]{2,1,0:T(8,128)(2,1)S(1)}, u32[]{:S(2)}) copy-start(bf16[16,192,128]{2,1,0:T(8,128)(2,1)S(1)} %all-to-all-done.1.in_ref.refs_3_) | copy-start | bytes 2359300
  75.0 27.3 %collective-permute-start.1 = (bf16[16,32,128]{2,1,0:T(8,128)(2,1)S(1)}, bf16[16,32,128]{2,1,0:T(8,128)(2,1)S(1)}, u32[]{:S(2)}, u32[]{:S(2)}) collective-permute-start(bf16[16,32,128]{2,1,0:T(8,128)(2,1)S(1)} %slice.4), channel_id=1, source_target_pairs={{0,32},{32,0},{1,33},{33,1},{2,34},{34,2},{3,35},{35,3},{4,36},{36... | collective-permute-start | bytes 393224 | tf_op jit(solution)/shard_map/ppermute | solution.py:445
  89.1 0.9 copy-start.7
  102.4 8.7 %copy-start.3 = (bf16[32,32,128]{2,1,0:T(8,128)(2,1)}, bf16[32,32,128]{2,1,0:T(8,128)(2,1)S(1)}, u32[]{:S(2)}) copy-start(bf16[32,32,128]{2,1,0:T(8,128)(2,1)S(1)} %pad_maximum_fusion.own_ref) | copy-start | bytes 786436
  102.4 13.3 %collective-permute-start.2 = (bf16[32,32,128]{2,1,0:T(8,128)(2,1)S(1)}, bf16[32,32,128]{2,1,0:T(8,128)(2,1)S(1)}, u32[]{:S(2)}, u32[]{:S(2)}) collective-permute-start(bf16[32,32,128]{2,1,0:T(8,128)(2,1)S(1)} %pad_maximum_fusion.own_ref), channel_id=1, source_target_pairs={{0,64},{64,128},{128,192},{192,0},{1,65},{65,129},{129,193},{193,1... | collective-permute-start | bytes 786440 | tf_op jit(solution)/shard_map/ppermute | solution.py:448
  102.9 12.8 %collective-permute-start.3 = (bf16[32,32,128]{2,1,0:T(8,128)(2,1)S(1)}, bf16[32,32,128]{2,1,0:T(8,128)(2,1)S(1)}, u32[]{:S(2)}, u32[]{:S(2)}) collective-permute-start(bf16[32,32,128]{2,1,0:T(8,128)(2,1)S(1)} %pad_maximum_fusion.own_ref), channel_id=1, source_target_pairs={{0,128},{64,192},{128,0},{192,64},{1,129},{65,193},{129,1},{193,65... | collective-permute-start | bytes 786440 | tf_op jit(solution)/shard_map/ppermute | solution.py:448
  104.6 11.8 %collective-permute-start.4 = (bf16[32,32,128]{2,1,0:T(8,128)(2,1)S(1)}, bf16[32,32,128]{2,1,0:T(8,128)(2,1)S(1)}, u32[]{:S(2)}, u32[]{:S(2)}) collective-permute-start(bf16[32,32,128]{2,1,0:T(8,128)(2,1)S(1)} %pad_maximum_fusion.own_ref), channel_id=1, source_target_pairs={{0,192},{64,0},{128,64},{192,128},{1,193},{65,1},{129,65},{193,129... | collective-permute-start | bytes 786440 | tf_op jit(solution)/shard_map/ppermute | solution.py:448
  115.7 0.7 copy-start.8
  115.7 0.8 copy-start.9
  116.5 0.7 copy-start.10
  122.5 21.1 %all-to-all-start.2 = ((bf16[16,72,128]{2,1,0:T(8,128)(2,1)}), bf16[16,72,128]{2,1,0:T(8,128)(2,1)S(1)}, u32[]{:S(2)}, u32[]{:S(2)}) async-start(bf16[16,72,128]{2,1,0:T(8,128)(2,1)} %far.1), calls=%async_computation.2 | async-start | bytes 589824 | tf_op jit(solution)/shard_map/all_to_all | solution.py:431
  143.6 0.7 copy-start.1
